TPU v7x, 256 devices: a whole 4x4x8 slice. The times are simulated.
256 devices in a mesh: gx: 32 (over y, x, core), gy: 8 (over z).
Axes of the slice: x: 4, y: 4, z: 8, core: 2. Of those that a mesh axis runs over, the one named last changes fastest.
Arguments:
- displacement: float32 [3, 512, 256, 128], P(None, 'gx', 'gy'), may hold values from -4 to 4
- force: float32 [3, 512, 256, 128], P(None, 'gx', 'gy'), may hold values from -12 to 12
- damage: float32 [512, 256, 128], P('gx', 'gy'), may hold values from 0 to 0.8
- history: float32 [512, 256, 128], P('gx', 'gy'), may hold values from 0.05 to 3
- crack_flags: int32 [512, 256, 128], P('gx', 'gy'), may hold values 0 or 1
Outputs:
- displacement_out: float32 [3, 512, 256, 128], P(None, 'gx', 'gy')
- damage_out: float32 [512, 256, 128], P('gx', 'gy')
- history_out: float32 [512, 256, 128], P('gx', 'gy')
All inputs are finite; a program needn't handle non-finite values. No bound on the sum of `crack_flags` on one device may be relied on, other than what follows from the above.
Results may differ from a plain program's by a relative error of at most 0.0003.
Values sent between devices are 32-bit elements; how exact they have to be, the bound alone decides.
No kernel may reach another device: no remote copies, remote signals or barrier semaphores. Data moves between devices by JAX's collectives and lax.ppermute only.
A program may use at most 64 MiB of HBM per device.

v0:
```python
import jax
import jax.numpy as jnp
from jax import lax
from jax.sharding import Mesh
from jax.sharding import PartitionSpec as P

ITERS = 3
GX = ("gx_0", "gx_1", "gx_2")


shear_modulus = 1.0
lame_first = 1.5
spring_term = 0.5
stiff_floor = 0.001
crack_load = 4.0
tough_ratio = 0.5
length_term = 2.0
stress_index = ((0, 3, 4), (3, 1, 5), (4, 5, 2))


def padded_2(shard, sides, width):
    for axis, dim in sides:
        size, length = (lax.axis_size(axis), shard.shape[dim])
        up = [(i, (i + 1) % size) for i in range(size - 1)]
        down = [(j, i) for i, j in up]
        last = lax.slice_in_dim(shard, length - width, length, axis=dim)
        leading = lax.slice_in_dim(shard, 0, width, axis=dim)
        before = lax.ppermute(last, axis, up)
        after = lax.ppermute(leading, axis, down)
        shard = jnp.concatenate([before, shard, after], axis=dim)
    return shard


def extended_2(shard, sides, width):
    edges = {}
    for axis, dim in sides:
        size, length = (lax.axis_size(axis), shard.shape[dim])
        up = [(i, (i + 1) % size) for i in range(size - 1)]
        last = lax.slice_in_dim(shard, length - width, length, axis=dim)
        leading = lax.slice_in_dim(shard, 0, width, axis=dim)
        edges[dim] = (
            lax.ppermute(last, axis, up),
            lax.ppermute(leading, axis, [(b, a) for a, b in up]),
        )
    done = []
    for _, dim in sides:
        low, high = edges[dim]
        around = [(width, width) if d in done else (0, 0) for d in range(shard.ndim)]
        shard = jnp.concatenate([jnp.pad(low, around), shard, jnp.pad(high, around)], axis=dim)
        done.append(dim)
    return shard


def sent_to_all(shard, axis):
    length = lax.axis_size(axis)
    return lax.all_to_all(
        jnp.broadcast_to(shard[None], (length, *shard.shape)), axis, 0, 0, tiled=True
    )


def taken_together(shard, axis):
    everything = sent_to_all(shard, axis)
    return jnp.sum(everything, axis=0)


def over_axes(shard, axes):
    far, near = axes
    return taken_together(taken_together(shard, near), far)


def packed_total(arrays, axis):
    ravelled, at, outs = (jnp.concatenate([a.reshape(-1) for a in arrays]), 0, [])
    total = over_axes(ravelled, axis)
    for a in arrays:
        outs.append(total[at : at + a.size].reshape(a.shape))
        at += a.size
    return tuple(outs)


def strains(padded):
    base = padded[:, :-1, :-1, :-1]
    grads = []
    for component in range(3):
        grads.append(
            (
                padded[component, 1:, :-1, :-1] - base[component],
                padded[component, :-1, 1:, :-1] - base[component],
                padded[component, :-1, :-1, 1:] - base[component],
            )
        )
    return (
        grads[0][0],
        grads[1][1],
        grads[2][2],
        0.5 * (grads[0][1] + grads[1][0]),
        0.5 * (grads[0][2] + grads[2][0]),
        0.5 * (grads[1][2] + grads[2][1]),
    )


def lowered(values, direction):
    if direction == 0:
        return values[:-1, 1:, 1:]
    if direction == 1:
        return values[1:, :-1, 1:]
    return values[1:, 1:, :-1]


def elastic(padded, padded_gain):
    strain = strains(padded)
    weight = padded_gain[:-1, :-1, :-1]
    trace = strain[0] + strain[1] + strain[2]
    stress = [
        weight * (2.0 * shear_modulus * strain[index] + lame_first * trace) for index in range(3)
    ]
    stress = stress + [weight * (2.0 * shear_modulus * strain[index]) for index in range(3, 6)]
    images = []
    for component in range(3):
        summed = spring_term * padded[component, 1:-1, 1:-1, 1:-1]
        for direction in range(3):
            values = stress[stress_index[component][direction]]
            summed = summed + lowered(values, direction) - values[1:, 1:, 1:]
        images.append(summed)
    return (jnp.stack(images), strain)


def energy(strain):
    owned = [item[1:, 1:, 1:] for item in strain]
    trace = owned[0] + owned[1] + owned[2]
    squares = (
        owned[0] ** 2
        + owned[1] ** 2
        + owned[2] ** 2
        + 2.0 * (owned[3] ** 2 + owned[4] ** 2 + owned[5] ** 2)
    )
    bulk_half = 0.5 * (lame_first + 2.0 * shear_modulus / 3.0)
    return bulk_half * jnp.maximum(trace, 0.0) ** 2 + shear_modulus * (
        squares - trace * trace / 3.0
    )


def damage_apply(padded, driving):
    center = padded[1:-1, 1:-1, 1:-1]
    beside_all = (
        padded[2:, 1:-1, 1:-1]
        + padded[:-2, 1:-1, 1:-1]
        + padded[1:-1, 2:, 1:-1]
        + padded[1:-1, :-2, 1:-1]
        + padded[1:-1, 1:-1, 2:]
        + padded[1:-1, 1:-1, :-2]
    )
    return (tough_ratio + 2.0 * driving) * center + length_term * (6.0 * center - beside_all)


def pad_depth(values):
    widths = [(0, 0)] * (values.ndim - 1) + [(1, 1)]
    return jnp.pad(values, widths)


def vector_rim(values):
    extended = padded_2(values, ((GX, 1), ("gy", 2)), 1)
    return pad_depth(extended)


def scalar_rim(values):
    extended = extended_2(values, ((GX, 0), ("gy", 1)), 1)
    return pad_depth(extended)


def paired_sums(resid, image):
    return packed_total(
        (jnp.sum(resid * resid), jnp.sum(resid * image)), (("gx_0", "gx_1"), ("gx_2", "gy"))
    )


def add_scaled(first, second, factor):
    return jax.tree.map(lambda left, right: left + factor * right, first, second)


def solve(operate, start, target, first):
    current = start
    image_start, aside_now = first
    resid = target - image_start
    image, aside_resid = operate(resid)
    norm_now, product = paired_sums(resid, image)
    alpha = norm_now / product
    direction, along, aside_dir = (resid, image, aside_resid)
    for number in range(ITERS):
        current = current + alpha * direction
        aside_now = add_scaled(aside_now, aside_dir, alpha)
        resid = resid - alpha * along
        if number + 1 < ITERS:
            image, aside_resid = operate(resid)
            norm_next, product = paired_sums(resid, image)
            ratio = norm_next / norm_now
            alpha = norm_next / (product - ratio * norm_next / alpha)
            direction = resid + ratio * direction
            along = image + ratio * along
            aside_dir = add_scaled(aside_resid, aside_dir, ratio)
            norm_now = norm_next
    return (current, aside_now)


def body(displacement, force, damage, history, crack_flags):
    gain = (1.0 - damage) ** 2 + stiff_floor
    stacked = extended_2(jnp.stack([gain, damage]), ((GX, 1), ("gy", 2)), 1)
    padded_gain = pad_depth(stacked[0])
    padded_damage = pad_depth(stacked[1])

    def elastic_step(values):
        image, strain = elastic(vector_rim(values), padded_gain)
        return (image, ())

    moved, strain = solve(elastic_step, displacement, force, elastic_step(displacement))
    strain = elastic(vector_rim(moved), padded_gain)[1]
    psi = energy(strain)
    history_out = jnp.maximum(
        jnp.maximum(history, psi), crack_load * crack_flags.astype(jnp.float32)
    )

    def damage_step(values):
        return (damage_apply(scalar_rim(values), history_out), ())

    first_damage = (damage_apply(padded_damage, history_out), ())
    damage_out, unused = solve(damage_step, damage, 2.0 * history_out, first_damage)
    return (moved, damage_out, history_out)


def solution(mesh):
    finer = Mesh(mesh.devices.reshape(4, 4, 2, mesh.shape["gy"]), ("gx_0", "gx_1", "gx_2", "gy"))
    return jax.shard_map(
        body,
        mesh=finer,
        in_specs=(
            P(None, GX, "gy", None),
            P(None, GX, "gy", None),
            P(GX, "gy", None),
            P(GX, "gy", None),
            P(GX, "gy", None),
        ),
        out_specs=(P(None, GX, "gy", None), P(GX, "gy", None), P(GX, "gy", None)),
        check_vma=False,
    )
```

profile of v0, /device:TPU:1, one launch (start us, length us, event | category | flops | bytes accessed | tf_op | source)
XLA Modules:
  0.0 356.1 jit_solution(1214154949304351495)
XLA Ops:
  2.6 4.4 %collective-permute-start = (f32[2,16,1,128]{3,2,1,0:T(1,128)S(1)}, f32[2,16,1,128]{3,2,1,0:T(1,128)S(1)}, u32[]{:S(2)}, u32[]{:S(2)}) collective-permute-start(f32[2,16,1,128]{3,2,1,0:T(1,128)S(1)} %get-tuple-element.93), channel_id=1, source_target_pairs={{0,1},{1,2},{2,3},{3,4},{4,5},{5,6},{6,7},{8,9},{9,10},{10,11},{11... | collective-permute-start | bytes 49160 | tf_op jit(solution)/shard_map/ppermute | solution.py:42
  9.0 3.9 %collective-permute-start.1 = (f32[2,1,32,128]{3,2,1,0:T(8,128)S(1)}, f32[2,1,32,128]{3,2,1,0:T(8,128)S(1)}, u32[]{:S(2)}, u32[]{:S(2)}) collective-permute-start(f32[2,1,32,128]{3,2,1,0:T(8,128)S(1)} %get-tuple-element.91), channel_id=1, source_target_pairs={{0,8},{8,16},{16,24},{24,32},{32,40},{40,48},{48,56},{56,64},{64,7... | collective-permute-start | bytes 98312 | tf_op jit(solution)/shard_map/ppermute | solution.py:42
  17.7 3.6 %collective-permute-start.4 = (f32[3,1,32,128]{3,2,1,0:T(8,128)S(1)}, f32[3,1,32,128]{3,2,1,0:T(8,128)S(1)}, u32[]{:S(2)}, u32[]{:S(2)}) collective-permute-start(f32[3,1,32,128]{3,2,1,0:T(8,128)S(1)} %get-tuple-element.88), channel_id=1, source_target_pairs={{0,8},{8,16},{16,24},{24,32},{32,40},{40,48},{48,56},{56,64},{64,7... | collective-permute-start | bytes 147464 | tf_op jit(solution)/shard_map/ppermute | solution.py:28
  22.6 4.3 %collective-permute-start.6 = (f32[3,18,1,128]{3,2,1,0:T(1,128)S(1)}, f32[3,18,1,128]{3,2,1,0:T(1,128)S(1)}, u32[]{:S(2)}, u32[]{:S(2)}) collective-permute-start(f32[3,18,1,128]{3,2,1,0:T(1,128)S(1)} %get-tuple-element.77), channel_id=1, source_target_pairs={{0,1},{1,2},{2,3},{3,4},{4,5},{5,6},{6,7},{8,9},{9,10},{10,11},{11... | collective-permute-start | bytes 82952 | tf_op jit(solution)/shard_map/ppermute | solution.py:28
  28.3 3.4 collective-permute-done.7
  36.3 5.5 %collective-permute-start.8 = (f32[3,1,32,128]{3,2,1,0:T(8,128)S(1)}, f32[3,1,32,128]{3,2,1,0:T(8,128)S(1)}, u32[]{:S(2)}, u32[]{:S(2)}) collective-permute-start(f32[3,1,32,128]{3,2,1,0:T(8,128)S(1)} %get-tuple-element.85), channel_id=1, source_target_pairs={{0,8},{8,16},{16,24},{24,32},{32,40},{40,48},{48,56},{56,64},{64,7... | collective-permute-start | bytes 147464 | tf_op jit(solution)/shard_map/ppermute | solution.py:28
  43.8 3.5 collective-permute-done.9
  47.3 4.6 %collective-permute-start.10 = (f32[3,18,1,128]{3,2,1,0:T(1,128)S(1)}, f32[3,18,1,128]{3,2,1,0:T(1,128)S(1)}, u32[]{:S(2)}, u32[]{:S(2)}) collective-permute-start(f32[3,18,1,128]{3,2,1,0:T(1,128)S(1)} %get-tuple-element.75), channel_id=1, source_target_pairs={{0,1},{1,2},{2,3},{3,4},{4,5},{5,6},{6,7},{8,9},{9,10},{10,11},{11... | collective-permute-start | bytes 82952 | tf_op jit(solution)/shard_map/ppermute | solution.py:28
  53.2 4.8 %collective-permute-done.11 = f32[3,18,1,128]{3,2,1,0:T(1,128)S(1)} collective-permute-done((f32[3,18,1,128]{3,2,1,0:T(1,128)S(1)}, f32[3,18,1,128]{3,2,1,0:T(1,128)S(1)}, u32[]{:S(2)}, u32[]{:S(2)}) %collective-permute-start.11) | collective-permute-done | bytes 27680 | tf_op jit(solution)/shard_map/ppermute | solution.py:29
  64.4 13.5 %all_to_all.72 = f32[16,1,2]{2,1,0:T(1,128)S(1)} all-to-all(f32[16,1,2]{2,1,0:T(1,128)S(1)} %broadcast_in_dim.24), channel_id=1, replica_groups=mesh['gx_0'=4,'gx_1'=4,'gx_2'=2,'gy'=8] {'gx_2','gy'}, dimensions={0} | all-to-all | bytes 256 | tf_op jit(solution)/shard_map/all_to_all | solution.py:56
  78.0 18.8 %all_to_all.73 = f32[16,1,2]{2,1,0:T(1,128)S(1)} all-to-all(f32[16,1,2]{2,1,0:T(1,128)S(1)} %broadcast_in_dim.25), channel_id=1, replica_groups=mesh['gx_0'=4,'gx_1'=4,'gx_2'=2,'gy'=8] {'gx_0','gx_1'}, dimensions={0} | all-to-all | bytes 256 | tf_op jit(solution)/shard_map/all_to_all | solution.py:56
  98.9 4.2 %collective-permute-start.12 = (f32[3,1,32,128]{3,2,1,0:T(8,128)S(1)}, f32[3,1,32,128]{3,2,1,0:T(8,128)S(1)}, u32[]{:S(2)}, u32[]{:S(2)}) collective-permute-start(f32[3,1,32,128]{3,2,1,0:T(8,128)S(1)} %get-tuple-element.83), channel_id=1, source_target_pairs={{0,8},{8,16},{16,24},{24,32},{32,40},{40,48},{48,56},{56,64},{64,7... | collective-permute-start | bytes 147464 | tf_op jit(solution)/shard_map/ppermute | solution.py:28
  105.0 3.5 collective-permute-done.13
  112.3 3.1 collective-permute-done.15
  122.6 10.0 %all_to_all.74 = f32[16,1,2]{2,1,0:T(1,128)S(1)} all-to-all(f32[16,1,2]{2,1,0:T(1,128)S(1)} %broadcast_in_dim.26), channel_id=1, replica_groups=mesh['gx_0'=4,'gx_1'=4,'gx_2'=2,'gy'=8] {'gx_2','gy'}, dimensions={0} | all-to-all | bytes 256 | tf_op jit(solution)/shard_map/all_to_all | solution.py:56
  132.6 13.6 %all_to_all.75 = f32[16,1,2]{2,1,0:T(1,128)S(1)} all-to-all(f32[16,1,2]{2,1,0:T(1,128)S(1)} %broadcast_in_dim.27), channel_id=1, replica_groups=mesh['gx_0'=4,'gx_1'=4,'gx_2'=2,'gy'=8] {'gx_0','gx_1'}, dimensions={0} | all-to-all | bytes 256 | tf_op jit(solution)/shard_map/all_to_all | solution.py:56
  152.7 4.2 %collective-permute-start.16 = (f32[3,1,32,128]{3,2,1,0:T(8,128)S(1)}, f32[3,1,32,128]{3,2,1,0:T(8,128)S(1)}, u32[]{:S(2)}, u32[]{:S(2)}) collective-permute-start(f32[3,1,32,128]{3,2,1,0:T(8,128)S(1)} %get-tuple-element.81), channel_id=1, source_target_pairs={{0,8},{8,16},{16,24},{24,32},{32,40},{40,48},{48,56},{56,64},{64,7... | collective-permute-start | bytes 147464 | tf_op jit(solution)/shard_map/ppermute | solution.py:28
  158.8 3.5 collective-permute-done.17
  165.9 3.3 collective-permute-done.19
  176.1 10.0 %all_to_all.76 = f32[16,1,2]{2,1,0:T(1,128)S(1)} all-to-all(f32[16,1,2]{2,1,0:T(1,128)S(1)} %broadcast_in_dim.28), channel_id=1, replica_groups=mesh['gx_0'=4,'gx_1'=4,'gx_2'=2,'gy'=8] {'gx_2','gy'}, dimensions={0} | all-to-all | bytes 256 | tf_op jit(solution)/shard_map/all_to_all | solution.py:56
  186.1 13.6 %all_to_all.77 = f32[16,1,2]{2,1,0:T(1,128)S(1)} all-to-all(f32[16,1,2]{2,1,0:T(1,128)S(1)} %broadcast_in_dim.29), channel_id=1, replica_groups=mesh['gx_0'=4,'gx_1'=4,'gx_2'=2,'gy'=8] {'gx_0','gx_1'}, dimensions={0} | all-to-all | bytes 256 | tf_op jit(solution)/shard_map/all_to_all | solution.py:56
  206.1 4.2 %collective-permute-start.20 = (f32[3,1,32,128]{3,2,1,0:T(8,128)S(1)}, f32[3,1,32,128]{3,2,1,0:T(8,128)S(1)}, u32[]{:S(2)}, u32[]{:S(2)}) collective-permute-start(f32[3,1,32,128]{3,2,1,0:T(8,128)S(1)} %get-tuple-element.79), channel_id=1, source_target_pairs={{0,8},{8,16},{16,24},{24,32},{32,40},{40,48},{48,56},{56,64},{64,7... | collective-permute-start | bytes 147464 | tf_op jit(solution)/shard_map/ppermute | solution.py:28
  212.2 3.5 collective-permute-done.21
  225.3 3.3 collective-permute-start.25
  239.7 10.9 %all_to_all.78 = f32[16,1,2]{2,1,0:T(1,128)S(1)} all-to-all(f32[16,1,2]{2,1,0:T(1,128)S(1)} %broadcast_in_dim.30), channel_id=1, replica_groups=mesh['gx_0'=4,'gx_1'=4,'gx_2'=2,'gy'=8] {'gx_2','gy'}, dimensions={0} | all-to-all | bytes 256 | tf_op jit(solution)/shard_map/all_to_all | solution.py:56
  250.6 15.6 %all_to_all.79 = f32[16,1,2]{2,1,0:T(1,128)S(1)} all-to-all(f32[16,1,2]{2,1,0:T(1,128)S(1)} %broadcast_in_dim.31), channel_id=1, replica_groups=mesh['gx_0'=4,'gx_1'=4,'gx_2'=2,'gy'=8] {'gx_0','gx_1'}, dimensions={0} | all-to-all | bytes 256 | tf_op jit(solution)/shard_map/all_to_all | solution.py:56
  268.1 4.2 %collective-permute-start.29 = (f32[1,32,128]{2,1,0:T(8,128)S(1)}, f32[1,32,128]{2,1,0:T(8,128)S(1)}, u32[]{:S(2)}, u32[]{:S(2)}) collective-permute-start(f32[1,32,128]{2,1,0:T(8,128)S(1)} %get-tuple-element.99), channel_id=1, source_target_pairs={{0,8},{8,16},{16,24},{24,32},{32,40},{40,48},{48,56},{56,64},{64,7... | collective-permute-start | bytes 49160 | tf_op jit(solution)/shard_map/ppermute | solution.py:42
  283.6 10.0 %all_to_all.80 = f32[16,1,2]{2,1,0:T(1,128)S(1)} all-to-all(f32[16,1,2]{2,1,0:T(1,128)S(1)} %broadcast_in_dim.32), channel_id=1, replica_groups=mesh['gx_0'=4,'gx_1'=4,'gx_2'=2,'gy'=8] {'gx_2','gy'}, dimensions={0} | all-to-all | bytes 256 | tf_op jit(solution)/shard_map/all_to_all | solution.py:56
  293.6 13.5 %all_to_all.81 = f32[16,1,2]{2,1,0:T(1,128)S(1)} all-to-all(f32[16,1,2]{2,1,0:T(1,128)S(1)} %broadcast_in_dim.33), channel_id=1, replica_groups=mesh['gx_0'=4,'gx_1'=4,'gx_2'=2,'gy'=8] {'gx_0','gx_1'}, dimensions={0} | all-to-all | bytes 256 | tf_op jit(solution)/shard_map/all_to_all | solution.py:56
  312.2 4.2 %collective-permute-start.33 = (f32[1,32,128]{2,1,0:T(8,128)S(1)}, f32[1,32,128]{2,1,0:T(8,128)S(1)}, u32[]{:S(2)}, u32[]{:S(2)}) collective-permute-start(f32[1,32,128]{2,1,0:T(8,128)S(1)} %get-tuple-element.95), channel_id=1, source_target_pairs={{0,8},{8,16},{16,24},{24,32},{32,40},{40,48},{48,56},{56,64},{64,7... | collective-permute-start | bytes 49160 | tf_op jit(solution)/shard_map/ppermute | solution.py:42
  327.5 10.0 %all_to_all.82 = f32[16,1,2]{2,1,0:T(1,128)S(1)} all-to-all(f32[16,1,2]{2,1,0:T(1,128)S(1)} %broadcast_in_dim.34), channel_id=1, replica_groups=mesh['gx_0'=4,'gx_1'=4,'gx_2'=2,'gy'=8] {'gx_2','gy'}, dimensions={0} | all-to-all | bytes 256 | tf_op jit(solution)/shard_map/all_to_all | solution.py:56
  337.5 13.5 %all_to_all.83 = f32[16,1,2]{2,1,0:T(1,128)S(1)} all-to-all(f32[16,1,2]{2,1,0:T(1,128)S(1)} %broadcast_in_dim.35), channel_id=1, replica_groups=mesh['gx_0'=4,'gx_1'=4,'gx_2'=2,'gy'=8] {'gx_0','gx_1'}, dimensions={0} | all-to-all | bytes 256 | tf_op jit(solution)/shard_map/all_to_all | solution.py:56
  (179 shorter events, 103.7 us)
Async XLA Ops:
  2.6 15.1 %collective-permute-start = (f32[2,16,1,128]{3,2,1,0:T(1,128)S(1)}, f32[2,16,1,128]{3,2,1,0:T(1,128)S(1)}, u32[]{:S(2)}, u32[]{:S(2)}) collective-permute-start(f32[2,16,1,128]{3,2,1,0:T(1,128)S(1)} %get-tuple-element.93), channel_id=1, source_target_pairs={{0,1},{1,2},{2,3},{3,4},{4,5},{5,6},{6,7},{8,9},{9,10},{10,11},{11... | collective-permute-start | bytes 49160 | tf_op jit(solution)/shard_map/ppermute | solution.py:42
  7.0 14.3 %collective-permute-start.3 = (f32[2,16,1,128]{3,2,1,0:T(1,128)S(1)}, f32[2,16,1,128]{3,2,1,0:T(1,128)S(1)}, u32[]{:S(2)}, u32[]{:S(2)}) collective-permute-start(f32[2,16,1,128]{3,2,1,0:T(1,128)S(1)} %get-tuple-element.94), channel_id=1, source_target_pairs={{1,0},{2,1},{3,2},{4,3},{5,4},{6,5},{7,6},{9,8},{10,9},{11,10},{12... | collective-permute-start | bytes 49160 | tf_op jit(solution)/shard_map/ppermute | solution.py:43
  9.0 12.3 %collective-permute-start.1 = (f32[2,1,32,128]{3,2,1,0:T(8,128)S(1)}, f32[2,1,32,128]{3,2,1,0:T(8,128)S(1)}, u32[]{:S(2)}, u32[]{:S(2)}) collective-permute-start(f32[2,1,32,128]{3,2,1,0:T(8,128)S(1)} %get-tuple-element.91), channel_id=1, source_target_pairs={{0,8},{8,16},{16,24},{24,32},{32,40},{40,48},{48,56},{56,64},{64,7... | collective-permute-start | bytes 98312 | tf_op jit(solution)/shard_map/ppermute | solution.py:42
  13.0 8.4 %collective-permute-start.2 = (f32[2,1,32,128]{3,2,1,0:T(8,128)S(1)}, f32[2,1,32,128]{3,2,1,0:T(8,128)S(1)}, u32[]{:S(2)}, u32[]{:S(2)}) collective-permute-start(f32[2,1,32,128]{3,2,1,0:T(8,128)S(1)} %get-tuple-element.92), channel_id=1, source_target_pairs={{8,0},{16,8},{24,16},{32,24},{40,32},{48,40},{56,48},{64,56},{72,6... | collective-permute-start | bytes 98312 | tf_op jit(solution)/shard_map/ppermute | solution.py:43
  15.7 6.8 %collective-permute-start.5 = (f32[3,1,32,128]{3,2,1,0:T(8,128)S(1)}, f32[3,1,32,128]{3,2,1,0:T(8,128)S(1)}, u32[]{:S(2)}, u32[]{:S(2)}) collective-permute-start(f32[3,1,32,128]{3,2,1,0:T(8,128)S(1)} %get-tuple-element.87), channel_id=1, source_target_pairs={{8,0},{16,8},{24,16},{32,24},{40,32},{48,40},{56,48},{64,56},{72,6... | collective-permute-start | bytes 147464 | tf_op jit(solution)/shard_map/ppermute | solution.py:29
  17.7 4.8 %collective-permute-start.4 = (f32[3,1,32,128]{3,2,1,0:T(8,128)S(1)}, f32[3,1,32,128]{3,2,1,0:T(8,128)S(1)}, u32[]{:S(2)}, u32[]{:S(2)}) collective-permute-start(f32[3,1,32,128]{3,2,1,0:T(8,128)S(1)} %get-tuple-element.88), channel_id=1, source_target_pairs={{0,8},{8,16},{16,24},{24,32},{32,40},{40,48},{48,56},{56,64},{64,7... | collective-permute-start | bytes 147464 | tf_op jit(solution)/shard_map/ppermute | solution.py:28
  22.6 5.6 %collective-permute-start.6 = (f32[3,18,1,128]{3,2,1,0:T(1,128)S(1)}, f32[3,18,1,128]{3,2,1,0:T(1,128)S(1)}, u32[]{:S(2)}, u32[]{:S(2)}) collective-permute-start(f32[3,18,1,128]{3,2,1,0:T(1,128)S(1)} %get-tuple-element.77), channel_id=1, source_target_pairs={{0,1},{1,2},{2,3},{3,4},{4,5},{5,6},{6,7},{8,9},{9,10},{10,11},{11... | collective-permute-start | bytes 82952 | tf_op jit(solution)/shard_map/ppermute | solution.py:28
  26.9 4.8 %collective-permute-start.7 = (f32[3,18,1,128]{3,2,1,0:T(1,128)S(1)}, f32[3,18,1,128]{3,2,1,0:T(1,128)S(1)}, u32[]{:S(2)}, u32[]{:S(2)}) collective-permute-start(f32[3,18,1,128]{3,2,1,0:T(1,128)S(1)} %get-tuple-element.78), channel_id=1, source_target_pairs={{1,0},{2,1},{3,2},{4,3},{5,4},{6,5},{7,6},{9,8},{10,9},{11,10},{12... | collective-permute-start | bytes 82952 | tf_op jit(solution)/shard_map/ppermute | solution.py:29
  36.3 7.4 %collective-permute-start.8 = (f32[3,1,32,128]{3,2,1,0:T(8,128)S(1)}, f32[3,1,32,128]{3,2,1,0:T(8,128)S(1)}, u32[]{:S(2)}, u32[]{:S(2)}) collective-permute-start(f32[3,1,32,128]{3,2,1,0:T(8,128)S(1)} %get-tuple-element.85), channel_id=1, source_target_pairs={{0,8},{8,16},{16,24},{24,32},{32,40},{40,48},{48,56},{56,64},{64,7... | collective-permute-start | bytes 147464 | tf_op jit(solution)/shard_map/ppermute | solution.py:28
  41.8 5.4 %collective-permute-start.9 = (f32[3,1,32,128]{3,2,1,0:T(8,128)S(1)}, f32[3,1,32,128]{3,2,1,0:T(8,128)S(1)}, u32[]{:S(2)}, u32[]{:S(2)}) collective-permute-start(f32[3,1,32,128]{3,2,1,0:T(8,128)S(1)} %get-tuple-element.86), channel_id=1, source_target_pairs={{8,0},{16,8},{24,16},{32,24},{40,32},{48,40},{56,48},{64,56},{72,6... | collective-permute-start | bytes 147464 | tf_op jit(solution)/shard_map/ppermute | solution.py:29
  47.3 5.9 %collective-permute-start.10 = (f32[3,18,1,128]{3,2,1,0:T(1,128)S(1)}, f32[3,18,1,128]{3,2,1,0:T(1,128)S(1)}, u32[]{:S(2)}, u32[]{:S(2)}) collective-permute-start(f32[3,18,1,128]{3,2,1,0:T(1,128)S(1)} %get-tuple-element.75), channel_id=1, source_target_pairs={{0,1},{1,2},{2,3},{3,4},{4,5},{5,6},{6,7},{8,9},{9,10},{10,11},{11... | collective-permute-start | bytes 82952 | tf_op jit(solution)/shard_map/ppermute | solution.py:28
  51.9 6.1 %collective-permute-start.11 = (f32[3,18,1,128]{3,2,1,0:T(1,128)S(1)}, f32[3,18,1,128]{3,2,1,0:T(1,128)S(1)}, u32[]{:S(2)}, u32[]{:S(2)}) collective-permute-start(f32[3,18,1,128]{3,2,1,0:T(1,128)S(1)} %get-tuple-element.76), channel_id=1, source_target_pairs={{1,0},{2,1},{3,2},{4,3},{5,4},{6,5},{7,6},{9,8},{10,9},{11,10},{12... | collective-permute-start | bytes 82952 | tf_op jit(solution)/shard_map/ppermute | solution.py:29
  98.9 6.2 %collective-permute-start.12 = (f32[3,1,32,128]{3,2,1,0:T(8,128)S(1)}, f32[3,1,32,128]{3,2,1,0:T(8,128)S(1)}, u32[]{:S(2)}, u32[]{:S(2)}) collective-permute-start(f32[3,1,32,128]{3,2,1,0:T(8,128)S(1)} %get-tuple-element.83), channel_id=1, source_target_pairs={{0,8},{8,16},{16,24},{24,32},{32,40},{40,48},{48,56},{56,64},{64,7... | collective-permute-start | bytes 147464 | tf_op jit(solution)/shard_map/ppermute | solution.py:28
  103.1 5.4 %collective-permute-start.13 = (f32[3,1,32,128]{3,2,1,0:T(8,128)S(1)}, f32[3,1,32,128]{3,2,1,0:T(8,128)S(1)}, u32[]{:S(2)}, u32[]{:S(2)}) collective-permute-start(f32[3,1,32,128]{3,2,1,0:T(8,128)S(1)} %get-tuple-element.84), channel_id=1, source_target_pairs={{8,0},{16,8},{24,16},{32,24},{40,32},{48,40},{56,48},{64,56},{72,6... | collective-permute-start | bytes 147464 | tf_op jit(solution)/shard_map/ppermute | solution.py:29
  108.6 3.7 %collective-permute-start.14 = (f32[3,18,1,128]{3,2,1,0:T(1,128)S(1)}, f32[3,18,1,128]{3,2,1,0:T(1,128)S(1)}, u32[]{:S(2)}, u32[]{:S(2)}) collective-permute-start(f32[3,18,1,128]{3,2,1,0:T(1,128)S(1)} %get-tuple-element.73), channel_id=1, source_target_pairs={{0,1},{1,2},{2,3},{3,4},{4,5},{5,6},{6,7},{8,9},{9,10},{10,11},{11... | collective-permute-start | bytes 82952 | tf_op jit(solution)/shard_map/ppermute | solution.py:28
  110.8 4.6 %collective-permute-start.15 = (f32[3,18,1,128]{3,2,1,0:T(1,128)S(1)}, f32[3,18,1,128]{3,2,1,0:T(1,128)S(1)}, u32[]{:S(2)}, u32[]{:S(2)}) collective-permute-start(f32[3,18,1,128]{3,2,1,0:T(1,128)S(1)} %get-tuple-element.74), channel_id=1, source_target_pairs={{1,0},{2,1},{3,2},{4,3},{5,4},{6,5},{7,6},{9,8},{10,9},{11,10},{12... | collective-permute-start | bytes 82952 | tf_op jit(solution)/shard_map/ppermute | solution.py:29
  152.7 6.2 %collective-permute-start.16 = (f32[3,1,32,128]{3,2,1,0:T(8,128)S(1)}, f32[3,1,32,128]{3,2,1,0:T(8,128)S(1)}, u32[]{:S(2)}, u32[]{:S(2)}) collective-permute-start(f32[3,1,32,128]{3,2,1,0:T(8,128)S(1)} %get-tuple-element.81), channel_id=1, source_target_pairs={{0,8},{8,16},{16,24},{24,32},{32,40},{40,48},{48,56},{56,64},{64,7... | collective-permute-start | bytes 147464 | tf_op jit(solution)/shard_map/ppermute | solution.py:28
  156.9 5.4 %collective-permute-start.17 = (f32[3,1,32,128]{3,2,1,0:T(8,128)S(1)}, f32[3,1,32,128]{3,2,1,0:T(8,128)S(1)}, u32[]{:S(2)}, u32[]{:S(2)}) collective-permute-start(f32[3,1,32,128]{3,2,1,0:T(8,128)S(1)} %get-tuple-element.82), channel_id=1, source_target_pairs={{8,0},{16,8},{24,16},{32,24},{40,32},{48,40},{56,48},{64,56},{72,6... | collective-permute-start | bytes 147464 | tf_op jit(solution)/shard_map/ppermute | solution.py:29
  164.6 4.6 %collective-permute-start.19 = (f32[3,18,1,128]{3,2,1,0:T(1,128)S(1)}, f32[3,18,1,128]{3,2,1,0:T(1,128)S(1)}, u32[]{:S(2)}, u32[]{:S(2)}) collective-permute-start(f32[3,18,1,128]{3,2,1,0:T(1,128)S(1)} %get-tuple-element.72), channel_id=1, source_target_pairs={{1,0},{2,1},{3,2},{4,3},{5,4},{6,5},{7,6},{9,8},{10,9},{11,10},{12... | collective-permute-start | bytes 82952 | tf_op jit(solution)/shard_map/ppermute | solution.py:29
  206.1 6.2 %collective-permute-start.20 = (f32[3,1,32,128]{3,2,1,0:T(8,128)S(1)}, f32[3,1,32,128]{3,2,1,0:T(8,128)S(1)}, u32[]{:S(2)}, u32[]{:S(2)}) collective-permute-start(f32[3,1,32,128]{3,2,1,0:T(8,128)S(1)} %get-tuple-element.79), channel_id=1, source_target_pairs={{0,8},{8,16},{16,24},{24,32},{32,40},{40,48},{48,56},{56,64},{64,7... | collective-permute-start | bytes 147464 | tf_op jit(solution)/shard_map/ppermute | solution.py:28
  210.3 5.4 %collective-permute-start.21 = (f32[3,1,32,128]{3,2,1,0:T(8,128)S(1)}, f32[3,1,32,128]{3,2,1,0:T(8,128)S(1)}, u32[]{:S(2)}, u32[]{:S(2)}) collective-permute-start(f32[3,1,32,128]{3,2,1,0:T(8,128)S(1)} %get-tuple-element.80), channel_id=1, source_target_pairs={{8,0},{16,8},{24,16},{32,24},{40,32},{48,40},{56,48},{64,56},{72,6... | collective-permute-start | bytes 147464 | tf_op jit(solution)/shard_map/ppermute | solution.py:29
  215.7 3.8 %collective-permute-start.22 = (f32[3,18,1,128]{3,2,1,0:T(1,128)S(1)}, f32[3,18,1,128]{3,2,1,0:T(1,128)S(1)}, u32[]{:S(2)}, u32[]{:S(2)}) collective-permute-start(f32[3,18,1,128]{3,2,1,0:T(1,128)S(1)} %get-tuple-element.69), channel_id=1, source_target_pairs={{0,1},{1,2},{2,3},{3,4},{4,5},{5,6},{6,7},{8,9},{9,10},{10,11},{11... | collective-permute-start | bytes 82952 | tf_op jit(solution)/shard_map/ppermute | solution.py:28
  218.0 4.6 %collective-permute-start.23 = (f32[3,18,1,128]{3,2,1,0:T(1,128)S(1)}, f32[3,18,1,128]{3,2,1,0:T(1,128)S(1)}, u32[]{:S(2)}, u32[]{:S(2)}) collective-permute-start(f32[3,18,1,128]{3,2,1,0:T(1,128)S(1)} %get-tuple-element.70), channel_id=1, source_target_pairs={{1,0},{2,1},{3,2},{4,3},{5,4},{6,5},{7,6},{9,8},{10,9},{11,10},{12... | collective-permute-start | bytes 82952 | tf_op jit(solution)/shard_map/ppermute | solution.py:29
  225.3 11.9 %collective-permute-start.25 = (f32[1,32,128]{2,1,0:T(8,128)S(1)}, f32[1,32,128]{2,1,0:T(8,128)S(1)}, u32[]{:S(2)}, u32[]{:S(2)}) collective-permute-start(f32[1,32,128]{2,1,0:T(8,128)S(1)} %get-tuple-element.103), channel_id=1, source_target_pairs={{0,8},{8,16},{16,24},{24,32},{32,40},{40,48},{48,56},{56,64},{64,7... | collective-permute-start | bytes 49160 | tf_op jit(solution)/shard_map/ppermute | solution.py:42
  228.6 8.6 %collective-permute-start.24 = (f32[1,32,128]{2,1,0:T(8,128)S(1)}, f32[1,32,128]{2,1,0:T(8,128)S(1)}, u32[]{:S(2)}, u32[]{:S(2)}) collective-permute-start(f32[1,32,128]{2,1,0:T(8,128)S(1)} %get-tuple-element.104), channel_id=1, source_target_pairs={{8,0},{16,8},{24,16},{32,24},{40,32},{48,40},{56,48},{64,56},{72,6... | collective-permute-start | bytes 49160 | tf_op jit(solution)/shard_map/ppermute | solution.py:43
  232.7 4.4 %collective-permute-start.26 = (f32[16,1,128]{2,1,0:T(1,128)S(1)}, f32[16,1,128]{2,1,0:T(1,128)S(1)}, u32[]{:S(2)}, u32[]{:S(2)}) collective-permute-start(f32[16,1,128]{2,1,0:T(1,128)S(1)} %get-tuple-element.106), channel_id=1, source_target_pairs={{1,0},{2,1},{3,2},{4,3},{5,4},{6,5},{7,6},{9,8},{10,9},{11,10},{12... | collective-permute-start | bytes 24584 | tf_op jit(solution)/shard_map/ppermute | solution.py:43
  268.1 12.8 %collective-permute-start.29 = (f32[1,32,128]{2,1,0:T(8,128)S(1)}, f32[1,32,128]{2,1,0:T(8,128)S(1)}, u32[]{:S(2)}, u32[]{:S(2)}) collective-permute-start(f32[1,32,128]{2,1,0:T(8,128)S(1)} %get-tuple-element.99), channel_id=1, source_target_pairs={{0,8},{8,16},{16,24},{24,32},{32,40},{40,48},{48,56},{56,64},{64,7... | collective-permute-start | bytes 49160 | tf_op jit(solution)/shard_map/ppermute | solution.py:42
  272.4 8.6 %collective-permute-start.28 = (f32[1,32,128]{2,1,0:T(8,128)S(1)}, f32[1,32,128]{2,1,0:T(8,128)S(1)}, u32[]{:S(2)}, u32[]{:S(2)}) collective-permute-start(f32[1,32,128]{2,1,0:T(8,128)S(1)} %get-tuple-element.100), channel_id=1, source_target_pairs={{8,0},{16,8},{24,16},{32,24},{40,32},{48,40},{56,48},{64,56},{72,6... | collective-permute-start | bytes 49160 | tf_op jit(solution)/shard_map/ppermute | solution.py:43
  276.5 4.4 %collective-permute-start.30 = (f32[16,1,128]{2,1,0:T(1,128)S(1)}, f32[16,1,128]{2,1,0:T(1,128)S(1)}, u32[]{:S(2)}, u32[]{:S(2)}) collective-permute-start(f32[16,1,128]{2,1,0:T(1,128)S(1)} %get-tuple-element.102), channel_id=1, source_target_pairs={{1,0},{2,1},{3,2},{4,3},{5,4},{6,5},{7,6},{9,8},{10,9},{11,10},{12... | collective-permute-start | bytes 24584 | tf_op jit(solution)/shard_map/ppermute | solution.py:43
  312.2 12.8 %collective-permute-start.33 = (f32[1,32,128]{2,1,0:T(8,128)S(1)}, f32[1,32,128]{2,1,0:T(8,128)S(1)}, u32[]{:S(2)}, u32[]{:S(2)}) collective-permute-start(f32[1,32,128]{2,1,0:T(8,128)S(1)} %get-tuple-element.95), channel_id=1, source_target_pairs={{0,8},{8,16},{16,24},{24,32},{32,40},{40,48},{48,56},{56,64},{64,7... | collective-permute-start | bytes 49160 | tf_op jit(solution)/shard_map/ppermute | solution.py:42
  316.4 8.6 %collective-permute-start.32 = (f32[1,32,128]{2,1,0:T(8,128)S(1)}, f32[1,32,128]{2,1,0:T(8,128)S(1)}, u32[]{:S(2)}, u32[]{:S(2)}) collective-permute-start(f32[1,32,128]{2,1,0:T(8,128)S(1)} %get-tuple-element.96), channel_id=1, source_target_pairs={{8,0},{16,8},{24,16},{32,24},{40,32},{48,40},{56,48},{64,56},{72,6... | collective-permute-start | bytes 49160 | tf_op jit(solution)/shard_map/ppermute | solution.py:43
  320.6 4.4 %collective-permute-start.34 = (f32[16,1,128]{2,1,0:T(1,128)S(1)}, f32[16,1,128]{2,1,0:T(1,128)S(1)}, u32[]{:S(2)}, u32[]{:S(2)}) collective-permute-start(f32[16,1,128]{2,1,0:T(1,128)S(1)} %get-tuple-element.98), channel_id=1, source_target_pairs={{1,0},{2,1},{3,2},{4,3},{5,4},{6,5},{7,6},{9,8},{10,9},{11,10},{12... | collective-permute-start | bytes 24584 | tf_op jit(solution)/shard_map/ppermute | solution.py:43
  (15 other events, 234.2 us)
where the time goes:
time: 358 us; the launch traced here: 356 us
  blocking collectives  153 us (43%)
  starting transfers between devices  93.3 us (26%)
  other arithmetic  42.1 us (12%)
  waiting for transfers between devices  40.9 us (11%)
  between operations  20.4 us (6%)
  local copies, waits for them, and re-layouts  6.52 us (2%)
    all_to_all x12, blocking collectives, sent_to_all(): lax.all_to_all(jnp.broadcast_to(shard[None], (length, *shard.shape)), axi...  153 us
    ppermute x10, starting transfers between devices, padded_2(): before = lax.ppermute(last, axis, up)  37.3 us
    ppermute x10, waiting for transfers between devices, padded_2(): after = lax.ppermute(leading, axis, down)  31.6 us
    ppermute x8, starting transfers between devices, extended_2(): lax.ppermute(last, axis, up)  26.7 us
    ppermute x10, starting transfers between devices, padded_2(): after = lax.ppermute(leading, axis, down)  16.5 us
    ppermute x8, starting transfers between devices, extended_2(): lax.ppermute(leading, axis, [(b, a) for a, b in up])  12.9 us
    ppermute x8, waiting for transfers between devices, extended_2(): lax.ppermute(leading, axis, [(b, a) for a, b in up])  9.22 us
    concatenate x6, other arithmetic, packed_total(): jnp.concatenate([a.reshape(-1) for a in arrays])  7.94 us
  transfers between devices with their start and end apart: 36, of which 13 were waited for; matrix products, arithmetic and copies ran while one was open for 1% of the time, Pallas kernels for 0%

commit v1 on v0

v1 whole, which is shorter than its diff:
```python
import jax
import jax.numpy as jnp
from jax import lax
from jax.experimental import pallas as pl
from jax.experimental.pallas import tpu as pltpu
from jax.sharding import PartitionSpec as P

INTERPRET = False
f32 = jnp.float32

spring_term = 0.5
stiff_floor = 0.001
crack_load = 4.0
tough_ratio = 0.5
length_term = 2.0
bulk_half = 0.5 * (1.5 + 2.0 / 3.0)

LX, LY, LZ = 16, 32, 128
ROWS, DEPTH, OFF = 40, 23, 3

SHIFT_U = 14.0
SHIFT_D = 18.0


def call(kernel, outs, scratch=(), limit=8 << 20, name=None):
    vmem = pl.BlockSpec(memory_space=pltpu.VMEM)
    smem = pl.BlockSpec(memory_space=pltpu.SMEM)

    def run(*args, flags=None):
        specs = [vmem] * len(args)
        if flags is not None:
            args, specs = (*args, flags), specs + [smem]
        return pl.pallas_call(
            kernel,
            out_shape=[jax.ShapeDtypeStruct(s, f32) for s in outs],
            in_specs=specs,
            out_specs=[vmem] * len(outs),
            scratch_shapes=[pltpu.VMEM(s, f32) for s in scratch],
            compiler_params=pltpu.CompilerParams(vmem_limit_bytes=limit),
            interpret=INTERPRET,
            name=name,
        )(*args)

    return run


def roll(x, shift, axis):
    return pltpu.roll(x, shift % x.shape[axis], axis)


def next_row(x):
    return roll(x, -1, 0)


def last_row(x):
    return roll(x, 1, 0)


def lanes(shape):
    return lax.broadcasted_iota(jnp.int32, shape, 1)


def next_lane(x):
    return jnp.where(lanes(x.shape) == LZ - 1, 0.0, roll(x, -1, 1))


def last_lane(x):
    return jnp.where(lanes(x.shape) == 0, 0.0, roll(x, 1, 1))


def low_half():
    return lax.broadcasted_iota(jnp.int32, (8, LZ), 0) < 4


def pack_first(one, two):
    return jnp.where(low_half(), one, roll(two, 4, 0))


def pack_last(one, two):
    return jnp.where(low_half(), roll(two, 4, 0), one)


def unpack(high, low, second):
    if second:
        return roll(jnp.where(low_half(), low, high), 4, 0)
    return jnp.where(low_half(), high, low)


def row_mask(flags):
    row = lax.broadcasted_iota(jnp.int32, (ROWS, LZ), 0)
    return jnp.where(row < LY, 1.0, jnp.where(row < LY + 4, flags[3], flags[2]))


def layer_flag(flags, i):
    return jnp.where(i < OFF, flags[0], jnp.where(i >= OFF + LX, flags[1], 1.0))


def pack_rows_kernel(disp, force, damage, first, last):
    def pack(field, k, at):
        first[at, k] = pack_first(field(k, 0), field(k + 8, 0))
        last[at, k] = pack_last(field(k, 24), field(k + 8, 24))

    def step(k, carry):
        for j in range(3):
            pack(lambda i, r: disp[j, i, r : r + 8], k, j)
            pack(lambda i, r: force[j, i, r : r + 8], k, 3 + j)
        pack(lambda i, r: damage[i, r : r + 8], k, 6)
        return carry

    lax.fori_loop(0, 8, step, 0, unroll=2)


def pack_layers_kernel(disp, force, damage, high, low, first, last):
    def put(ref, at, own, field, c):
        ref[at, 0:LY] = own[c]
        ref[at, LY:ROWS] = unpack(high[field, c % 8], low[field, c % 8], c >= 8)

    at = bt = 0
    for field in range(7):
        own = disp.at[field] if field < 3 else force.at[field - 3] if field < 6 else damage
        ahead, behind = (3, 2) if 3 <= field < 6 else (4, 3)
        for c in range(ahead):
            put(first, at, own, field, c)
            at += 1
        for c in range(LX - behind, LX):
            put(last, bt, own, field, c)
            bt += 1


def stress(u, n, gain):
    dx = [n[j] - u[j] for j in range(3)]
    dy = [next_row(u[j]) - u[j] for j in range(3)]
    dz = [next_lane(u[j]) - u[j] for j in range(3)]
    twice = gain + gain
    part = 0.75 * (dx[0] + dy[1] + dz[2])
    return (
        twice * (dx[0] + part),
        twice * (dy[1] + part),
        twice * (dz[2] + part),
        gain * (dx[1] + dy[0]),
        gain * (dx[2] + dz[0]),
        gain * (dy[2] + dz[1]),
    )


def divergence(u, s, before, diag):
    s00, s11, s22, s01, s02, s12 = s
    return (
        diag * u[0] + before[0] + last_row(s01) + last_lane(s02) - (s00 + s01 + s02),
        diag * u[1] + before[1] + last_row(s11) + last_lane(s12) - (s01 + s11 + s12),
        diag * u[2] + before[2] + last_row(s12) + last_lane(s22) - (s02 + s12 + s22),
    )


def fold(x):
    return x[0:8] + x[8:16] + x[16:24] + x[24:32]


def moments_out(out, sums):
    lane = lanes((1, LZ))
    row = jnp.zeros((1, LZ), f32)
    for k, value in enumerate(sums):
        total = jnp.sum(jnp.sum(value, axis=0, keepdims=True), axis=1, keepdims=True)
        row = jnp.where(lane == k, total, row)
    out[...] = jnp.broadcast_to(row, out.shape)


def elastic_kernel(
    disp, force, damage, high, low, layers_high, layers_low, flags,
    wide, v0, v1, v2, wide_damage, sums, load, gain,
):
    for field in range(7):
        if field < 3:
            own, into, ahead, behind = disp.at[field], wide.at[field], 4, 3
        elif field < 6:
            own, into, ahead, behind = force.at[field - 3], load.at[field - 3], 3, 2
        else:
            own, into, ahead, behind = damage, wide_damage, 4, 3
        start = 4 * field if field < 3 else 12 + 3 * (field - 3) if field < 6 else 21
        into[OFF + LX : OFF + LX + ahead] = layers_high[start : start + ahead]
        start = 3 * field if field < 3 else 9 + 2 * (field - 3) if field < 6 else 15
        into[OFF - behind : OFF] = layers_low[start : start + behind]
        if 3 <= field < 6:
            into[0] = jnp.zeros((ROWS, LZ), f32)

        def assemble(k, carry):
            into[OFF + k, 0:LY] = own[k]
            into[OFF + k + 8, 0:LY] = own[k + 8]
            into[OFF + k, LY:ROWS] = unpack(high[field, k], low[field, k], False)
            into[OFF + k + 8, LY:ROWS] = unpack(high[field, k], low[field, k], True)
            return carry

        lax.fori_loop(0, 8, assemble, 0, unroll=2)

    rows = row_mask(flags)

    def fill_gain(i, carry):
        left = 1.0 - wide_damage[i]
        gain[i] = (left * left + stiff_floor) * (rows * layer_flag(flags, i))
        return carry

    lax.fori_loop(0, DEPTH - 1, fill_gain, 0)

    none = jnp.zeros((ROWS, LZ), f32)

    def sweep(source, begin, end, diag, store):
        def step(i, carry):
            before, u = carry
            n = tuple(source[j, i + 1] for j in range(3))
            s = stress(u, n, gain[i])
            store(i, divergence(u, s, before, diag))
            return (s[0], s[3], s[4]), n

        first = tuple(source[j, OFF + begin] for j in range(3))
        lax.fori_loop(OFF + begin, OFF + end, step, ((none,) * 3, first))

    def store0(i, image):
        mask = rows * layer_flag(flags, i)
        for j in range(3):
            v0[j, i] = (load[j, i] - image[j]) * mask

    def store_to(ref):
        def store(i, image):
            mask = rows * layer_flag(flags, i)
            for j in range(3):
                ref[j, i] = image[j] * mask

        return store

    sweep(wide, -3, LX + 3, spring_term, store0)
    sweep(v0, -2, LX + 2, spring_term - SHIFT_U, store_to(v1))
    sweep(v1, -1, LX + 1, spring_term - SHIFT_U, store_to(v2))

    def add(c, acc):
        u = [v2[j, OFF + c] for j in range(3)]
        n = [v2[j, OFF + c + 1, 0:LY] for j in range(3)]
        up = [next_row(u[j])[0:LY] for j in range(3)]
        u = [u[j][0:LY] for j in range(3)]
        dx = [n[j] - u[j] for j in range(3)]
        dy = [up[j] - u[j] for j in range(3)]
        dz = [next_lane(u[j]) - u[j] for j in range(3)]
        trace = dx[0] + dy[1] + dz[2]
        e01, e02, e12 = dx[1] + dy[0], dx[2] + dz[0], dy[2] + dz[1]
        work = 2.0 * (dx[0] * dx[0] + dy[1] * dy[1] + dz[2] * dz[2])
        work = work + 1.5 * (trace * trace) + (e01 * e01 + e02 * e02 + e12 * e12)
        work = gain[OFF + c, 0:LY] * work
        a = [v0[j, OFF + c, 0:LY] for j in range(3)]
        b = [v1[j, OFF + c, 0:LY] for j in range(3)]

        def dot(x, y):
            return x[0] * y[0] + x[1] * y[1] + x[2] * y[2]

        square = dot(u, u)
        new = (
            dot(a, a), dot(a, b), dot(b, b), dot(b, u), square,
            work + (spring_term - SHIFT_U) * square,
        )
        return tuple(x + fold(y) for x, y in zip(acc, new))

    zero = jnp.zeros((8, LZ), f32)
    moments_out(sums, lax.fori_loop(0, LX, add, (zero,) * 6))


def coefficients(gathered, shift):
    row = jnp.sum(gathered[...], axis=0, keepdims=True)
    lane = lanes((1, LZ))
    mu = [
        jnp.broadcast_to(
            jnp.sum(jnp.where(lane == k, row, 0.0), axis=1, keepdims=True), (1, LZ)
        )
        for k in range(6)
    ]

    def inner(a, b, up=0):
        total = None
        for i, x in enumerate(a):
            for j, y in enumerate(b):
                term = x * y * mu[i + j + up]
                total = term if total is None else total + term
        return total

    one = jnp.ones((1, LZ), f32)
    resid, direction = [one], [one]
    found = []
    norm = mu[0]
    for number in range(3):
        work = inner(direction, direction, 1) + shift * inner(direction, direction)
        alpha = norm / work
        for i, x in enumerate(direction):
            if i < len(found):
                found[i] = found[i] + alpha * x
            else:
                found.append(alpha * x)
        if number < 2:
            image = [shift * x for x in direction] + [jnp.zeros((1, LZ), f32)]
            for i, x in enumerate(direction):
                image[i + 1] = image[i + 1] + x
            resid = [
                (resid[i] if i < len(resid) else 0.0) - alpha * x for i, x in enumerate(image)
            ]
            new = inner(resid, resid)
            ratio = new / norm
            direction = [
                x + ratio * direction[i] if i < len(direction) else x
                for i, x in enumerate(resid)
            ]
            norm = new
    return found


def history_kernel(
    gathered, wide, v0, v1, v2, history, crack, moved, found, first, last
):
    a0, a1, a2 = coefficients(gathered, SHIFT_U)

    def current(c):
        return tuple(
            wide[j, OFF + c] + a0 * v0[j, OFF + c] + a1 * v1[j, OFF + c] + a2 * v2[j, OFF + c]
            for j in range(3)
        )

    def step(c, u):
        n = current(c + 1)
        for j in range(3):
            moved[j, c] = u[j][0:LY]
        up = [next_row(u[j])[0:LY] for j in range(3)]
        here = [u[j][0:LY] for j in range(3)]
        dx = [n[j][0:LY] - here[j] for j in range(3)]
        dy = [up[j] - here[j] for j in range(3)]
        dz = [next_lane(here[j]) - here[j] for j in range(3)]
        trace = dx[0] + dy[1] + dz[2]
        e01, e02, e12 = dx[1] + dy[0], dx[2] + dz[0], dy[2] + dz[1]
        squares = dx[0] * dx[0] + dy[1] * dy[1] + dz[2] * dz[2]
        squares = squares + 0.5 * (e01 * e01 + e02 * e02 + e12 * e12)
        positive = jnp.maximum(trace, 0.0)
        psi = bulk_half * (positive * positive) + (squares - trace * trace / 3.0)
        flagged = crack_load * crack[c].astype(f32)
        found[c] = jnp.maximum(jnp.maximum(history[c], psi), flagged)
        return n

    lax.fori_loop(0, LX, step, current(0))

    def pack(k, carry):
        first[k] = pack_first(found[k, 0:8], found[k + 8, 0:8])
        last[k] = pack_last(found[k, 24:32], found[k + 8, 24:32])
        return carry

    lax.fori_loop(0, 8, pack, 0, unroll=2)


def pack_history_kernel(found, high, low, first, last):
    for at in range(3):
        first[at, 0:LY] = found[at]
        first[at, LY:ROWS] = unpack(high[at], low[at], False)
    for at, c in enumerate((LX - 2, LX - 1)):
        last[at, 0:LY] = found[c]
        last[at, LY:ROWS] = unpack(high[c - 8], low[c - 8], True)


def damage_kernel(
    found, high, low, layers_high, layers_low, wide_damage, flags, w0, w1, w2, sums, drive
):
    drive[OFF + LX : OFF + LX + 3] = layers_high[...]
    drive[OFF - 2 : OFF] = layers_low[...]

    def assemble(k, carry):
        drive[OFF + k, 0:LY] = found[k]
        drive[OFF + k + 8, 0:LY] = found[k + 8]
        drive[OFF + k, LY:ROWS] = unpack(high[k], low[k], False)
        drive[OFF + k + 8, LY:ROWS] = unpack(high[k], low[k], True)
        return carry

    lax.fori_loop(0, 8, assemble, 0, unroll=2)
    rows = row_mask(flags)

    def sweep(source, begin, end, store):
        def step(i, carry):
            before, now = carry
            n = source[i + 1]
            beside = before + n + next_row(now) + last_row(now)
            beside = beside + next_lane(now) + last_lane(now)
            store(i, now, beside)
            return now, n

        start = OFF + begin
        lax.fori_loop(start, OFF + end, step, (source[start - 1], source[start]))

    full = tough_ratio + 6.0 * length_term

    def store0(i, now, beside):
        twice = 2.0 * drive[i]
        image = (full + twice) * now - length_term * beside
        w0[i] = (twice - image) * (rows * layer_flag(flags, i))

    def store_to(ref):
        def store(i, now, beside):
            diag = (full - SHIFT_D) + 2.0 * drive[i]
            ref[i] = (diag * now - length_term * beside) * (rows * layer_flag(flags, i))

        return store

    sweep(wide_damage, -2, LX + 3, store0)
    sweep(w0, -1, LX + 2, store_to(w1))
    sweep(w1, 0, LX + 1, store_to(w2))

    lane = lanes((LY, LZ))
    row = lax.broadcasted_iota(jnp.int32, (LY, LZ), 0)
    edge = jnp.where(lane == 0, length_term, 0.0)
    edge = edge + jnp.where(row == 0, length_term * (1.0 - flags[2]), 0.0)
    edge = edge + (tough_ratio - SHIFT_D)

    def add(c, acc):
        wide_now = w2[OFF + c]
        u = wide_now[0:LY]
        dx = w2[OFF + c + 1, 0:LY] - u
        dy = next_row(wide_now)[0:LY] - u
        dz = next_lane(u) - u
        side = jnp.where(c == 0, length_term * (1.0 - flags[0]), 0.0)
        square = u * u
        work = (edge + side + 2.0 * drive[OFF + c, 0:LY]) * square
        work = work + length_term * (dx * dx + dy * dy + dz * dz)
        a, b = w0[OFF + c, 0:LY], w1[OFF + c, 0:LY]
        new = (a * a, a * b, b * b, b * u, square, work)
        return tuple(x + fold(y) for x, y in zip(acc, new))

    zero = jnp.zeros((8, LZ), f32)
    moments_out(sums, lax.fori_loop(0, LX, add, (zero,) * 6))


def update_kernel(gathered, damage, w0, w1, w2, out):
    b0, b1, b2 = coefficients(gathered, SHIFT_D)

    def step(c, carry):
        image = b0 * w0[OFF + c, 0:LY] + b1 * w1[OFF + c, 0:LY] + b2 * w2[OFF + c, 0:LY]
        out[c] = damage[c] + image
        return carry

    lax.fori_loop(0, LX, step, 0, unroll=2)


def exchange(first, last, axis):
    size = lax.axis_size(axis)
    up = [(i, i + 1) for i in range(size - 1)]
    down = [(b, a) for a, b in up]
    return lax.ppermute(first, axis, down), lax.ppermute(last, axis, up)


def body(displacement, force, damage, history, crack_flags):
    both = ("gx", "gy")
    count = lax.axis_size(both)
    ix, iy = lax.axis_index("gx"), lax.axis_index("gy")
    flags = jnp.stack(
        [ix > 0, ix < lax.axis_size("gx") - 1, iy > 0, iy < lax.axis_size("gy") - 1]
    ).astype(f32)
    wide_shape = (3, DEPTH, ROWS, LZ)
    field_shape = (DEPTH, ROWS, LZ)

    def gather(sums):
        return lax.all_to_all(sums, both, 0, 0, tiled=True)

    rows = call(pack_rows_kernel, [(7, 8, 8, LZ)] * 2, name="pack_rows")(
        displacement, force, damage
    )
    high, low = exchange(*rows, "gy")
    layers = call(pack_layers_kernel, [(25, ROWS, LZ), (18, ROWS, LZ)], name="pack_layers")(
        displacement, force, damage, high, low
    )
    layers_high, layers_low = exchange(*layers, "gx")
    wide, v0, v1, v2, wide_damage, sums = call(
        elastic_kernel,
        [wide_shape] * 4 + [field_shape, (count, LZ)],
        [wide_shape, field_shape],
        name="elastic",
        limit=16 << 20,
    )(displacement, force, damage, high, low, layers_high, layers_low, flags=flags)
    moved, found, first, last = call(
        history_kernel,
        [(3, LX, LY, LZ), (LX, LY, LZ), (8, 8, LZ), (8, 8, LZ)],
        name="history",
    )(gather(sums), wide, v0, v1, v2, history, crack_flags)
    high, low = exchange(first, last, "gy")
    layers = call(pack_history_kernel, [(3, ROWS, LZ), (2, ROWS, LZ)], name="pack_history")(
        found, high, low
    )
    layers_high, layers_low = exchange(*layers, "gx")
    w0, w1, w2, sums = call(
        damage_kernel, [field_shape] * 3 + [(count, LZ)], [field_shape], name="damage"
    )(found, high, low, layers_high, layers_low, wide_damage, flags=flags)
    (damage_out,) = call(update_kernel, [(LX, LY, LZ)], name="update")(
        gather(sums), damage, w0, w1, w2
    )
    return moved, damage_out, found


def solution(mesh):
    return jax.shard_map(
        body,
        mesh=mesh,
        in_specs=(
            P(None, "gx", "gy", None),
            P(None, "gx", "gy", None),
            P("gx", "gy", None),
            P("gx", "gy", None),
            P("gx", "gy", None),
        ),
        out_specs=(P(None, "gx", "gy", None), P("gx", "gy", None), P("gx", "gy", None)),
        check_vma=False,
    )
```

time: 358 us -> 121 us (0.34)
  blocking collectives: 153 us -> 55.7 us
  starting transfers between devices: 93.3 us -> 25 us
  other arithmetic: 42.1 us -> 0.08 us
  waiting for transfers between devices: 40.9 us -> 9.96 us
  Pallas kernels: 0 us -> 23.9 us
  between operations: 20.4 us -> 0.78 us
    all_to_all x12 -> x2, blocking collectives: 153 us -> 55.7 us  [gather(): return lax.all_to_all(sums, both, 0, 0, tiled=True)]
    ppermute x36 -> x8, starting transfers between devices: 93.3 us -> 25 us  [exchange(): return (lax.ppermute(first, axis, down), lax.ppermute(last, axis, up))]
    ppermute x36 -> x8, waiting for transfers between devices: 40.9 us -> 9.96 us  [exchange(): return (lax.ppermute(first, axis, down), lax.ppermute(last, axis, up))]
    pallas_call x0 -> x7, Pallas kernels: none -> 23.9 us  [run(): pl.pallas_call(kernel, out_shape=[jax.ShapeDtypeStruct(s, f32) for s in o...]
    concatenate x15 -> x0, other arithmetic: 14.5 us -> none  [the longest x6 7.94 us: packed_total(): jnp.concatenate([a.reshape(-1) for a in arrays])]
    mul x8 -> x0, other arithmetic: 7.93 us -> none  [the longest x4 4.72 us: elastic(): weight * (2.0 * shear_modulus * strain[index])]
    reduce_sum x18 -> x0, other arithmetic: 6.3 us -> none  [the longest x6 5.88 us: paired_sums(): jnp.sum(resid * resid)]
    another operation x9 -> x0, other arithmetic: 5.78 us -> none  [the longest x8 4.72 us: elastic(): return (jnp.stack(images), strain)]
  transfers between devices with their start and end apart: 36 -> 8, of which waited for: 13 -> 6; matrix products, arithmetic and copies ran while one was open for 1% -> 0% of each run, Pallas kernels for 0% -> 0%
where the time goes in v1:
time: 121 us
  blocking collectives  55.7 us (46%)
  starting transfers between devices  25 us (21%)
  Pallas kernels  23.9 us (20%)
  waiting for transfers between devices  9.96 us (8%)
  local copies, waits for them, and re-layouts  5.14 us (4%)
    all_to_all x2, blocking collectives, gather(): return lax.all_to_all(sums, both, 0, 0, tiled=True)  55.7 us
    ppermute x8, starting transfers between devices, exchange(): return (lax.ppermute(first, axis, down), lax.ppermute(last, axis, up))  25 us
    pallas_call x7, Pallas kernels, run(): pl.pallas_call(kernel, out_shape=[jax.ShapeDtypeStruct(s, f32) for s in o...  23.9 us
    ppermute x8, waiting for transfers between devices, exchange(): return (lax.ppermute(first, axis, down), lax.ppermute(last, axis, up))  9.96 us
    unnamed x20, local copies, waits for them, and re-layouts  5.14 us
  transfers between devices with their start and end apart: 8, of which 6 were waited for; matrix products, arithmetic and copies ran while one was open for 0% of the time, Pallas kernels for 0%

profile of v1, /device:TPU:1, one launch (start us, length us, event | category | flops | bytes accessed | tf_op | source)
XLA Modules:
  0.0 120.5 jit_solution(8556129461469893971)
XLA Ops:
  0.6 0.0 copy-start
  0.6 1.1 copy-done
  1.8 1.1 copy-done.2
  2.9 0.9 copy-done.4
  3.9 0.1 pack_rows.1
  3.9 0.0 copy-start.1
  3.9 0.0 copy-start.3
  4.0 0.0 copy-start.5
  4.0 1.4 %collective-permute-start = (f32[7,8,8,128]{3,2,1,0:T(8,128)S(1)}, f32[7,8,8,128]{3,2,1,0:T(8,128)S(1)}, u32[]{:S(2)}, u32[]{:S(2)}) collective-permute-start(f32[7,8,8,128]{3,2,1,0:T(8,128)S(1)} %get-tuple-element.23), channel_id=1, source_target_pairs={{1,0},{2,1},{3,2},{4,3},{5,4},{6,5},{7,6},{9,8},{10,9},{11,10},{12... | collective-permute-start | bytes 688136 | tf_op jit(solution)/shard_map/ppermute | solution.py:445
  5.4 5.0 %collective-permute-start.1 = (f32[7,8,8,128]{3,2,1,0:T(8,128)S(1)}, f32[7,8,8,128]{3,2,1,0:T(8,128)S(1)}, u32[]{:S(2)}, u32[]{:S(2)}) collective-permute-start(f32[7,8,8,128]{3,2,1,0:T(8,128)S(1)} %get-tuple-element.24), channel_id=1, source_target_pairs={{0,1},{1,2},{2,3},{3,4},{4,5},{5,6},{6,7},{8,9},{9,10},{10,11},{11... | collective-permute-start | bytes 688136 | tf_op jit(solution)/shard_map/ppermute | solution.py:445
  10.4 1.5 %collective-permute-done.high = f32[7,8,8,128]{3,2,1,0:T(8,128)S(1)} collective-permute-done((f32[7,8,8,128]{3,2,1,0:T(8,128)S(1)}, f32[7,8,8,128]{3,2,1,0:T(8,128)S(1)}, u32[]{:S(2)}, u32[]{:S(2)}) %collective-permute-start) | collective-permute-done | bytes 229408 | tf_op jit(solution)/shard_map/ppermute | solution.py:445
  11.9 1.5 %collective-permute-done.1.low = f32[7,8,8,128]{3,2,1,0:T(8,128)S(1)} collective-permute-done((f32[7,8,8,128]{3,2,1,0:T(8,128)S(1)}, f32[7,8,8,128]{3,2,1,0:T(8,128)S(1)}, u32[]{:S(2)}, u32[]{:S(2)}) %collective-permute-start.1) | collective-permute-done | bytes 229408 | tf_op jit(solution)/shard_map/ppermute | solution.py:445
  13.3 0.8 pack_layers.1
  14.2 5.2 %collective-permute-start.2 = (f32[25,40,128]{2,1,0:T(8,128)}, f32[25,40,128]{2,1,0:T(8,128)S(1)}, u32[]{:S(2)}, u32[]{:S(2)}) collective-permute-start(f32[25,40,128]{2,1,0:T(8,128)} %get-tuple-element.25), channel_id=1, source_target_pairs={{8,0},{16,8},{24,16},{32,24},{40,32},{48,40},{56,48},{64,56},{72,6... | collective-permute-start | bytes 1536008 | tf_op jit(solution)/shard_map/ppermute | solution.py:445
  19.4 2.5 %collective-permute-start.3 = (f32[18,40,128]{2,1,0:T(8,128)S(1)}, f32[18,40,128]{2,1,0:T(8,128)S(1)}, u32[]{:S(2)}, u32[]{:S(2)}) collective-permute-start(f32[18,40,128]{2,1,0:T(8,128)S(1)} %get-tuple-element.26), channel_id=1, source_target_pairs={{0,8},{8,16},{16,24},{24,32},{32,40},{40,48},{48,56},{56,64},{64,7... | collective-permute-start | bytes 1105928 | tf_op jit(solution)/shard_map/ppermute | solution.py:445
  22.0 0.1 add_convert_fusion.flags
  22.1 4.3 %collective-permute-done.3.layers_low = f32[18,40,128]{2,1,0:T(8,128)S(1)} collective-permute-done((f32[18,40,128]{2,1,0:T(8,128)S(1)}, f32[18,40,128]{2,1,0:T(8,128)S(1)}, u32[]{:S(2)}, u32[]{:S(2)}) %collective-permute-start.3) | collective-permute-done | bytes 368672 | tf_op jit(solution)/shard_map/ppermute | solution.py:445
  26.4 0.6 collective-permute-done.2.layers_high
  27.0 12.6 %elastic.1 = (f32[3,23,40,128]{3,2,1,0:T(8,128)S(1)}, f32[3,23,40,128]{3,2,1,0:T(8,128)S(1)}, f32[3,23,40,128]{3,2,1,0:T(8,128)S(1)}, f32[3,23,40,128]{3,2,1,0:T...) custom-call(f32[3,16,32,128]{3,2,1,0:T(8,128)S(1)} %copy-done.1, f32[3,16,32,128]{3,2,1,0:T(8,128)S(1)} %copy-done.3, ...), custom_call_target="tpu_custom_call" | custom-call | tf_op jit(solution)/shard_map/elastic/pallas_call | solution.py:33
  39.6 30.5 %all_to_all.22 = f32[256,1,128]{2,1,0:T(1,128)S(1)} all-to-all(f32[256,1,128]{2,1,0:T(1,128)S(1)} %bitcast.14), channel_id=1, replica_groups=mesh['gx'=32,'gy'=8] {'gx','gy'}, dimensions={0} | all-to-all | bytes 262144 | tf_op jit(solution)/shard_map/all_to_all | solution.py:459
  70.1 2.7 %history.2 = (f32[3,16,32,128]{3,2,1,0:T(8,128)}, f32[16,32,128]{2,1,0:T(8,128)}, f32[8,8,128]{2,1,0:T(8,128)S(1)}, f32[8,8,128]{2,1,0:T(8,128)S(1)}) custom-call(f32[256,128]{1,0:T(8,128)S(1)} %bitcast.12, f32[3,23,40,128]{3,2,1,0:T(8,128)S(1)} %get-tuple-element.28.wide, f32[3,23,40,128]{3,2,1,0:T(8,128)S(1)} %get-tuple-element.29.v0, ...), custom_call_target="tpu_custom_call" | custom-call | tf_op jit(solution)/shard_map/history/pallas_call | solution.py:33
  72.8 1.3 %collective-permute-start.4 = (f32[8,8,128]{2,1,0:T(8,128)S(1)}, f32[8,8,128]{2,1,0:T(8,128)S(1)}, u32[]{:S(2)}, u32[]{:S(2)}) collective-permute-start(f32[8,8,128]{2,1,0:T(8,128)S(1)} %get-tuple-element.34), channel_id=1, source_target_pairs={{1,0},{2,1},{3,2},{4,3},{5,4},{6,5},{7,6},{9,8},{10,9},{11,10},{12... | collective-permute-start | bytes 98312 | tf_op jit(solution)/shard_map/ppermute | solution.py:445
  74.1 4.0 %collective-permute-start.5 = (f32[8,8,128]{2,1,0:T(8,128)S(1)}, f32[8,8,128]{2,1,0:T(8,128)S(1)}, u32[]{:S(2)}, u32[]{:S(2)}) collective-permute-start(f32[8,8,128]{2,1,0:T(8,128)S(1)} %get-tuple-element.35), channel_id=1, source_target_pairs={{0,1},{1,2},{2,3},{3,4},{4,5},{5,6},{6,7},{8,9},{9,10},{10,11},{11... | collective-permute-start | bytes 98312 | tf_op jit(solution)/shard_map/ppermute | solution.py:445
  78.1 1.0 collective-permute-done.5.low
  79.1 0.9 copy-done.6
  80.0 3.6 %collective-permute-start.6 = (f32[3,40,128]{2,1,0:T(8,128)S(1)}, f32[3,40,128]{2,1,0:T(8,128)S(1)}, u32[]{:S(2)}, u32[]{:S(2)}) collective-permute-start(f32[3,40,128]{2,1,0:T(8,128)S(1)} %get-tuple-element.36), channel_id=1, source_target_pairs={{8,0},{16,8},{24,16},{32,24},{40,32},{48,40},{56,48},{64,56},{72,6... | collective-permute-start | bytes 184328 | tf_op jit(solution)/shard_map/ppermute | solution.py:445
  83.6 2.0 %collective-permute-start.7 = (f32[2,40,128]{2,1,0:T(8,128)S(1)}, f32[2,40,128]{2,1,0:T(8,128)S(1)}, u32[]{:S(2)}, u32[]{:S(2)}) collective-permute-start(f32[2,40,128]{2,1,0:T(8,128)S(1)} %get-tuple-element.37), channel_id=1, source_target_pairs={{0,8},{8,16},{16,24},{24,32},{32,40},{40,48},{48,56},{56,64},{64,7... | collective-permute-start | bytes 122888 | tf_op jit(solution)/shard_map/ppermute | solution.py:445
  85.6 1.1 collective-permute-done.7.layers_low
  86.7 0.9 copy-done.7
  87.7 6.7 %damage.8 = (f32[23,40,128]{2,1,0:T(8,128)S(1)}, f32[23,40,128]{2,1,0:T(8,128)S(1)}, f32[23,40,128]{2,1,0:T(8,128)S(1)}, f32[256,128]{1,0:T(8,128)S(1)}) custom-call(f32[16,32,128]{2,1,0:T(8,128)S(1)} %copy-done.7, f32[8,8,128]{2,1,0:T(8,128)S(1)} %collective-permute-done.4.high, f32[8,8,128]{2,1,0:T(8,128)S(1)} %collective-permute-done.5.low, ...), custom_call_target="tpu_custom_call" | custom-call | tf_op jit(solution)/shard_map/damage/pallas_call | solution.py:33
  94.4 25.2 %all_to_all.23 = f32[256,1,128]{2,1,0:T(1,128)S(1)} all-to-all(f32[256,1,128]{2,1,0:T(1,128)S(1)} %bitcast.15), channel_id=1, replica_groups=mesh['gx'=32,'gy'=8] {'gx','gy'}, dimensions={0} | all-to-all | bytes 262144 | tf_op jit(solution)/shard_map/all_to_all | solution.py:459
  119.5 1.0 update.1
  (14 shorter events, 0.0 us)
Async XLA Ops:
  0.6 1.1 copy-start
  1.8 1.1 copy-start.2
  2.9 0.9 copy-start.4
  3.9 23.0 %copy-start.1 = (f32[3,16,32,128]{3,2,1,0:T(8,128)S(1)}, f32[3,16,32,128]{3,2,1,0:T(8,128)}, u32[]{:S(2)}) copy-start(f32[3,16,32,128]{3,2,1,0:T(8,128)} %disp.5) | copy-start | bytes 2359300
  3.9 23.0 %copy-start.3 = (f32[3,16,32,128]{3,2,1,0:T(8,128)S(1)}, f32[3,16,32,128]{3,2,1,0:T(8,128)}, u32[]{:S(2)}) copy-start(f32[3,16,32,128]{3,2,1,0:T(8,128)} %force.5) | copy-start | bytes 2359300
  4.0 23.0 %copy-start.5 = (f32[16,32,128]{2,1,0:T(8,128)S(1)}, f32[16,32,128]{2,1,0:T(8,128)}, u32[]{:S(2)}) copy-start(f32[16,32,128]{2,1,0:T(8,128)} %damage.9) | copy-start | bytes 786436
  4.0 7.9 %collective-permute-start = (f32[7,8,8,128]{3,2,1,0:T(8,128)S(1)}, f32[7,8,8,128]{3,2,1,0:T(8,128)S(1)}, u32[]{:S(2)}, u32[]{:S(2)}) collective-permute-start(f32[7,8,8,128]{3,2,1,0:T(8,128)S(1)} %get-tuple-element.23), channel_id=1, source_target_pairs={{1,0},{2,1},{3,2},{4,3},{5,4},{6,5},{7,6},{9,8},{10,9},{11,10},{12... | collective-permute-start | bytes 688136 | tf_op jit(solution)/shard_map/ppermute | solution.py:445
  5.4 7.9 %collective-permute-start.1 = (f32[7,8,8,128]{3,2,1,0:T(8,128)S(1)}, f32[7,8,8,128]{3,2,1,0:T(8,128)S(1)}, u32[]{:S(2)}, u32[]{:S(2)}) collective-permute-start(f32[7,8,8,128]{3,2,1,0:T(8,128)S(1)} %get-tuple-element.24), channel_id=1, source_target_pairs={{0,1},{1,2},{2,3},{3,4},{4,5},{5,6},{6,7},{8,9},{9,10},{10,11},{11... | collective-permute-start | bytes 688136 | tf_op jit(solution)/shard_map/ppermute | solution.py:445
  14.2 12.8 %collective-permute-start.2 = (f32[25,40,128]{2,1,0:T(8,128)}, f32[25,40,128]{2,1,0:T(8,128)S(1)}, u32[]{:S(2)}, u32[]{:S(2)}) collective-permute-start(f32[25,40,128]{2,1,0:T(8,128)} %get-tuple-element.25), channel_id=1, source_target_pairs={{8,0},{16,8},{24,16},{32,24},{40,32},{48,40},{56,48},{64,56},{72,6... | collective-permute-start | bytes 1536008 | tf_op jit(solution)/shard_map/ppermute | solution.py:445
  19.4 7.0 %collective-permute-start.3 = (f32[18,40,128]{2,1,0:T(8,128)S(1)}, f32[18,40,128]{2,1,0:T(8,128)S(1)}, u32[]{:S(2)}, u32[]{:S(2)}) collective-permute-start(f32[18,40,128]{2,1,0:T(8,128)S(1)} %get-tuple-element.26), channel_id=1, source_target_pairs={{0,8},{8,16},{16,24},{24,32},{32,40},{40,48},{48,56},{56,64},{64,7... | collective-permute-start | bytes 1105928 | tf_op jit(solution)/shard_map/ppermute | solution.py:445
  22.1 48.0 %copy-start.8 = (f32[16,32,128]{2,1,0:T(8,128)S(1)}, f32[16,32,128]{2,1,0:T(8,128)}, u32[]{:S(2)}) copy-start(f32[16,32,128]{2,1,0:T(8,128)} %history.3) | copy-start | bytes 786436
  22.1 48.0 %copy-start.9 = (s32[16,32,128]{2,1,0:T(8,128)S(1)}, s32[16,32,128]{2,1,0:T(8,128)}, u32[]{:S(2)}) copy-start(s32[16,32,128]{2,1,0:T(8,128)} %crack.1) | copy-start | bytes 786436
  72.8 5.3 %collective-permute-start.4 = (f32[8,8,128]{2,1,0:T(8,128)S(1)}, f32[8,8,128]{2,1,0:T(8,128)S(1)}, u32[]{:S(2)}, u32[]{:S(2)}) collective-permute-start(f32[8,8,128]{2,1,0:T(8,128)S(1)} %get-tuple-element.34), channel_id=1, source_target_pairs={{1,0},{2,1},{3,2},{4,3},{5,4},{6,5},{7,6},{9,8},{10,9},{11,10},{12... | collective-permute-start | bytes 98312 | tf_op jit(solution)/shard_map/ppermute | solution.py:445
  74.1 5.0 %collective-permute-start.5 = (f32[8,8,128]{2,1,0:T(8,128)S(1)}, f32[8,8,128]{2,1,0:T(8,128)S(1)}, u32[]{:S(2)}, u32[]{:S(2)}) collective-permute-start(f32[8,8,128]{2,1,0:T(8,128)S(1)} %get-tuple-element.35), channel_id=1, source_target_pairs={{0,1},{1,2},{2,3},{3,4},{4,5},{5,6},{6,7},{8,9},{9,10},{10,11},{11... | collective-permute-start | bytes 98312 | tf_op jit(solution)/shard_map/ppermute | solution.py:445
  79.1 0.9 copy-start.6
  80.0 6.7 %collective-permute-start.6 = (f32[3,40,128]{2,1,0:T(8,128)S(1)}, f32[3,40,128]{2,1,0:T(8,128)S(1)}, u32[]{:S(2)}, u32[]{:S(2)}) collective-permute-start(f32[3,40,128]{2,1,0:T(8,128)S(1)} %get-tuple-element.36), channel_id=1, source_target_pairs={{8,0},{16,8},{24,16},{32,24},{40,32},{48,40},{56,48},{64,56},{72,6... | collective-permute-start | bytes 184328 | tf_op jit(solution)/shard_map/ppermute | solution.py:445
  83.6 3.1 %collective-permute-start.7 = (f32[2,40,128]{2,1,0:T(8,128)S(1)}, f32[2,40,128]{2,1,0:T(8,128)S(1)}, u32[]{:S(2)}, u32[]{:S(2)}) collective-permute-start(f32[2,40,128]{2,1,0:T(8,128)S(1)} %get-tuple-element.37), channel_id=1, source_target_pairs={{0,8},{8,16},{16,24},{24,32},{32,40},{40,48},{48,56},{56,64},{64,7... | collective-permute-start | bytes 122888 | tf_op jit(solution)/shard_map/ppermute | solution.py:445
  86.7 1.0 copy-start.7

commit v2 on v1

v2 whole, which is shorter than its diff:
```python
import jax
import jax.numpy as jnp
from jax import lax
from jax.experimental import pallas as pl
from jax.experimental.pallas import tpu as pltpu
from jax.sharding import PartitionSpec as P


INTERPRET = False
f32 = jnp.float32

spring_term = 0.5
stiff_floor = 0.001
crack_load = 4.0
tough_ratio = 0.5
length_term = 2.0
bulk_half = 0.5 * (1.5 + 2.0 / 3.0)

LX, LY, LZ = 16, 32, 128
ROWS, SHORT, DEPTH, OFF = 48, 40, 23, 3

SHIFT_U = 14.0
SHIFT_D = 18.0

VECTOR = (3, DEPTH, ROWS, LZ)
SCALAR = (DEPTH, ROWS, LZ)
BRIEF = (DEPTH, SHORT, LZ)


def call(kernel, outs, scratch=(), limit=8 << 20, aliases=None, hbm=False):
    vmem = pl.BlockSpec(memory_space=pltpu.VMEM)
    smem = pl.BlockSpec(memory_space=pltpu.SMEM)

    def run(*args, flags=None):
        specs = [pl.BlockSpec(memory_space=pl.ANY) if hbm else vmem] * len(args)
        if flags is not None:
            args, specs = (*args, flags), specs + [smem]
        return pl.pallas_call(
            kernel,
            out_shape=[jax.ShapeDtypeStruct(s, f32) for s in outs],
            in_specs=specs,
            out_specs=[vmem] * len(outs),
            scratch_shapes=[pltpu.VMEM(s, f32) if isinstance(s, tuple) else s for s in scratch],
            input_output_aliases=aliases or {},
            compiler_params=pltpu.CompilerParams(vmem_limit_bytes=limit),
            interpret=INTERPRET,
        )(*args)

    return run


def roll(x, shift, axis):
    return pltpu.roll(x, shift % x.shape[axis], axis)


def next_row(x):
    return roll(x, -1, 0)


def last_row(x):
    return roll(x, 1, 0)


def lanes(shape):
    return lax.broadcasted_iota(jnp.int32, shape, 1)


def next_lane(x):
    return jnp.where(lanes(x.shape) == LZ - 1, 0.0, roll(x, -1, 1))


def last_lane(x):
    return jnp.where(lanes(x.shape) == 0, 0.0, roll(x, 1, 1))


def tile_row():
    return lax.broadcasted_iota(jnp.int32, (8, LZ), 0)


def pack_first(u, load, damage, past):
    row = tile_row()
    tiles = [jnp.where(row == 7, roll(past, 7 - j, 0), u[j]) for j in range(3)]
    return tiles + [jnp.where(row < 6, load[j], roll(damage, 6 - 2 * j, 0)) for j in range(3)]


def pack_last(u, load, damage, past):
    row = tile_row()
    return list(u) + [
        jnp.where(row < 4, roll(damage, 4, 0), load[0]),
        jnp.where(row < 4, damage, load[1]),
        jnp.where(row < 4, roll(past, 4, 0), load[2]),
    ]


def damage_tiles(high, low, k):
    row = tile_row()
    above = jnp.where(row < 2, roll(high[3, k], 2, 0), roll(high[4, k], 4, 0))
    above = jnp.where(row < 4, above, roll(high[5, k], 6, 0))
    below = jnp.where(row < 4, low[4, k], roll(low[3, k], 4, 0))
    return above, below


def past_tile(high, low, k):
    row = tile_row()
    above = jnp.where(row < 1, roll(high[0, k], 1, 0), roll(high[1, k], 2, 0))
    above = jnp.where(row < 2, above, roll(high[2, k], 3, 0))
    return jnp.where(row < 4, above, roll(low[5, k], 4, 0))


def brief(above, below):
    return jnp.where(tile_row() < 4, above, below)


def row_mask(flags):
    row = lax.broadcasted_iota(jnp.int32, (ROWS - LY, LZ), 0)
    return jnp.where(row < 8, flags[3], flags[2])


def pack_rows_kernel(
    disp, force, damage, history, crack, first, last, top, bottom, top_crack, bottom_crack, sem
):
    copies = []
    for rows, into, into_crack in ((0, top, top_crack), (24, bottom, bottom_crack)):
        for source, target in (
            (disp.at[:, :, rows : rows + 8], into.at[0:3]),
            (force.at[:, :, rows : rows + 8], into.at[3:6]),
            (damage.at[:, rows : rows + 8], into.at[6]),
            (history.at[:, rows : rows + 8], into.at[7]),
            (crack.at[:, rows : rows + 8], into_crack),
        ):
            copies.append(pltpu.make_async_copy(source, target, sem.at[len(copies)]))
    for copy in copies:
        copy.start()
    for copy in copies:
        copy.wait()

    def step(k, carry):
        for into, flag, out, pack in (
            (top, top_crack, first, pack_first),
            (bottom, bottom_crack, last, pack_last),
        ):
            past = jnp.maximum(into[7, k], crack_load * flag[k].astype(f32))
            tiles = pack(
                [into[j, k] for j in range(3)], [into[3 + j, k] for j in range(3)],
                into[6, k], past,
            )
            for at, tile in enumerate(tiles):
                out[at, k] = tile
        return carry

    lax.fori_loop(0, LX, step, 0, unroll=2)


def pack_layers_kernel(disp, force, damage, high, low, first, last):
    at = {True: 0, False: 0}
    for field in range(7):
        own = disp.at[field] if field < 3 else force.at[field - 3] if field < 6 else damage
        ahead, behind = (3, 2) if 3 <= field < 6 else (4, 3)
        for c in (*range(ahead), *range(LX - behind, LX)):
            out, front = (first, True) if c < ahead else (last, False)
            if field < 6:
                above, below = high[field, c], low[field, c]
            else:
                above, below = damage_tiles(high, low, c)
            out[at[front], 0:LY] = own[c]
            out[at[front], LY : LY + 8] = above
            out[at[front], LY + 8 : ROWS] = below
            at[front] += 1


def stress(u, n, gain):
    dx = [n[j] - u[j] for j in range(3)]
    dy = [next_row(u[j]) - u[j] for j in range(3)]
    dz = [next_lane(u[j]) - u[j] for j in range(3)]
    twice = gain + gain
    part = 0.75 * (dx[0] + dy[1] + dz[2])
    return (
        twice * (dx[0] + part),
        twice * (dy[1] + part),
        twice * (dz[2] + part),
        gain * (dx[1] + dy[0]),
        gain * (dx[2] + dz[0]),
        gain * (dy[2] + dz[1]),
    )


def divergence(u, s, before, diag):
    s00, s11, s22, s01, s02, s12 = s
    return (
        diag * u[0] + before[0] + last_row(s01) + last_lane(s02) - (s00 + s01 + s02),
        diag * u[1] + before[1] + last_row(s11) + last_lane(s12) - (s01 + s11 + s12),
        diag * u[2] + before[2] + last_row(s12) + last_lane(s22) - (s02 + s12 + s22),
    )


def vector(ref, i):
    return tuple(ref[j, i] for j in range(3))


def sweep(source, gain, begin, end, diag, store, unroll=None):
    u, n = vector(source, begin), vector(source, begin + 1)
    s = stress(u, n, gain[begin])

    def step(i, carry):
        before, u = carry
        n = vector(source, i + 1)
        s = stress(u, n, gain[i])
        store(i, divergence(u, s, before, diag))
        return (s[0], s[3], s[4]), n

    carry = ((s[0], s[3], s[4]), n)
    if unroll is None:
        for i in range(begin + 1, end):
            carry = step(i, carry)
    else:
        lax.fori_loop(begin + 1, end, step, carry, unroll=unroll)


def store_to(ref, mask, flag=None, load=None):
    def store(i, image):
        for j in range(3):
            value = image[j] if load is None else load(j, i) - image[j]
            own, rest = value[0:LY], value[LY:ROWS] * mask
            if flag is not None:
                own, rest = own * flag, rest * flag
            ref[j, i, 0:LY] = own
            ref[j, i, LY:ROWS] = rest

    return store


def fold(x):
    return x[0:8] + x[8:16] + x[16:24] + x[24:32]


def moments_out(out, sums):
    lane = lanes((1, LZ))
    row = jnp.zeros((1, LZ), f32)
    for k, value in enumerate(sums):
        total = jnp.sum(jnp.sum(value, axis=0, keepdims=True), axis=1, keepdims=True)
        row = jnp.where(lane == k, total, row)
    out[...] = jnp.broadcast_to(row, out.shape)


def elastic_moments(v0, v1, v2, gain):
    def add(i, acc):
        u = vector(v2, i)
        up = [next_row(x)[0:LY] for x in u]
        u = [x[0:LY] for x in u]
        dx = [v2[j, i + 1, 0:LY] - u[j] for j in range(3)]
        dy = [up[j] - u[j] for j in range(3)]
        dz = [next_lane(u[j]) - u[j] for j in range(3)]
        trace = dx[0] + dy[1] + dz[2]
        e01, e02, e12 = dx[1] + dy[0], dx[2] + dz[0], dy[2] + dz[1]
        work = 2.0 * (dx[0] * dx[0] + dy[1] * dy[1] + dz[2] * dz[2])
        work = work + 1.5 * (trace * trace) + (e01 * e01 + e02 * e02 + e12 * e12)
        work = gain[i, 0:LY] * work
        a = [v0[j, i, 0:LY] for j in range(3)]
        b = [v1[j, i, 0:LY] for j in range(3)]

        def dot(x, y):
            return x[0] * y[0] + x[1] * y[1] + x[2] * y[2]

        square = dot(u, u)
        new = (
            dot(a, a), dot(a, b), dot(b, b), dot(b, u), square,
            work + (spring_term - SHIFT_U) * square,
        )
        return tuple(x + fold(y) for x, y in zip(acc, new))

    return add


def inner_kernel(
    disp, force, damage, history, crack, high, low, flags,
    wide, load, gain, v0, v1, v2, short_damage, past, partial,
):
    mask = row_mask(flags)

    def assemble(k, carry):
        i = OFF + k
        for j in range(3):
            wide[j, i, 0:LY] = disp[j, k]
            wide[j, i, LY : LY + 8] = high[j, k]
            wide[j, i, LY + 8 : ROWS] = low[j, k]
            load[j, k, 0:LY] = force[j, k]
            load[j, k, LY : LY + 8] = high[3 + j, k]
            load[j, k, LY + 8 : ROWS] = low[3 + j, k]
        own = damage[k]
        above, below = damage_tiles(high, low, k)
        short_damage[i, 0:LY] = own
        short_damage[i, LY:SHORT] = brief(above, below)
        left = 1.0 - own
        gain[i, 0:LY] = left * left + stiff_floor
        left = 1.0 - above
        gain[i, LY : LY + 8] = (left * left + stiff_floor) * mask[0:8]
        left = 1.0 - below
        gain[i, LY + 8 : ROWS] = (left * left + stiff_floor) * mask[8:16]
        past[k, 0:LY] = jnp.maximum(history[k], crack_load * crack[k].astype(f32))
        past[k, LY:SHORT] = past_tile(high, low, k)
        return carry

    lax.fori_loop(0, LX, assemble, 0, unroll=2)
    diag = spring_term - SHIFT_U
    first = store_to(v0, mask, load=lambda j, i: load[j, i - OFF])
    sweep(wide, gain, OFF, OFF + 15, spring_term, first, unroll=UNROLL)
    sweep(v0, gain, OFF + 1, OFF + 14, diag, store_to(v1, mask), unroll=UNROLL)
    sweep(v1, gain, OFF + 2, OFF + 13, diag, store_to(v2, mask), unroll=UNROLL)
    zero = jnp.zeros((8, LZ), f32)
    add = elastic_moments(v0, v1, v2, gain)
    for k, value in enumerate(
        lax.fori_loop(OFF + 3, OFF + 12, add, (zero,) * 6, unroll=3)
    ):
        partial[k] = value


UNROLL = 4


def outer_kernel(
    wide_in, load, gain_in, v0_in, v1_in, v2_in, short_in, past, partial,
    layers_high, layers_low, flags,
    wide, gain, v0, v1, v2, short_damage, sums, first, last,
):
    mask = row_mask(flags)
    for j in range(3):
        wide[j, OFF + LX : DEPTH] = layers_high[4 * j : 4 * j + 4]
        wide[j, 0:OFF] = layers_low[3 * j : 3 * j + 3]
    for side, count, at, base, flag in (
        (layers_high, 4, OFF + LX, 21, flags[1]), (layers_low, 3, 0, 15, flags[0])
    ):
        for c in range(count):
            value = side[base + c]
            short_damage[at + c, 0:LY] = value[0:LY]
            short_damage[at + c, LY:SHORT] = brief(value[LY : LY + 8], value[LY + 8 : ROWS])
            left = 1.0 - value
            value = (left * left + stiff_floor) * flag
            gain[at + c, 0:LY] = value[0:LY]
            gain[at + c, LY:ROWS] = value[LY:ROWS] * mask

    def force_at(j, i):
        if i < OFF:
            return layers_low[9 + 2 * j + i - 1]
        if i >= OFF + LX:
            return layers_high[12 + 3 * j + i - OFF - LX]
        return load[j, i - OFF]

    def both(source, target, low_end, high_begin, diag, load=None):
        def store(i, image):
            flag = flags[0] if i < OFF else flags[1] if i >= OFF + LX else None
            store_to(target, mask, flag, load)(i, image)

        begin = low_end - 4
        sweep(source, gain, begin, low_end, diag, store)
        sweep(source, gain, high_begin, high_begin + 5, diag, store)

    diag = spring_term - SHIFT_U
    both(wide, v0, OFF + 1, OFF + 14, spring_term, force_at)
    both(v0, v1, OFF + 2, OFF + 13, diag)
    both(v1, v2, OFF + 3, OFF + 12, diag)

    add = elastic_moments(v0, v1, v2, gain)
    acc = tuple(partial[k] for k in range(6))
    for i in (*range(OFF, OFF + 3), *range(OFF + 12, OFF + 16)):
        acc = add(i, acc)
    moments_out(sums, acc)

    def put(out, at, ref, j, c):
        out[at, 0:LY] = ref[j, OFF + c, 0:LY]
        out[at, LY:SHORT] = brief(ref[j, OFF + c, LY : LY + 8], ref[j, OFF + c, LY + 8 : ROWS])

    for j in range(3):
        put(first, j, v0, j, 3)
        for c in range(2):
            put(first, 3 + 2 * j + c, v1, j, 2 + c)
            put(last, 3 + 2 * j + c, v2, j, 14 + c)
        for c in range(3):
            put(first, 9 + 3 * j + c, v2, j, 1 + c)
        put(last, j, v1, j, 14)
    first[18:21] = past[0:3]
    last[9:11] = past[14:16]


def coefficients(gathered, shift):
    row = jnp.sum(gathered[...], axis=0, keepdims=True)
    lane = lanes((1, LZ))
    mu = [
        jnp.broadcast_to(
            jnp.sum(jnp.where(lane == k, row, 0.0), axis=1, keepdims=True), (1, LZ)
        )
        for k in range(6)
    ]

    def inner(a, b, up=0):
        total = None
        for i, x in enumerate(a):
            for j, y in enumerate(b):
                term = x * y * mu[i + j + up]
                total = term if total is None else total + term
        return total

    one = jnp.ones((1, LZ), f32)
    resid, direction = [one], [one]
    found = []
    norm = mu[0]
    for number in range(3):
        work = inner(direction, direction, 1) + shift * inner(direction, direction)
        alpha = norm / work
        for i, x in enumerate(direction):
            if i < len(found):
                found[i] = found[i] + alpha * x
            else:
                found.append(alpha * x)
        if number < 2:
            image = [shift * x for x in direction] + [jnp.zeros((1, LZ), f32)]
            for i, x in enumerate(direction):
                image[i + 1] = image[i + 1] + x
            resid = [
                (resid[i] if i < len(resid) else 0.0) - alpha * x for i, x in enumerate(image)
            ]
            new = inner(resid, resid)
            ratio = new / norm
            direction = [
                x + ratio * direction[i] if i < len(direction) else x
                for i, x in enumerate(resid)
            ]
            norm = new
    return found


def damage_kernel(
    gathered, wide, v0, v1, v2, short_damage, past, high, low, flags,
    moved, found, w0, w1, w2, sums, now, drive,
):
    a0, a1, a2 = coefficients(gathered, SHIFT_U)

    def cut(value):
        return value[0:LY], brief(value[LY : LY + 8], value[LY + 8 : ROWS])

    def put(j, i, base, far):
        body, rest = cut(base)
        now[j, i, 0:LY] = body
        now[j, i, LY:SHORT] = rest
        if far is not None:
            now[j, i] = now[j, i] + far

    def middle(i, carry):
        for j in range(3):
            value = wide[j, i] + a0 * v0[j, i] + a1 * v1[j, i] + a2 * v2[j, i]
            put(j, i, value, None)
            moved[j, i - OFF] = value[0:LY]
        return carry

    lax.fori_loop(OFF, OFF + LX, middle, 0, unroll=2)
    for j in range(3):
        i = OFF + LX
        put(j, i, wide[j, i] + a0 * v0[j, i] + a1 * v1[j, i] + a2 * v2[j, i], None)
        i = OFF - 2
        put(j, i, wide[j, i] + a0 * v0[j, i], a1 * low[j] + a2 * low[3 + 2 * j])
        i = OFF - 1
        put(j, i, wide[j, i] + a0 * v0[j, i] + a1 * v1[j, i], a2 * low[4 + 2 * j])
        i = OFF + LX + 1
        put(j, i, wide[j, i] + a0 * v0[j, i] + a1 * v1[j, i], a2 * high[9 + 3 * j])
        i = OFF + LX + 2
        put(j, i, wide[j, i] + a0 * v0[j, i], a1 * high[3 + 2 * j] + a2 * high[10 + 3 * j])
        i = OFF + LX + 3
        far = a0 * high[j] + a1 * high[4 + 2 * j] + a2 * high[11 + 3 * j]
        put(j, i, wide[j, i], far)

    row = lax.broadcasted_iota(jnp.int32, (8, LZ), 0)
    mask = jnp.where(row < 4, flags[3], flags[2])

    def energy(i):
        u, n = vector(now, i), vector(now, i + 1)
        dx = [n[j] - u[j] for j in range(3)]
        dy = [next_row(u[j]) - u[j] for j in range(3)]
        dz = [next_lane(u[j]) - u[j] for j in range(3)]
        trace = dx[0] + dy[1] + dz[2]
        e01, e02, e12 = dx[1] + dy[0], dx[2] + dz[0], dy[2] + dz[1]
        squares = dx[0] * dx[0] + dy[1] * dy[1] + dz[2] * dz[2]
        squares = squares + 0.5 * (e01 * e01 + e02 * e02 + e12 * e12)
        positive = jnp.maximum(trace, 0.0)
        return bulk_half * (positive * positive) + (squares - trace * trace * (1.0 / 3.0))

    def step(i, carry):
        value = jnp.maximum(past[i - OFF], energy(i))
        drive[i] = value
        found[i - OFF] = value[0:LY]
        return carry

    lax.fori_loop(OFF, OFF + LX, step, 0, unroll=4)
    for c in range(3):
        i = OFF + LX + c
        drive[i] = jnp.maximum(high[18 + c], energy(i))
    for c in range(2):
        i = OFF - 2 + c
        drive[i] = jnp.maximum(low[9 + c], energy(i))

    def flag_of(i):
        return jnp.where(i < OFF, flags[0], jnp.where(i >= OFF + LX, flags[1], 1.0))

    def apply(source, begin, end, make, target):
        def step(i, carry):
            before, here = carry
            n = source[i + 1]
            beside = before + n + next_row(here) + last_row(here)
            beside = beside + next_lane(here) + last_lane(here)
            value = make(i, here, beside) * flag_of(i)
            target[i, 0:LY] = value[0:LY]
            target[i, LY:SHORT] = value[LY:SHORT] * mask
            return here, n

        lax.fori_loop(begin, end, step, (source[begin - 1], source[begin]), unroll=4)

    full = tough_ratio + 6.0 * length_term

    def start(i, here, beside):
        twice = 2.0 * drive[i]
        return twice - ((full + twice) * here - length_term * beside)

    def image(i, here, beside):
        return ((full - SHIFT_D) + 2.0 * drive[i]) * here - length_term * beside

    apply(short_damage, OFF - 2, OFF + LX + 3, start, w0)
    apply(w0, OFF - 1, OFF + LX + 2, image, w1)
    apply(w1, OFF, OFF + LX + 1, image, w2)

    lane = lanes((LY, LZ))
    row = lax.broadcasted_iota(jnp.int32, (LY, LZ), 0)
    edge = jnp.where(lane == 0, length_term, 0.0)
    edge = edge + jnp.where(row == 0, length_term * (1.0 - flags[2]), 0.0)
    edge = edge + (tough_ratio - SHIFT_D)

    def add(i, acc):
        wide_now = w2[i]
        u = wide_now[0:LY]
        dx = w2[i + 1, 0:LY] - u
        dy = next_row(wide_now)[0:LY] - u
        dz = next_lane(u) - u
        side = jnp.where(i == OFF, length_term * (1.0 - flags[0]), 0.0)
        square = u * u
        work = (edge + side + 2.0 * drive[i, 0:LY]) * square
        work = work + length_term * (dx * dx + dy * dy + dz * dz)
        a, b = w0[i, 0:LY], w1[i, 0:LY]
        new = (a * a, a * b, b * b, b * u, square, work)
        return tuple(x + fold(y) for x, y in zip(acc, new))

    zero = jnp.zeros((8, LZ), f32)
    moments_out(sums, lax.fori_loop(OFF, OFF + LX, add, (zero,) * 6, unroll=4))


def update_kernel(gathered, damage, w0, w1, w2, out):
    b0, b1, b2 = coefficients(gathered, SHIFT_D)

    def step(c, carry):
        i = OFF + c
        image = b0 * w0[i, 0:LY] + b1 * w1[i, 0:LY] + b2 * w2[i, 0:LY]
        out[c] = damage[c] + image
        return carry

    lax.fori_loop(0, LX, step, 0, unroll=2)


def exchange(first, last, axis):
    size = lax.axis_size(axis)
    up = [(i, i + 1) for i in range(size - 1)]
    down = [(b, a) for a, b in up]
    high = lax.ppermute(first, axis, down)
    low = lax.ppermute(last, axis, up)
    return high, low


def step(displacement, force, damage, history, crack_flags):
    axes = ("gx", "gy")
    count = lax.axis_size(axes)
    ix, iy = lax.axis_index("gx"), lax.axis_index("gy")
    flags = jnp.stack(
        [ix > 0, ix < lax.axis_size("gx") - 1, iy > 0, iy < lax.axis_size("gy") - 1]
    ).astype(f32)

    def gather(sums):
        return lax.all_to_all(sums, axes, 0, 0, tiled=True)

    edge_rows = (8, LX, 8, LZ)
    rows = call(
        pack_rows_kernel,
        [(6, LX, 8, LZ)] * 2,
        [
            edge_rows, edge_rows,
            pltpu.VMEM((LX, 8, LZ), jnp.int32), pltpu.VMEM((LX, 8, LZ), jnp.int32),
            pltpu.SemaphoreType.DMA((10,)),
        ],
        hbm=True,
    )(displacement, force, damage, history, crack_flags)
    high, low = exchange(*rows, "gy")
    layers = call(pack_layers_kernel, [(25, ROWS, LZ), (18, ROWS, LZ)])(
        displacement, force, damage, high, low
    )
    layers_high, layers_low = exchange(*layers, "gx")
    wide, load, gain, v0, v1, v2, short_damage, past, partial = call(
        inner_kernel,
        [VECTOR, (3, LX, ROWS, LZ), SCALAR, VECTOR, VECTOR, VECTOR, BRIEF]
        + [(LX, SHORT, LZ), (6, 8, LZ)],
    )(displacement, force, damage, history, crack_flags, high, low, flags=flags)
    wide, gain, v0, v1, v2, short_damage, sums, first, last = call(
        outer_kernel,
        [VECTOR, SCALAR, VECTOR, VECTOR, VECTOR, BRIEF]
        + [(count, LZ), (21, SHORT, LZ), (11, SHORT, LZ)],
        aliases={0: 0, 2: 1, 3: 2, 4: 3, 5: 4, 6: 5},
    )(
        wide, load, gain, v0, v1, v2, short_damage, past, partial,
        layers_high, layers_low, flags=flags,
    )
    high, low = exchange(first, last, "gx")
    gathered = gather(sums)
    moved, found, w0, w1, w2, sums = call(
        damage_kernel,
        [(3, LX, LY, LZ), (LX, LY, LZ), BRIEF, BRIEF, BRIEF, (count, LZ)],
        [(3, DEPTH, SHORT, LZ), BRIEF],
    )(gathered, wide, v0, v1, v2, short_damage, past, high, low, flags=flags)
    (damage_out,) = call(update_kernel, [(LX, LY, LZ)])(
        gather(sums), damage, w0, w1, w2
    )
    return moved, damage_out, found


def solution(mesh):
    return jax.shard_map(
        step,
        mesh=mesh,
        in_specs=(
            P(None, "gx", "gy", None),
            P(None, "gx", "gy", None),
            P("gx", "gy", None),
            P("gx", "gy", None),
            P("gx", "gy", None),
        ),
        out_specs=(P(None, "gx", "gy", None), P("gx", "gy", None), P("gx", "gy", None)),
        check_vma=False,
    )
```

time: 121 us -> 112 us (0.926)
  blocking collectives: 55.7 us -> 20.9 us
  local copies, waits for them, and re-layouts: 5.14 us -> 19.7 us
  starting transfers between devices: 25 us -> 37.6 us
  Pallas kernels: 23.9 us -> 16.8 us
  waiting for transfers between devices: 9.96 us -> 15.4 us
    all_to_all x2 -> x1, blocking collectives: 55.7 us -> 20.9 us  [gather(): return lax.all_to_all(sums, axes, 0, 0, tiled=True)]
    all_to_all x0 -> x1, starting transfers between devices: none -> 17.3 us  [gather(): return lax.all_to_all(sums, axes, 0, 0, tiled=True)]
    unnamed x20 -> x48, local copies, waits for them, and re-layouts: 5.14 us -> 19.7 us
    pallas_call x7 -> x6, Pallas kernels: 23.9 us -> 16.8 us  [run(): pl.pallas_call(kernel, out_shape=[jax.ShapeDtypeStruct(s, f32) for s in o...]
    all_to_all x0 -> x1, waiting for transfers between devices: none -> 5.96 us  [gather(): return lax.all_to_all(sums, axes, 0, 0, tiled=True)]
    ppermute x8 -> x6, starting transfers between devices: 25 us -> 20.3 us  [the longest x3 11.6 us: exchange(): low = lax.ppermute(last, axis, up)]
    ppermute x8 -> x6, waiting for transfers between devices: 9.96 us -> 9.42 us  [the longest x3 5.06 us: exchange(): high = lax.ppermute(first, axis, down)]
  transfers between devices with their start and end apart: 8 -> 7, of which waited for: 6 -> 4; matrix products, arithmetic and copies ran while one was open for 0% -> 0% of each run, Pallas kernels for 0% -> 4%
where the time goes in v2:
time: 112 us; the launch traced here: 111 us
  starting transfers between devices  37.6 us (34%)
  blocking collectives  20.9 us (19%)
  local copies, waits for them, and re-layouts  19.7 us (18%)
  Pallas kernels  16.8 us (15%)
  waiting for transfers between devices  15.4 us (14%)
    all_to_all x1, blocking collectives, gather(): return lax.all_to_all(sums, axes, 0, 0, tiled=True)  20.9 us
    unnamed x48, local copies, waits for them, and re-layouts  19.7 us
    all_to_all x1, starting transfers between devices, gather(): return lax.all_to_all(sums, axes, 0, 0, tiled=True)  17.3 us
    pallas_call x6, Pallas kernels, run(): pl.pallas_call(kernel, out_shape=[jax.ShapeDtypeStruct(s, f32) for s in o...  16.8 us
    ppermute x3, starting transfers between devices, exchange(): low = lax.ppermute(last, axis, up)  11.6 us
    ppermute x3, starting transfers between devices, exchange(): high = lax.ppermute(first, axis, down)  8.7 us
    all_to_all x1, waiting for transfers between devices, gather(): return lax.all_to_all(sums, axes, 0, 0, tiled=True)  5.96 us
    ppermute x3, waiting for transfers between devices, exchange(): high = lax.ppermute(first, axis, down)  5.06 us
  transfers between devices with their start and end apart: 7, of which 4 were waited for; matrix products, arithmetic and copies ran while one was open for 0% of the time, Pallas kernels for 4%

profile of v2, /device:TPU:1, one launch (start us, length us, event | category | flops | bytes accessed | tf_op | source)
XLA Modules:
  0.0 111.3 jit_solution(10217063124082903468)
XLA Ops:
  0.6 1.1 %copy-done = f32[3,16,32,128]{3,2,1,0:T(8,128)S(1)} copy-done((f32[3,16,32,128]{3,2,1,0:T(8,128)S(1)}, f32[3,16,32,128]{3,2,1,0:T(8,128)}, u32[]{:S(2)}) %copy-start) | copy-done | bytes 786456
  1.8 1.1 %copy-done.2 = f32[3,16,32,128]{3,2,1,0:T(8,128)S(1)} copy-done((f32[3,16,32,128]{3,2,1,0:T(8,128)S(1)}, f32[3,16,32,128]{3,2,1,0:T(8,128)}, u32[]{:S(2)}) %copy-start.2) | copy-done | bytes 786456
  2.9 0.9 copy-done.10
  3.9 0.9 copy-done.20
  4.8 0.9 copy-done.22
  6.2 1.4 %collective-permute-start = (f32[6,16,8,128]{3,2,1,0:T(8,128)S(1)}, f32[6,16,8,128]{3,2,1,0:T(8,128)S(1)}, u32[]{:S(2)}, u32[]{:S(2)}) collective-permute-start(f32[6,16,8,128]{3,2,1,0:T(8,128)S(1)} %get-tuple-element.30), channel_id=1, source_target_pairs={{1,0},{2,1},{3,2},{4,3},{5,4},{6,5},{7,6},{9,8},{10,9},{11,10},{12... | collective-permute-start | bytes 1179656 | tf_op jit(solution)/shard_map/ppermute | solution.py:568
  7.6 5.0 %collective-permute-start.1 = (f32[6,16,8,128]{3,2,1,0:T(8,128)S(1)}, f32[6,16,8,128]{3,2,1,0:T(8,128)S(1)}, u32[]{:S(2)}, u32[]{:S(2)}) collective-permute-start(f32[6,16,8,128]{3,2,1,0:T(8,128)S(1)} %get-tuple-element.31), channel_id=1, source_target_pairs={{0,1},{1,2},{2,3},{3,4},{4,5},{5,6},{6,7},{8,9},{9,10},{10,11},{11... | collective-permute-start | bytes 1179656 | tf_op jit(solution)/shard_map/ppermute | solution.py:569
  12.6 5.0 %collective-permute-done.high = f32[6,16,8,128]{3,2,1,0:T(8,128)S(1)} collective-permute-done((f32[6,16,8,128]{3,2,1,0:T(8,128)S(1)}, f32[6,16,8,128]{3,2,1,0:T(8,128)S(1)}, u32[]{:S(2)}, u32[]{:S(2)}) %collective-permute-start) | collective-permute-done | bytes 393248 | tf_op jit(solution)/shard_map/ppermute | solution.py:568
  18.6 1.1 shard_map.78
  19.7 5.2 %collective-permute-start.2 = (f32[25,48,128]{2,1,0:T(8,128)}, f32[25,48,128]{2,1,0:T(8,128)}, u32[]{:S(2)}, u32[]{:S(2)}) collective-permute-start(f32[25,48,128]{2,1,0:T(8,128)} %get-tuple-element.41), channel_id=1, source_target_pairs={{8,0},{16,8},{24,16},{32,24},{40,32},{48,40},{56,48},{64,56},{72,6... | collective-permute-start | bytes 1843208 | tf_op jit(solution)/shard_map/ppermute | solution.py:568
  24.9 3.0 %collective-permute-start.3 = (f32[18,48,128]{2,1,0:T(8,128)}, f32[18,48,128]{2,1,0:T(8,128)}, u32[]{:S(2)}, u32[]{:S(2)}) collective-permute-start(f32[18,48,128]{2,1,0:T(8,128)} %get-tuple-element.42), channel_id=1, source_target_pairs={{0,8},{8,16},{16,24},{24,32},{32,40},{40,48},{48,56},{56,64},{64,7... | collective-permute-start | bytes 1327112 | tf_op jit(solution)/shard_map/ppermute | solution.py:569
  28.1 1.0 copy-done.15
  29.1 1.0 copy-done.17
  31.0 0.9 copy-done.23
  32.0 4.8 %shard_map.77 = (f32[3,23,48,128]{3,2,1,0:T(8,128)S(1)}, f32[3,16,48,128]{3,2,1,0:T(8,128)S(1)}, f32[23,48,128]{2,1,0:T(8,128)S(1)}, f32[3,23,48,128]{3,2,1,0:T(...) custom-call(f32[3,16,32,128]{3,2,1,0:T(8,128)S(1)} %copy-done.1, ...), custom_call_target="tpu_custom_call" | custom-call | tf_op jit(solution)/shard_map/pallas_call | solution.py:38
  36.8 4.4 %shard_map.79 = (f32[3,23,48,128]{3,2,1,0:T(8,128)S(1)}, f32[23,48,128]{2,1,0:T(8,128)S(1)}, f32[3,23,48,128]{3,2,1,0:T(8,128)S(1)}, f32[3,23,48,128]{3,2,1,0:T(...) custom-call(f32[3,23,48,128]{3,2,1,0:T(8,128)S(1)} %get-tuple-elemen, ...), custom_call_target="tpu_custom_call", output_to_operand_aliasing={{0}: (0, {}), {1}: (2, {}), {2}: (3, {}), {3}: (4, {}), {4}... | custom-call | tf_op jit(solution)/shard_map/pallas_call | solution.py:38
  41.2 1.2 %copy-done.4 = f32[3,23,48,128]{3,2,1,0:T(8,128)} copy-done((f32[3,23,48,128]{3,2,1,0:T(8,128)}, f32[3,23,48,128]{3,2,1,0:T(8,128)S(1)}, u32[]{:S(2)}) %copy-start.4) | copy-done | bytes 1695768
  42.4 1.2 %copy-done.6 = f32[3,23,48,128]{3,2,1,0:T(8,128)} copy-done((f32[3,23,48,128]{3,2,1,0:T(8,128)}, f32[3,23,48,128]{3,2,1,0:T(8,128)S(1)}, u32[]{:S(2)}) %copy-start.6) | copy-done | bytes 1695768
  43.5 1.2 %copy-done.8 = f32[3,23,48,128]{3,2,1,0:T(8,128)} copy-done((f32[3,23,48,128]{3,2,1,0:T(8,128)}, f32[3,23,48,128]{3,2,1,0:T(8,128)S(1)}, u32[]{:S(2)}) %copy-start.8) | copy-done | bytes 1695768
  45.5 2.0 %collective-permute-start.4 = (f32[21,40,128]{2,1,0:T(8,128)S(1)}, f32[21,40,128]{2,1,0:T(8,128)S(1)}, u32[]{:S(2)}, u32[]{:S(2)}) collective-permute-start(f32[21,40,128]{2,1,0:T(8,128)S(1)} %get-tuple-element.49), channel_id=1, source_target_pairs={{8,0},{16,8},{24,16},{32,24},{40,32},{48,40},{56,48},{64,56},{72,6... | collective-permute-start | bytes 1290248 | tf_op jit(solution)/shard_map/ppermute | solution.py:568
  47.6 17.3 %all-to-all-start = ((f32[256,1,128]{2,1,0:T(1,128)}), f32[256,1,128]{2,1,0:T(1,128)S(1)}, u32[]{:S(2)}, u32[]{:S(2)}) async-start(f32[256,1,128]{2,1,0:T(1,128)} %bitcast.5), calls=%async_computation | async-start | bytes 262144 | tf_op jit(solution)/shard_map/all_to_all | solution.py:582
  64.9 3.5 %collective-permute-start.5 = (f32[11,40,128]{2,1,0:T(8,128)S(1)}, f32[11,40,128]{2,1,0:T(8,128)S(1)}, u32[]{:S(2)}, u32[]{:S(2)}) collective-permute-start(f32[11,40,128]{2,1,0:T(8,128)S(1)} %get-tuple-element.50), channel_id=1, source_target_pairs={{0,8},{8,16},{16,24},{24,32},{32,40},{40,48},{48,56},{56,64},{64,7... | collective-permute-start | bytes 675848 | tf_op jit(solution)/shard_map/ppermute | solution.py:569
  68.5 3.5 %collective-permute-done.5.low = f32[11,40,128]{2,1,0:T(8,128)S(1)} collective-permute-done((f32[11,40,128]{2,1,0:T(8,128)S(1)}, f32[11,40,128]{2,1,0:T(8,128)S(1)}, u32[]{:S(2)}, u32[]{:S(2)}) %collective-permute-start.5) | collective-permute-done | bytes 225312 | tf_op jit(solution)/shard_map/ppermute | solution.py:569
  71.9 6.0 %all-to-all-done = f32[256,1,128]{2,1,0:T(1,128)S(1)} async-done(((f32[256,1,128]{2,1,0:T(1,128)}), f32[256,1,128]{2,1,0:T(1,128)S(1)}, u32[]{:S(2)}, u32[]{:S(2)}) %all-to-all-start) | async-done | bytes 131104 | tf_op jit(solution)/shard_map/all_to_all | solution.py:582
  77.9 1.4 %copy-done.5 = f32[3,23,48,128]{3,2,1,0:T(8,128)S(1)} copy-done((f32[3,23,48,128]{3,2,1,0:T(8,128)S(1)}, f32[3,23,48,128]{3,2,1,0:T(8,128)}, u32[]{:S(2)}) %copy-start.5) | copy-done | bytes 1695768
  79.3 1.4 %copy-done.7 = f32[3,23,48,128]{3,2,1,0:T(8,128)S(1)} copy-done((f32[3,23,48,128]{3,2,1,0:T(8,128)S(1)}, f32[3,23,48,128]{3,2,1,0:T(8,128)}, u32[]{:S(2)}) %copy-start.7) | copy-done | bytes 1695768
  80.8 1.4 %copy-done.9 = f32[3,23,48,128]{3,2,1,0:T(8,128)S(1)} copy-done((f32[3,23,48,128]{3,2,1,0:T(8,128)S(1)}, f32[3,23,48,128]{3,2,1,0:T(8,128)}, u32[]{:S(2)}) %copy-start.9) | copy-done | bytes 1695768
  82.2 1.0 copy-done.13
  83.3 1.0 copy-done.19
  84.2 5.2 %shard_map.80 = (f32[3,16,32,128]{3,2,1,0:T(8,128)}, f32[16,32,128]{2,1,0:T(8,128)}, f32[23,40,128]{2,1,0:T(8,128)S(1)}, f32[23,40,128]{2,1,0:T(8,128)S(1)}, f32...) custom-call(f32[256,128]{1,0:T(8,128)S(1)} %bitcast.12, f32[3,23,48,128]{3,2,1,0:T(8,128)S(1)} %get-tuple-element.44.wide, ...), custom_call_target="tpu_custom_call" | custom-call | tf_op jit(solution)/shard_map/pallas_call | solution.py:38
  89.4 20.9 %all_to_all.22 = f32[256,1,128]{2,1,0:T(1,128)S(1)} all-to-all(f32[256,1,128]{2,1,0:T(1,128)S(1)} %bitcast.14), channel_id=1, replica_groups=mesh['gx'=32,'gy'=8] {'gx','gy'}, dimensions={0} | all-to-all | bytes 262144 | tf_op jit(solution)/shard_map/all_to_all | solution.py:582
  110.3 1.0 shard_map.81
  (38 shorter events, 3.1 us)
Async XLA Ops:
  0.6 1.1 %copy-start = (f32[3,16,32,128]{3,2,1,0:T(8,128)S(1)}, f32[3,16,32,128]{3,2,1,0:T(8,128)}, u32[]{:S(2)}) copy-start(f32[3,16,32,128]{3,2,1,0:T(8,128)} %disp.5) | copy-start | bytes 2359300
  1.8 1.1 %copy-start.2 = (f32[3,16,32,128]{3,2,1,0:T(8,128)S(1)}, f32[3,16,32,128]{3,2,1,0:T(8,128)}, u32[]{:S(2)}) copy-start(f32[3,16,32,128]{3,2,1,0:T(8,128)} %force.5) | copy-start | bytes 2359300
  2.9 0.9 copy-start.10
  3.9 0.9 copy-start.20
  4.8 0.9 copy-start.22
  6.1 21.9 %copy-start.1 = (f32[3,16,32,128]{3,2,1,0:T(8,128)S(1)}, f32[3,16,32,128]{3,2,1,0:T(8,128)}, u32[]{:S(2)}) copy-start(f32[3,16,32,128]{3,2,1,0:T(8,128)} %disp.5) | copy-start | bytes 2359300
  6.2 21.9 %copy-start.3 = (f32[3,16,32,128]{3,2,1,0:T(8,128)S(1)}, f32[3,16,32,128]{3,2,1,0:T(8,128)}, u32[]{:S(2)}) copy-start(f32[3,16,32,128]{3,2,1,0:T(8,128)} %force.5) | copy-start | bytes 2359300
  6.2 21.9 %copy-start.11 = (f32[16,32,128]{2,1,0:T(8,128)S(1)}, f32[16,32,128]{2,1,0:T(8,128)}, u32[]{:S(2)}) copy-start(f32[16,32,128]{2,1,0:T(8,128)} %damage.7) | copy-start | bytes 786436
  6.2 11.5 %collective-permute-start = (f32[6,16,8,128]{3,2,1,0:T(8,128)S(1)}, f32[6,16,8,128]{3,2,1,0:T(8,128)S(1)}, u32[]{:S(2)}, u32[]{:S(2)}) collective-permute-start(f32[6,16,8,128]{3,2,1,0:T(8,128)S(1)} %get-tuple-element.30), channel_id=1, source_target_pairs={{1,0},{2,1},{3,2},{4,3},{5,4},{6,5},{7,6},{9,8},{10,9},{11,10},{12... | collective-permute-start | bytes 1179656 | tf_op jit(solution)/shard_map/ppermute | solution.py:568
  7.6 11.0 %collective-permute-start.1 = (f32[6,16,8,128]{3,2,1,0:T(8,128)S(1)}, f32[6,16,8,128]{3,2,1,0:T(8,128)S(1)}, u32[]{:S(2)}, u32[]{:S(2)}) collective-permute-start(f32[6,16,8,128]{3,2,1,0:T(8,128)S(1)} %get-tuple-element.31), channel_id=1, source_target_pairs={{0,1},{1,2},{2,3},{3,4},{4,5},{5,6},{6,7},{8,9},{9,10},{10,11},{11... | collective-permute-start | bytes 1179656 | tf_op jit(solution)/shard_map/ppermute | solution.py:569
  17.7 10.3 %copy-start.14 = (f32[6,16,8,128]{3,2,1,0:T(8,128)}, f32[6,16,8,128]{3,2,1,0:T(8,128)S(1)}, u32[]{:S(2)}) copy-start(f32[6,16,8,128]{3,2,1,0:T(8,128)S(1)} %collective-permute-done.high) | copy-start | bytes 1179652
  18.6 1.1 %copy-start.16 = (f32[6,16,8,128]{3,2,1,0:T(8,128)}, f32[6,16,8,128]{3,2,1,0:T(8,128)S(1)}, u32[]{:S(2)}) copy-start(f32[6,16,8,128]{3,2,1,0:T(8,128)S(1)} %collective-permute-done.1.low) | copy-start | bytes 1179652
  19.7 17.1 %collective-permute-start.2 = (f32[25,48,128]{2,1,0:T(8,128)}, f32[25,48,128]{2,1,0:T(8,128)}, u32[]{:S(2)}, u32[]{:S(2)}) collective-permute-start(f32[25,48,128]{2,1,0:T(8,128)} %get-tuple-element.41), channel_id=1, source_target_pairs={{8,0},{16,8},{24,16},{32,24},{40,32},{48,40},{56,48},{64,56},{72,6... | collective-permute-start | bytes 1843208 | tf_op jit(solution)/shard_map/ppermute | solution.py:568
  24.9 11.8 %collective-permute-start.3 = (f32[18,48,128]{2,1,0:T(8,128)}, f32[18,48,128]{2,1,0:T(8,128)}, u32[]{:S(2)}, u32[]{:S(2)}) collective-permute-start(f32[18,48,128]{2,1,0:T(8,128)} %get-tuple-element.42), channel_id=1, source_target_pairs={{0,8},{8,16},{16,24},{24,32},{32,40},{40,48},{48,56},{56,64},{64,7... | collective-permute-start | bytes 1327112 | tf_op jit(solution)/shard_map/ppermute | solution.py:569
  28.1 1.0 copy-start.15
  29.1 1.0 copy-start.17
  30.1 0.9 copy-start.21
  31.0 0.9 copy-start.23
  36.8 4.4 %copy-start.18 = (f32[16,40,128]{2,1,0:T(8,128)}, f32[16,40,128]{2,1,0:T(8,128)S(1)}, u32[]{:S(2)}) copy-start(f32[16,40,128]{2,1,0:T(8,128)S(1)} %get-tuple-element.39.past) | copy-start | bytes 983044
  41.2 1.2 %copy-start.4 = (f32[3,23,48,128]{3,2,1,0:T(8,128)}, f32[3,23,48,128]{3,2,1,0:T(8,128)S(1)}, u32[]{:S(2)}) copy-start(f32[3,23,48,128]{3,2,1,0:T(8,128)S(1)} %get-tuple-element.45.v0) | copy-start | bytes 5087236
  42.4 1.2 %copy-start.6 = (f32[3,23,48,128]{3,2,1,0:T(8,128)}, f32[3,23,48,128]{3,2,1,0:T(8,128)S(1)}, u32[]{:S(2)}) copy-start(f32[3,23,48,128]{3,2,1,0:T(8,128)S(1)} %get-tuple-element.46.v1) | copy-start | bytes 5087236
  43.5 1.2 %copy-start.8 = (f32[3,23,48,128]{3,2,1,0:T(8,128)}, f32[3,23,48,128]{3,2,1,0:T(8,128)S(1)}, u32[]{:S(2)}) copy-start(f32[3,23,48,128]{3,2,1,0:T(8,128)S(1)} %get-tuple-element.47.v2) | copy-start | bytes 5087236
  44.8 0.8 copy-start.12
  45.5 32.4 %collective-permute-start.4 = (f32[21,40,128]{2,1,0:T(8,128)S(1)}, f32[21,40,128]{2,1,0:T(8,128)S(1)}, u32[]{:S(2)}, u32[]{:S(2)}) collective-permute-start(f32[21,40,128]{2,1,0:T(8,128)S(1)} %get-tuple-element.49), channel_id=1, source_target_pairs={{8,0},{16,8},{24,16},{32,24},{40,32},{48,40},{56,48},{64,56},{72,6... | collective-permute-start | bytes 1290248 | tf_op jit(solution)/shard_map/ppermute | solution.py:568
  47.6 30.3 %all-to-all-start = ((f32[256,1,128]{2,1,0:T(1,128)}), f32[256,1,128]{2,1,0:T(1,128)S(1)}, u32[]{:S(2)}, u32[]{:S(2)}) async-start(f32[256,1,128]{2,1,0:T(1,128)} %bitcast.5), calls=%async_computation | async-start | bytes 262144 | tf_op jit(solution)/shard_map/all_to_all | solution.py:582
  64.9 7.0 %collective-permute-start.5 = (f32[11,40,128]{2,1,0:T(8,128)S(1)}, f32[11,40,128]{2,1,0:T(8,128)S(1)}, u32[]{:S(2)}, u32[]{:S(2)}) collective-permute-start(f32[11,40,128]{2,1,0:T(8,128)S(1)} %get-tuple-element.50), channel_id=1, source_target_pairs={{0,8},{8,16},{16,24},{24,32},{32,40},{40,48},{48,56},{56,64},{64,7... | collective-permute-start | bytes 675848 | tf_op jit(solution)/shard_map/ppermute | solution.py:569
  77.9 1.5 %copy-start.5 = (f32[3,23,48,128]{3,2,1,0:T(8,128)S(1)}, f32[3,23,48,128]{3,2,1,0:T(8,128)}, u32[]{:S(2)}) copy-start(f32[3,23,48,128]{3,2,1,0:T(8,128)} %copy-done.4) | copy-start | bytes 5087236
  79.3 1.5 %copy-start.7 = (f32[3,23,48,128]{3,2,1,0:T(8,128)S(1)}, f32[3,23,48,128]{3,2,1,0:T(8,128)}, u32[]{:S(2)}) copy-start(f32[3,23,48,128]{3,2,1,0:T(8,128)} %copy-done.6) | copy-start | bytes 5087236
  80.8 1.5 %copy-start.9 = (f32[3,23,48,128]{3,2,1,0:T(8,128)S(1)}, f32[3,23,48,128]{3,2,1,0:T(8,128)}, u32[]{:S(2)}) copy-start(f32[3,23,48,128]{3,2,1,0:T(8,128)} %copy-done.8) | copy-start | bytes 5087236
  82.2 1.0 copy-start.13
  83.3 1.0 copy-start.19

commit v3 on v2

--- a/solution.py
+++ b/solution.py
@@ -27,17 +27,29 @@
 BRIEF = (DEPTH, SHORT, LZ)
 
 
+def fast(shape):
+    if INTERPRET:
+        return jax.ShapeDtypeStruct(shape, f32)
+    return pltpu.VMEM(shape, f32)
+
+
+def whole(*shape):
+    return jax.ShapeDtypeStruct(shape, f32)
+
+
 def call(kernel, outs, scratch=(), limit=8 << 20, aliases=None, hbm=False):
     vmem = pl.BlockSpec(memory_space=pltpu.VMEM)
     smem = pl.BlockSpec(memory_space=pltpu.SMEM)
 
     def run(*args, flags=None):
-        specs = [pl.BlockSpec(memory_space=pl.ANY) if hbm else vmem] * len(args)
+        specs = [pl.BlockSpec(memory_space=pltpu.HBM) if hbm else vmem] * len(args)
+        if hbm and not INTERPRET:
+            args = [pltpu.with_memory_space_constraint(x, pltpu.HBM) for x in args]
         if flags is not None:
             args, specs = (*args, flags), specs + [smem]
         return pl.pallas_call(
             kernel,
-            out_shape=[jax.ShapeDtypeStruct(s, f32) for s in outs],
+            out_shape=[s if isinstance(s, jax.ShapeDtypeStruct) else fast(s) for s in outs],
             in_specs=specs,
             out_specs=[vmem] * len(outs),
             scratch_shapes=[pltpu.VMEM(s, f32) if isinstance(s, tuple) else s for s in scratch],
@@ -116,22 +128,39 @@
     return jnp.where(row < 8, flags[3], flags[2])
 
 
-def pack_rows_kernel(
-    disp, force, damage, history, crack, first, last, top, bottom, top_crack, bottom_crack, sem
+AHEAD = (4, 4, 4, 3, 3, 3, 4)
+BEHIND = (3, 3, 3, 2, 2, 2, 3)
+AHEAD_AT = tuple(sum(AHEAD[:k]) for k in range(7))
+BEHIND_AT = tuple(sum(BEHIND[:k]) for k in range(7))
+
+
+def pack_kernel(
+    disp, force, damage, history, crack,
+    first, last, front, back, front_first, front_last, back_first, back_last,
+    top, bottom, top_crack, bottom_crack, sem,
 ):
-    copies = []
+    fields = [disp.at[j] for j in range(3)] + [force.at[j] for j in range(3)] + [damage]
+    near, far = [], []
     for rows, into, into_crack in ((0, top, top_crack), (24, bottom, bottom_crack)):
-        for source, target in (
+        near += [
             (disp.at[:, :, rows : rows + 8], into.at[0:3]),
             (force.at[:, :, rows : rows + 8], into.at[3:6]),
             (damage.at[:, rows : rows + 8], into.at[6]),
             (history.at[:, rows : rows + 8], into.at[7]),
             (crack.at[:, rows : rows + 8], into_crack),
-        ):
-            copies.append(pltpu.make_async_copy(source, target, sem.at[len(copies)]))
+        ]
+    for k, field in enumerate(fields):
+        at = AHEAD_AT[k]
+        far.append((field.at[0 : AHEAD[k]], front.at[at : at + AHEAD[k]]))
+        at = BEHIND_AT[k]
+        far.append((field.at[LX - BEHIND[k] : LX], back.at[at : at + BEHIND[k]]))
+    copies = [
+        pltpu.make_async_copy(source, target, sem.at[n])
+        for n, (source, target) in enumerate(near + far)
+    ]
     for copy in copies:
         copy.start()
-    for copy in copies:
+    for copy in copies[: len(near)]:
         copy.wait()
 
     def step(k, carry):
@@ -149,23 +178,15 @@
         return carry
 
     lax.fori_loop(0, LX, step, 0, unroll=2)
-
-
-def pack_layers_kernel(disp, force, damage, high, low, first, last):
-    at = {True: 0, False: 0}
-    for field in range(7):
-        own = disp.at[field] if field < 3 else force.at[field - 3] if field < 6 else damage
-        ahead, behind = (3, 2) if 3 <= field < 6 else (4, 3)
-        for c in (*range(ahead), *range(LX - behind, LX)):
-            out, front = (first, True) if c < ahead else (last, False)
-            if field < 6:
-                above, below = high[field, c], low[field, c]
-            else:
-                above, below = damage_tiles(high, low, c)
-            out[at[front], 0:LY] = own[c]
-            out[at[front], LY : LY + 8] = above
-            out[at[front], LY + 8 : ROWS] = below
-            at[front] += 1
+    for k in range(7):
+        at = AHEAD_AT[k]
+        front_first[at : at + AHEAD[k]] = top[k, 0 : AHEAD[k]]
+        front_last[at : at + AHEAD[k]] = bottom[k, 0 : AHEAD[k]]
+        at = BEHIND_AT[k]
+        back_first[at : at + BEHIND[k]] = top[k, LX - BEHIND[k] : LX]
+        back_last[at : at + BEHIND[k]] = bottom[k, LX - BEHIND[k] : LX]
+    for copy in copies[len(near) :]:
+        copy.wait()
 
 
 def stress(u, n, gain):
@@ -281,15 +302,15 @@
         i = OFF + k
         for j in range(3):
             wide[j, i, 0:LY] = disp[j, k]
-            wide[j, i, LY : LY + 8] = high[j, k]
-            wide[j, i, LY + 8 : ROWS] = low[j, k]
+            wide[j, i, LY : LY + 8] = high[j, k] * flags[3]
+            wide[j, i, LY + 8 : ROWS] = low[j, k] * flags[2]
             load[j, k, 0:LY] = force[j, k]
             load[j, k, LY : LY + 8] = high[3 + j, k]
             load[j, k, LY + 8 : ROWS] = low[3 + j, k]
         own = damage[k]
         above, below = damage_tiles(high, low, k)
         short_damage[i, 0:LY] = own
-        short_damage[i, LY:SHORT] = brief(above, below)
+        short_damage[i, LY:SHORT] = brief(above * flags[3], below * flags[2])
         left = 1.0 - own
         gain[i, 0:LY] = left * left + stiff_floor
         left = 1.0 - above
@@ -319,30 +340,42 @@
 
 def outer_kernel(
     wide_in, load, gain_in, v0_in, v1_in, v2_in, short_in, past, partial,
-    layers_high, layers_low, flags,
-    wide, gain, v0, v1, v2, short_damage, sums, first, last,
+    ahead, ahead_high, ahead_low, behind, behind_high, behind_low, flags,
+    wide, gain, v0, v1, v2, short_damage, sums, first, last, edge_load,
 ):
     mask = row_mask(flags)
-    for j in range(3):
-        wide[j, OFF + LX : DEPTH] = layers_high[4 * j : 4 * j + 4]
-        wide[j, 0:OFF] = layers_low[3 * j : 3 * j + 3]
-    for side, count, at, base, flag in (
-        (layers_high, 4, OFF + LX, 21, flags[1]), (layers_low, 3, 0, 15, flags[0])
+    for counts, starts, at, middle, above, below, flag in (
+        (AHEAD, AHEAD_AT, OFF + LX, ahead, ahead_high, ahead_low, flags[1]),
+        (BEHIND, BEHIND_AT, OFF, behind, behind_high, behind_low, flags[0]),
     ):
-        for c in range(count):
-            value = side[base + c]
-            short_damage[at + c, 0:LY] = value[0:LY]
-            short_damage[at + c, LY:SHORT] = brief(value[LY : LY + 8], value[LY + 8 : ROWS])
-            left = 1.0 - value
-            value = (left * left + stiff_floor) * flag
-            gain[at + c, 0:LY] = value[0:LY]
-            gain[at + c, LY:ROWS] = value[LY:ROWS] * mask
+        for k in range(7):
+            begin = at if at > OFF else OFF - counts[k]
+            for c in range(counts[k]):
+                own = middle[starts[k] + c] * flag
+                high = above[starts[k] + c] * (flag * flags[3])
+                low = below[starts[k] + c] * (flag * flags[2])
+                i = begin + c
+                if k < 3:
+                    into = wide.at[k, i]
+                elif k < 6:
+                    into = edge_load.at[k - 3, i - 1 if i < OFF else i - OFF - LX + 2]
+                else:
+                    into = gain.at[i]
+                    short_damage[i, 0:LY] = own
+                    short_damage[i, LY:SHORT] = brief(high, low)
+                    own, high, low = ((1.0 - x) * (1.0 - x) + stiff_floor for x in (own, high, low))
+                    own = own * flag
+                    high = high * (mask[0:8] * flag)
+                    low = low * (mask[8:16] * flag)
+                into[0:LY] = own
+                into[LY : LY + 8] = high
+                into[LY + 8 : ROWS] = low
 
     def force_at(j, i):
         if i < OFF:
-            return layers_low[9 + 2 * j + i - 1]
+            return edge_load[j, i - 1]
         if i >= OFF + LX:
-            return layers_high[12 + 3 * j + i - OFF - LX]
+            return edge_load[j, i - OFF - LX + 2]
         return load[j, i - OFF]
 
     def both(source, target, low_end, high_begin, diag, load=None):
@@ -456,15 +489,19 @@
         i = OFF + LX
         put(j, i, wide[j, i] + a0 * v0[j, i] + a1 * v1[j, i] + a2 * v2[j, i], None)
         i = OFF - 2
-        put(j, i, wide[j, i] + a0 * v0[j, i], a1 * low[j] + a2 * low[3 + 2 * j])
+        far = (a1 * low[j] + a2 * low[3 + 2 * j]) * flags[0]
+        put(j, i, wide[j, i] + a0 * v0[j, i], far)
         i = OFF - 1
-        put(j, i, wide[j, i] + a0 * v0[j, i] + a1 * v1[j, i], a2 * low[4 + 2 * j])
+        far = (a2 * low[4 + 2 * j]) * flags[0]
+        put(j, i, wide[j, i] + a0 * v0[j, i] + a1 * v1[j, i], far)
         i = OFF + LX + 1
-        put(j, i, wide[j, i] + a0 * v0[j, i] + a1 * v1[j, i], a2 * high[9 + 3 * j])
+        far = (a2 * high[9 + 3 * j]) * flags[1]
+        put(j, i, wide[j, i] + a0 * v0[j, i] + a1 * v1[j, i], far)
         i = OFF + LX + 2
-        put(j, i, wide[j, i] + a0 * v0[j, i], a1 * high[3 + 2 * j] + a2 * high[10 + 3 * j])
+        far = (a1 * high[3 + 2 * j] + a2 * high[10 + 3 * j]) * flags[1]
+        put(j, i, wide[j, i] + a0 * v0[j, i], far)
         i = OFF + LX + 3
-        far = a0 * high[j] + a1 * high[4 + 2 * j] + a2 * high[11 + 3 * j]
+        far = (a0 * high[j] + a1 * high[4 + 2 * j] + a2 * high[11 + 3 * j]) * flags[1]
         put(j, i, wide[j, i], far)
 
     row = lax.broadcasted_iota(jnp.int32, (8, LZ), 0)
@@ -561,13 +598,16 @@
     lax.fori_loop(0, LX, step, 0, unroll=2)
 
 
-def exchange(first, last, axis):
-    size = lax.axis_size(axis)
-    up = [(i, i + 1) for i in range(size - 1)]
-    down = [(b, a) for a, b in up]
-    high = lax.ppermute(first, axis, down)
-    low = lax.ppermute(last, axis, up)
-    return high, low
+def send(values, dx, dy):
+    nx, ny = lax.axis_size("gx"), lax.axis_size("gy")
+    if not dy:
+        return lax.ppermute(values, "gx", [(i, (i + dx) % nx) for i in range(nx)])
+    if not dx:
+        return lax.ppermute(values, "gy", [(k, (k + dy) % ny) for k in range(ny)])
+    pairs = [
+        (i * ny + k, (i + dx) % nx * ny + (k + dy) % ny) for i in range(nx) for k in range(ny)
+    ]
+    return lax.ppermute(values, ("gx", "gy"), pairs)
 
 
 def step(displacement, force, damage, history, crack_flags):
@@ -582,21 +622,25 @@
         return lax.all_to_all(sums, axes, 0, 0, tiled=True)
 
     edge_rows = (8, LX, 8, LZ)
-    rows = call(
-        pack_rows_kernel,
-        [(6, LX, 8, LZ)] * 2,
+    front, back = sum(AHEAD), sum(BEHIND)
+    first, last, front_own, back_own, ff, fl, bf, bl = call(
+        pack_kernel,
+        [(6, LX, 8, LZ)] * 2
+        + [(front, LY, LZ), (back, LY, LZ)]
+        + [(front, 8, LZ)] * 2
+        + [(back, 8, LZ)] * 2,
         [
             edge_rows, edge_rows,
             pltpu.VMEM((LX, 8, LZ), jnp.int32), pltpu.VMEM((LX, 8, LZ), jnp.int32),
-            pltpu.SemaphoreType.DMA((10,)),
+            pltpu.SemaphoreType.DMA((24,)),
         ],
         hbm=True,
     )(displacement, force, damage, history, crack_flags)
-    high, low = exchange(*rows, "gy")
-    layers = call(pack_layers_kernel, [(25, ROWS, LZ), (18, ROWS, LZ)])(
-        displacement, force, damage, high, low
-    )
-    layers_high, layers_low = exchange(*layers, "gx")
+    high = send(first, 0, -1)
+    low = send(last, 0, 1)
+    ahead, behind = send(front_own, -1, 0), send(back_own, 1, 0)
+    ahead_high, ahead_low = send(ff, -1, -1), send(fl, -1, 1)
+    behind_high, behind_low = send(bf, 1, -1), send(bl, 1, 1)
     wide, load, gain, v0, v1, v2, short_damage, past, partial = call(
         inner_kernel,
         [VECTOR, (3, LX, ROWS, LZ), SCALAR, VECTOR, VECTOR, VECTOR, BRIEF]
@@ -606,19 +650,21 @@
         outer_kernel,
         [VECTOR, SCALAR, VECTOR, VECTOR, VECTOR, BRIEF]
         + [(count, LZ), (21, SHORT, LZ), (11, SHORT, LZ)],
+        scratch=[(3, 5, ROWS, LZ)],
         aliases={0: 0, 2: 1, 3: 2, 4: 3, 5: 4, 6: 5},
     )(
         wide, load, gain, v0, v1, v2, short_damage, past, partial,
-        layers_high, layers_low, flags=flags,
+        ahead, ahead_high, ahead_low, behind, behind_high, behind_low, flags=flags,
     )
-    high, low = exchange(first, last, "gx")
+    high = send(first, -1, 0)
+    low = send(last, 1, 0)
     gathered = gather(sums)
     moved, found, w0, w1, w2, sums = call(
         damage_kernel,
-        [(3, LX, LY, LZ), (LX, LY, LZ), BRIEF, BRIEF, BRIEF, (count, LZ)],
+        [whole(3, LX, LY, LZ), whole(LX, LY, LZ), BRIEF, BRIEF, BRIEF, (count, LZ)],
         [(3, DEPTH, SHORT, LZ), BRIEF],
     )(gathered, wide, v0, v1, v2, short_damage, past, high, low, flags=flags)
-    (damage_out,) = call(update_kernel, [(LX, LY, LZ)])(
+    (damage_out,) = call(update_kernel, [whole(LX, LY, LZ)])(
         gather(sums), damage, w0, w1, w2
     )
     return moved, damage_out, found

time: 112 us -> 107 us (0.955)
  starting transfers between devices: 37.6 us -> 33.2 us
  Pallas kernels: 16.8 us -> 18.3 us
    all_to_all x1, starting transfers between devices: 17.3 us -> 8.42 us  [gather(): return lax.all_to_all(sums, axes, 0, 0, tiled=True)]
    ppermute x6 -> x10, starting transfers between devices: 20.3 us -> 24.8 us  [the longest x4 12.7 us: send(): return lax.ppermute(values, ('gx', 'gy'), pairs)]
    pallas_call x6 -> x5, Pallas kernels: 16.8 us -> 18.3 us  [run(): pl.pallas_call(kernel, out_shape=[s if isinstance(s, jax.ShapeDtypeStruct...]
    ppermute x6 -> x10, waiting for transfers between devices: 9.42 us -> 8.16 us  [the longest x4 4.15 us: send(): return lax.ppermute(values, ('gx', 'gy'), pairs)]
    unnamed x48 -> x44, local copies, waits for them, and re-layouts: 19.7 us -> 19.6 us
  transfers between devices with their start and end apart: 7 -> 11, of which waited for: 4 -> 3; matrix products, arithmetic and copies ran while one was open for 0% -> 0% of each run, Pallas kernels for 4% -> 4%
where the time goes in v3:
time: 107 us
  starting transfers between devices  33.2 us (31%)
  blocking collectives  20.1 us (19%)
  local copies, waits for them, and re-layouts  19.6 us (18%)
  Pallas kernels  18.3 us (17%)
  waiting for transfers between devices  14.6 us (14%)
    all_to_all x1, blocking collectives, gather(): return lax.all_to_all(sums, axes, 0, 0, tiled=True)  20.1 us
    unnamed x44, local copies, waits for them, and re-layouts  19.6 us
    pallas_call x5, Pallas kernels, run(): pl.pallas_call(kernel, out_shape=[s if isinstance(s, jax.ShapeDtypeStruct...  18.3 us
    ppermute x4, starting transfers between devices, send(): return lax.ppermute(values, ('gx', 'gy'), pairs)  12.7 us
    all_to_all x1, starting transfers between devices, gather(): return lax.all_to_all(sums, axes, 0, 0, tiled=True)  8.42 us
    ppermute x2, starting transfers between devices, send(): return lax.ppermute(values, 'gy', [(k, (k + dy) % ny) for k in range(ny)])  6.47 us
    all_to_all x1, waiting for transfers between devices, gather(): return lax.all_to_all(sums, axes, 0, 0, tiled=True)  6.4 us
    ppermute x4, starting transfers between devices, send(): return lax.ppermute(values, 'gx', [(i, (i + dx) % nx) for i in range(nx)])  5.67 us
  transfers between devices with their start and end apart: 11, of which 3 were waited for; matrix products, arithmetic and copies ran while one was open for 0% of the time, Pallas kernels for 4%

profile of v3, /device:TPU:1, one launch (start us, length us, event | category | flops | bytes accessed | tf_op | source)
XLA Modules:
  0.0 106.7 jit_solution(15869591606383232933)
XLA Ops:
  0.6 2.6 %shard_map.76 = (f32[6,16,8,128]{3,2,1,0:T(8,128)S(1)}, f32[6,16,8,128]{3,2,1,0:T(8,128)S(1)}, f32[25,32,128]{2,1,0:T(8,128)}, f32[18,32,128]{2,1,0:T(8,128)}, f...) custom-call(f32[3,16,32,128]{3,2,1,0:T(8,128)} %disp.3, ...), custom_call_target="tpu_custom_call" | custom-call | tf_op jit(solution)/shard_map/pallas_call | solution.py:50
  3.3 6.5 %collective-permute-start = (f32[6,16,8,128]{3,2,1,0:T(8,128)S(1)}, f32[6,16,8,128]{3,2,1,0:T(8,128)S(1)}, u32[]{:S(2)}, u32[]{:S(2)}) collective-permute-start(f32[6,16,8,128]{3,2,1,0:T(8,128)S(1)} %get-tuple-element.34), channel_id=1, source_target_pairs={{0,7},{1,0},{2,1},{3,2},{4,3},{5,4},{6,5},{7,6},{8,15},{9,8},{10,9... | collective-permute-start | bytes 1179656 | tf_op jit(solution)/shard_map/ppermute | solution.py:606
  9.7 1.0 collective-permute-start.2
  10.7 1.1 %collective-permute-start.5 = (f32[18,32,128]{2,1,0:T(8,128)}, f32[18,32,128]{2,1,0:T(8,128)}, u32[]{:S(2)}, u32[]{:S(2)}) collective-permute-start(f32[18,32,128]{2,1,0:T(8,128)} %get-tuple-element.48), channel_id=1, source_target_pairs={{0,8},{8,16},{16,24},{24,32},{32,40},{40,48},{48,56},{56,64},{64,7... | collective-permute-start | bytes 884744 | tf_op jit(solution)/shard_map/ppermute | solution.py:604
  11.8 3.2 %collective-permute-start.6 = (f32[18,8,128]{2,1,0:T(8,128)S(1)}, f32[18,8,128]{2,1,0:T(8,128)S(1)}, u32[]{:S(2)}, u32[]{:S(2)}) collective-permute-start(f32[18,8,128]{2,1,0:T(8,128)S(1)} %get-tuple-element.49), channel_id=1, source_target_pairs={{0,15},{1,8},{2,9},{3,10},{4,11},{5,12},{6,13},{7,14},{8,23},{9,16... | collective-permute-start | bytes 221192 | tf_op jit(solution)/shard_map/ppermute | solution.py:610
  15.0 4.1 %collective-permute-done.6.behind_high = f32[18,8,128]{2,1,0:T(8,128)S(1)} collective-permute-done((f32[18,8,128]{2,1,0:T(8,128)S(1)}, f32[18,8,128]{2,1,0:T(8,128)S(1)}, u32[]{:S(2)}, u32[]{:S(2)}) %collective-permute-start.6) | collective-permute-done | bytes 73760 | tf_op jit(solution)/shard_map/ppermute | solution.py:610
  19.9 8.5 %collective-permute-start.3 = (f32[25,8,128]{2,1,0:T(8,128)}, f32[25,8,128]{2,1,0:T(8,128)S(1)}, u32[]{:S(2)}, u32[]{:S(2)}) collective-permute-start(f32[25,8,128]{2,1,0:T(8,128)} %get-tuple-element.46), channel_id=1, source_target_pairs={{0,255},{1,248},{2,249},{3,250},{4,251},{5,252},{6,253},{7,254},{8... | collective-permute-start | bytes 307208 | tf_op jit(solution)/shard_map/ppermute | solution.py:610
  29.2 1.0 collective-permute-start.4
  30.2 1.1 %copy-done.4 = f32[3,16,32,128]{3,2,1,0:T(8,128)S(1)} copy-done((f32[3,16,32,128]{3,2,1,0:T(8,128)S(1)}, f32[3,16,32,128]{3,2,1,0:T(8,128)}, u32[]{:S(2)}) %copy-start.4) | copy-done | bytes 786456
  31.4 1.1 %copy-done.5 = f32[3,16,32,128]{3,2,1,0:T(8,128)S(1)} copy-done((f32[3,16,32,128]{3,2,1,0:T(8,128)S(1)}, f32[3,16,32,128]{3,2,1,0:T(8,128)}, u32[]{:S(2)}) %copy-start.5) | copy-done | bytes 786456
  32.5 0.9 copy-done.6
  33.4 0.9 copy-done.12
  34.4 0.9 copy-done.13
  35.3 1.0 copy-done.15
  36.3 1.0 copy-done.17
  37.3 4.7 %shard_map.77 = (f32[3,23,48,128]{3,2,1,0:T(8,128)S(1)}, f32[3,16,48,128]{3,2,1,0:T(8,128)S(1)}, f32[23,48,128]{2,1,0:T(8,128)S(1)}, f32[3,23,48,128]{3,2,1,0:T(...) custom-call(f32[3,16,32,128]{3,2,1,0:T(8,128)S(1)} %copy-done.4, ...), custom_call_target="tpu_custom_call" | custom-call | tf_op jit(solution)/shard_map/pallas_call | solution.py:50
  42.1 4.3 %shard_map.78 = (f32[3,23,48,128]{3,2,1,0:T(8,128)S(1)}, f32[23,48,128]{2,1,0:T(8,128)S(1)}, f32[3,23,48,128]{3,2,1,0:T(8,128)S(1)}, f32[3,23,48,128]{3,2,1,0:T(...) custom-call(f32[3,23,48,128]{3,2,1,0:T(8,128)S(1)} %get-tuple-elemen, ...), custom_call_target="tpu_custom_call", output_to_operand_aliasing={{0}: (0, {}), {1}: (2, {}), {2}: (3, {}), {3}: (4, {}), {4}... | custom-call | tf_op jit(solution)/shard_map/pallas_call | solution.py:50
  46.4 1.2 %copy-done = f32[3,23,48,128]{3,2,1,0:T(8,128)} copy-done((f32[3,23,48,128]{3,2,1,0:T(8,128)}, f32[3,23,48,128]{3,2,1,0:T(8,128)S(1)}, u32[]{:S(2)}) %copy-start) | copy-done | bytes 1695768
  47.6 1.2 %copy-done.2 = f32[3,23,48,128]{3,2,1,0:T(8,128)} copy-done((f32[3,23,48,128]{3,2,1,0:T(8,128)}, f32[3,23,48,128]{3,2,1,0:T(8,128)S(1)}, u32[]{:S(2)}) %copy-start.2) | copy-done | bytes 1695768
  50.9 1.7 %collective-permute-start.8 = (f32[21,40,128]{2,1,0:T(8,128)}, f32[21,40,128]{2,1,0:T(8,128)}, u32[]{:S(2)}, u32[]{:S(2)}) collective-permute-start(f32[21,40,128]{2,1,0:T(8,128)} %get-tuple-element.57), channel_id=1, source_target_pairs={{0,248},{8,0},{16,8},{24,16},{32,24},{40,32},{48,40},{56,48},{64,5... | collective-permute-start | bytes 1290248 | tf_op jit(solution)/shard_map/ppermute | solution.py:604
  52.6 8.4 %all-to-all-start = ((f32[256,1,128]{2,1,0:T(1,128)}), f32[256,1,128]{2,1,0:T(1,128)S(1)}, u32[]{:S(2)}, u32[]{:S(2)}) async-start(f32[256,1,128]{2,1,0:T(1,128)} %bitcast.14), calls=%async_computation | async-start | bytes 262144 | tf_op jit(solution)/shard_map/all_to_all | solution.py:622
  61.1 1.9 %collective-permute-start.9 = (f32[11,40,128]{2,1,0:T(8,128)}, f32[11,40,128]{2,1,0:T(8,128)S(1)}, u32[]{:S(2)}, u32[]{:S(2)}) collective-permute-start(f32[11,40,128]{2,1,0:T(8,128)} %copy-done.21), channel_id=1, source_target_pairs={{0,8},{8,16},{16,24},{24,32},{32,40},{40,48},{48,56},{56,64},{64,7... | collective-permute-start | bytes 675848 | tf_op jit(solution)/shard_map/ppermute | solution.py:604
  62.9 4.0 %collective-permute-done.9.low = f32[11,40,128]{2,1,0:T(8,128)S(1)} collective-permute-done((f32[11,40,128]{2,1,0:T(8,128)}, f32[11,40,128]{2,1,0:T(8,128)S(1)}, u32[]{:S(2)}, u32[]{:S(2)}) %collective-permute-start.9) | collective-permute-done | bytes 225312 | tf_op jit(solution)/shard_map/ppermute | solution.py:604
  67.6 6.4 %all-to-all-done = f32[256,1,128]{2,1,0:T(1,128)S(1)} async-done(((f32[256,1,128]{2,1,0:T(1,128)}), f32[256,1,128]{2,1,0:T(1,128)S(1)}, u32[]{:S(2)}, u32[]{:S(2)}) %all-to-all-start) | async-done | bytes 131104 | tf_op jit(solution)/shard_map/all_to_all | solution.py:622
  74.0 1.4 %copy-done.1 = f32[3,23,48,128]{3,2,1,0:T(8,128)S(1)} copy-done((f32[3,23,48,128]{3,2,1,0:T(8,128)S(1)}, f32[3,23,48,128]{3,2,1,0:T(8,128)}, u32[]{:S(2)}) %copy-start.1) | copy-done | bytes 1695768
  75.5 1.4 %copy-done.3 = f32[3,23,48,128]{3,2,1,0:T(8,128)S(1)} copy-done((f32[3,23,48,128]{3,2,1,0:T(8,128)S(1)}, f32[3,23,48,128]{3,2,1,0:T(8,128)}, u32[]{:S(2)}) %copy-start.3) | copy-done | bytes 1695768
  76.9 1.0 copy-done.9
  78.0 1.0 copy-done.11
  78.9 0.9 copy-done.19
  79.9 5.7 %shard_map.79 = (f32[3,16,32,128]{3,2,1,0:T(8,128)}, f32[16,32,128]{2,1,0:T(8,128)}, f32[23,40,128]{2,1,0:T(8,128)S(1)}, f32[23,40,128]{2,1,0:T(8,128)S(1)}, f32...) custom-call(f32[256,128]{1,0:T(8,128)S(1)} %bitcast.12, f32[3,23,48,128]{3,2,1,0:T(8,128)S(1)} %get-tuple-element.52.wide, ...), custom_call_target="tpu_custom_call" | custom-call | tf_op jit(solution)/shard_map/pallas_call | solution.py:50
  85.6 20.1 %all_to_all.22 = f32[256,1,128]{2,1,0:T(1,128)S(1)} all-to-all(f32[256,1,128]{2,1,0:T(1,128)S(1)} %bitcast.15), channel_id=1, replica_groups=mesh['gx'=32,'gy'=8] {'gx','gy'}, dimensions={0} | all-to-all | bytes 262144 | tf_op jit(solution)/shard_map/all_to_all | solution.py:622
  105.8 1.0 shard_map.80
  (41 shorter events, 4.4 us)
Async XLA Ops:
  3.3 15.9 %collective-permute-start = (f32[6,16,8,128]{3,2,1,0:T(8,128)S(1)}, f32[6,16,8,128]{3,2,1,0:T(8,128)S(1)}, u32[]{:S(2)}, u32[]{:S(2)}) collective-permute-start(f32[6,16,8,128]{3,2,1,0:T(8,128)S(1)} %get-tuple-element.34), channel_id=1, source_target_pairs={{0,7},{1,0},{2,1},{3,2},{4,3},{5,4},{6,5},{7,6},{8,15},{9,8},{10,9... | collective-permute-start | bytes 1179656 | tf_op jit(solution)/shard_map/ppermute | solution.py:606
  9.7 18.7 %collective-permute-start.1 = (f32[6,16,8,128]{3,2,1,0:T(8,128)S(1)}, f32[6,16,8,128]{3,2,1,0:T(8,128)S(1)}, u32[]{:S(2)}, u32[]{:S(2)}) collective-permute-start(f32[6,16,8,128]{3,2,1,0:T(8,128)S(1)} %get-tuple-element.35), channel_id=1, source_target_pairs={{0,1},{1,2},{2,3},{3,4},{4,5},{5,6},{6,7},{7,0},{8,9},{9,10},{10,1... | collective-permute-start | bytes 1179656 | tf_op jit(solution)/shard_map/ppermute | solution.py:606
  9.7 32.4 %collective-permute-start.2 = (f32[25,32,128]{2,1,0:T(8,128)}, f32[25,32,128]{2,1,0:T(8,128)}, u32[]{:S(2)}, u32[]{:S(2)}) collective-permute-start(f32[25,32,128]{2,1,0:T(8,128)} %get-tuple-element.45), channel_id=1, source_target_pairs={{0,248},{8,0},{16,8},{24,16},{32,24},{40,32},{48,40},{56,48},{64,5... | collective-permute-start | bytes 1228808 | tf_op jit(solution)/shard_map/ppermute | solution.py:604
  10.7 31.4 %collective-permute-start.5 = (f32[18,32,128]{2,1,0:T(8,128)}, f32[18,32,128]{2,1,0:T(8,128)}, u32[]{:S(2)}, u32[]{:S(2)}) collective-permute-start(f32[18,32,128]{2,1,0:T(8,128)} %get-tuple-element.48), channel_id=1, source_target_pairs={{0,8},{8,16},{16,24},{24,32},{32,40},{40,48},{48,56},{56,64},{64,7... | collective-permute-start | bytes 884744 | tf_op jit(solution)/shard_map/ppermute | solution.py:604
  11.8 7.3 %collective-permute-start.6 = (f32[18,8,128]{2,1,0:T(8,128)S(1)}, f32[18,8,128]{2,1,0:T(8,128)S(1)}, u32[]{:S(2)}, u32[]{:S(2)}) collective-permute-start(f32[18,8,128]{2,1,0:T(8,128)S(1)} %get-tuple-element.49), channel_id=1, source_target_pairs={{0,15},{1,8},{2,9},{3,10},{4,11},{5,12},{6,13},{7,14},{8,23},{9,16... | collective-permute-start | bytes 221192 | tf_op jit(solution)/shard_map/ppermute | solution.py:610
  19.1 23.0 %collective-permute-start.7 = (f32[18,8,128]{2,1,0:T(8,128)}, f32[18,8,128]{2,1,0:T(8,128)S(1)}, u32[]{:S(2)}, u32[]{:S(2)}) collective-permute-start(f32[18,8,128]{2,1,0:T(8,128)} %get-tuple-element.50), channel_id=1, source_target_pairs={{0,9},{1,10},{2,11},{3,12},{4,13},{5,14},{6,15},{7,8},{8,17},{9,18... | collective-permute-start | bytes 221192 | tf_op jit(solution)/shard_map/ppermute | solution.py:610
  19.1 0.8 copy-start.14
  19.9 22.2 %collective-permute-start.3 = (f32[25,8,128]{2,1,0:T(8,128)}, f32[25,8,128]{2,1,0:T(8,128)S(1)}, u32[]{:S(2)}, u32[]{:S(2)}) collective-permute-start(f32[25,8,128]{2,1,0:T(8,128)} %get-tuple-element.46), channel_id=1, source_target_pairs={{0,255},{1,248},{2,249},{3,250},{4,251},{5,252},{6,253},{7,254},{8... | collective-permute-start | bytes 307208 | tf_op jit(solution)/shard_map/ppermute | solution.py:610
  28.4 0.8 copy-start.16
  29.2 13.0 %collective-permute-start.4 = (f32[25,8,128]{2,1,0:T(8,128)}, f32[25,8,128]{2,1,0:T(8,128)S(1)}, u32[]{:S(2)}, u32[]{:S(2)}) collective-permute-start(f32[25,8,128]{2,1,0:T(8,128)} %get-tuple-element.47), channel_id=1, source_target_pairs={{0,249},{1,250},{2,251},{3,252},{4,253},{5,254},{6,255},{7,248},{8... | collective-permute-start | bytes 307208 | tf_op jit(solution)/shard_map/ppermute | solution.py:610
  30.2 1.1 %copy-start.4 = (f32[3,16,32,128]{3,2,1,0:T(8,128)S(1)}, f32[3,16,32,128]{3,2,1,0:T(8,128)}, u32[]{:S(2)}) copy-start(f32[3,16,32,128]{3,2,1,0:T(8,128)} %disp.3) | copy-start | bytes 2359300
  31.4 1.1 %copy-start.5 = (f32[3,16,32,128]{3,2,1,0:T(8,128)S(1)}, f32[3,16,32,128]{3,2,1,0:T(8,128)}, u32[]{:S(2)}) copy-start(f32[3,16,32,128]{3,2,1,0:T(8,128)} %force.3) | copy-start | bytes 2359300
  32.5 0.9 copy-start.6
  33.4 0.9 copy-start.12
  34.4 0.9 copy-start.13
  35.3 1.0 copy-start.15
  36.3 1.0 copy-start.17
  42.1 4.3 %copy-start.10 = (f32[16,40,128]{2,1,0:T(8,128)}, f32[16,40,128]{2,1,0:T(8,128)S(1)}, u32[]{:S(2)}) copy-start(f32[16,40,128]{2,1,0:T(8,128)S(1)} %get-tuple-element.43.past) | copy-start | bytes 983044
  46.4 1.2 %copy-start = (f32[3,23,48,128]{3,2,1,0:T(8,128)}, f32[3,23,48,128]{3,2,1,0:T(8,128)S(1)}, u32[]{:S(2)}) copy-start(f32[3,23,48,128]{3,2,1,0:T(8,128)S(1)} %get-tuple-element.54.v1) | copy-start | bytes 5087236
  47.6 1.2 %copy-start.2 = (f32[3,23,48,128]{3,2,1,0:T(8,128)}, f32[3,23,48,128]{3,2,1,0:T(8,128)S(1)}, u32[]{:S(2)}) copy-start(f32[3,23,48,128]{3,2,1,0:T(8,128)S(1)} %get-tuple-element.55.v2) | copy-start | bytes 5087236
  48.8 0.8 copy-start.8
  50.2 0.7 copy-start.21
  50.9 23.1 %collective-permute-start.8 = (f32[21,40,128]{2,1,0:T(8,128)}, f32[21,40,128]{2,1,0:T(8,128)}, u32[]{:S(2)}, u32[]{:S(2)}) collective-permute-start(f32[21,40,128]{2,1,0:T(8,128)} %get-tuple-element.57), channel_id=1, source_target_pairs={{0,248},{8,0},{16,8},{24,16},{32,24},{40,32},{48,40},{56,48},{64,5... | collective-permute-start | bytes 1290248 | tf_op jit(solution)/shard_map/ppermute | solution.py:604
  52.6 21.4 %all-to-all-start = ((f32[256,1,128]{2,1,0:T(1,128)}), f32[256,1,128]{2,1,0:T(1,128)S(1)}, u32[]{:S(2)}, u32[]{:S(2)}) async-start(f32[256,1,128]{2,1,0:T(1,128)} %bitcast.14), calls=%async_computation | async-start | bytes 262144 | tf_op jit(solution)/shard_map/all_to_all | solution.py:622
  61.1 5.9 %collective-permute-start.9 = (f32[11,40,128]{2,1,0:T(8,128)}, f32[11,40,128]{2,1,0:T(8,128)S(1)}, u32[]{:S(2)}, u32[]{:S(2)}) collective-permute-start(f32[11,40,128]{2,1,0:T(8,128)} %copy-done.21), channel_id=1, source_target_pairs={{0,8},{8,16},{16,24},{24,32},{32,40},{40,48},{48,56},{56,64},{64,7... | collective-permute-start | bytes 675848 | tf_op jit(solution)/shard_map/ppermute | solution.py:604
  66.9 0.7 copy-start.18
  74.0 1.5 %copy-start.1 = (f32[3,23,48,128]{3,2,1,0:T(8,128)S(1)}, f32[3,23,48,128]{3,2,1,0:T(8,128)}, u32[]{:S(2)}) copy-start(f32[3,23,48,128]{3,2,1,0:T(8,128)} %copy-done) | copy-start | bytes 5087236
  75.5 1.5 %copy-start.3 = (f32[3,23,48,128]{3,2,1,0:T(8,128)S(1)}, f32[3,23,48,128]{3,2,1,0:T(8,128)}, u32[]{:S(2)}) copy-start(f32[3,23,48,128]{3,2,1,0:T(8,128)} %copy-done.2) | copy-start | bytes 5087236
  76.9 1.0 copy-start.9
  78.0 1.0 copy-start.11
  78.9 0.9 copy-start.19
  79.9 25.9 %copy-start.7 = (f32[16,32,128]{2,1,0:T(8,128)S(1)}, f32[16,32,128]{2,1,0:T(8,128)}, u32[]{:S(2)}) copy-start(f32[16,32,128]{2,1,0:T(8,128)} %damage.5) | copy-start | bytes 786436
  (1 other events, 0.7 us)

commit v4 on v3

--- a/solution.py
+++ b/solution.py
@@ -17,7 +17,7 @@
 bulk_half = 0.5 * (1.5 + 2.0 / 3.0)
 
 LX, LY, LZ = 16, 32, 128
-ROWS, SHORT, DEPTH, OFF = 48, 40, 23, 3
+ROWS, SHORT, DEPTH, OFF = 48, 40, 28, 5
 
 SHIFT_U = 14.0
 SHIFT_D = 18.0
@@ -97,18 +97,26 @@
 
 def pack_last(u, load, damage, past):
     row = tile_row()
-    return list(u) + [
-        jnp.where(row < 4, roll(damage, 4, 0), load[0]),
-        jnp.where(row < 4, damage, load[1]),
-        jnp.where(row < 4, roll(past, 4, 0), load[2]),
+    return [
+        jnp.where(row < 3, roll(damage, -1, 0), u[0]),
+        jnp.where(row < 3, roll(past, 2, 0), u[1]),
+        u[2],
+        jnp.where(row < 4, roll(load[1], 4, 0), load[0]),
+        jnp.where(row < 4, roll(damage, 4, 0), load[2]),
     ]
+
+
+def low_tile(low, field, k):
+    if field < 4:
+        return low[field, k]
+    return roll(low[3, k], 4, 0) if field == 4 else low[4, k]
 
 
 def damage_tiles(high, low, k):
     row = tile_row()
     above = jnp.where(row < 2, roll(high[3, k], 2, 0), roll(high[4, k], 4, 0))
     above = jnp.where(row < 4, above, roll(high[5, k], 6, 0))
-    below = jnp.where(row < 4, low[4, k], roll(low[3, k], 4, 0))
+    below = jnp.where(row < 4, roll(low[0, k], 1, 0), roll(low[4, k], 4, 0))
     return above, below
 
 
@@ -116,7 +124,7 @@
     row = tile_row()
     above = jnp.where(row < 1, roll(high[0, k], 1, 0), roll(high[1, k], 2, 0))
     above = jnp.where(row < 2, above, roll(high[2, k], 3, 0))
-    return jnp.where(row < 4, above, roll(low[5, k], 4, 0))
+    return jnp.where(row < 4, above, roll(low[1, k], -2, 0))
 
 
 def brief(above, below):
@@ -128,18 +136,20 @@
     return jnp.where(row < 8, flags[3], flags[2])
 
 
-AHEAD = (4, 4, 4, 3, 3, 3, 4)
-BEHIND = (3, 3, 3, 2, 2, 2, 3)
-AHEAD_AT = tuple(sum(AHEAD[:k]) for k in range(7))
-BEHIND_AT = tuple(sum(BEHIND[:k]) for k in range(7))
+AHEAD = (7, 7, 7, 6, 6, 6, 6, 3)
+BEHIND = (5, 5, 5, 4, 4, 4, 5, 2)
+AHEAD_AT = tuple(sum(AHEAD[:k]) for k in range(8))
+BEHIND_AT = tuple(sum(BEHIND[:k]) for k in range(8))
+FRONT, BACK = sum(AHEAD), sum(BEHIND)
 
 
 def pack_kernel(
     disp, force, damage, history, crack,
-    first, last, front, back, front_first, front_last, back_first, back_last,
-    top, bottom, top_crack, bottom_crack, sem,
+    first, last, front, back,
+    top, bottom, top_crack, bottom_crack, front_crack, back_crack, sem,
 ):
-    fields = [disp.at[j] for j in range(3)] + [force.at[j] for j in range(3)] + [damage]
+    fields = [disp.at[j] for j in range(3)] + [force.at[j] for j in range(3)]
+    fields += [damage, history]
     near, far = [], []
     for rows, into, into_crack in ((0, top, top_crack), (24, bottom, bottom_crack)):
         near += [
@@ -154,6 +164,8 @@
         far.append((field.at[0 : AHEAD[k]], front.at[at : at + AHEAD[k]]))
         at = BEHIND_AT[k]
         far.append((field.at[LX - BEHIND[k] : LX], back.at[at : at + BEHIND[k]]))
+    far.append((crack.at[0 : AHEAD[7]], front_crack))
+    far.append((crack.at[LX - BEHIND[7] : LX], back_crack))
     copies = [
         pltpu.make_async_copy(source, target, sem.at[n])
         for n, (source, target) in enumerate(near + far)
@@ -178,15 +190,31 @@
         return carry
 
     lax.fori_loop(0, LX, step, 0, unroll=2)
-    for k in range(7):
-        at = AHEAD_AT[k]
-        front_first[at : at + AHEAD[k]] = top[k, 0 : AHEAD[k]]
-        front_last[at : at + AHEAD[k]] = bottom[k, 0 : AHEAD[k]]
-        at = BEHIND_AT[k]
-        back_first[at : at + BEHIND[k]] = top[k, LX - BEHIND[k] : LX]
-        back_last[at : at + BEHIND[k]] = bottom[k, LX - BEHIND[k] : LX]
     for copy in copies[len(near) :]:
         copy.wait()
+    for out, flag, at in ((front, front_crack, AHEAD_AT[7]), (back, back_crack, BEHIND_AT[7])):
+        for c in range(flag.shape[0]):
+            out[at + c] = jnp.maximum(out[at + c], crack_load * flag[c].astype(f32))
+
+
+def corner_kernel(high, low, front, back):
+    for counts, starts, out, begin in (
+        (AHEAD, AHEAD_AT, front, 0), (BEHIND, BEHIND_AT, back, LX)
+    ):
+        for k in range(8):
+            for c in range(counts[k]):
+                at = starts[k] + c
+                layer = c if begin == 0 else LX - counts[k] + c
+                if k < 6:
+                    out[at, 0:8] = high[k, layer]
+                    out[at, 8:16] = low_tile(low, k, layer)
+                elif k == 6:
+                    above, below = damage_tiles(high, low, layer)
+                    out[at, 0:8] = above
+                    out[at, 8:16] = below
+                else:
+                    out[at, 0:8] = past_tile(high, low, layer)
+                    out[at, 8:16] = jnp.zeros((8, LZ), f32)
 
 
 def stress(u, n, gain):
@@ -303,10 +331,10 @@
         for j in range(3):
             wide[j, i, 0:LY] = disp[j, k]
             wide[j, i, LY : LY + 8] = high[j, k] * flags[3]
-            wide[j, i, LY + 8 : ROWS] = low[j, k] * flags[2]
+            wide[j, i, LY + 8 : ROWS] = low_tile(low, j, k) * flags[2]
             load[j, k, 0:LY] = force[j, k]
             load[j, k, LY : LY + 8] = high[3 + j, k]
-            load[j, k, LY + 8 : ROWS] = low[3 + j, k]
+            load[j, k, LY + 8 : ROWS] = low_tile(low, 3 + j, k)
         own = damage[k]
         above, below = damage_tiles(high, low, k)
         short_damage[i, 0:LY] = own
@@ -317,8 +345,8 @@
         gain[i, LY : LY + 8] = (left * left + stiff_floor) * mask[0:8]
         left = 1.0 - below
         gain[i, LY + 8 : ROWS] = (left * left + stiff_floor) * mask[8:16]
-        past[k, 0:LY] = jnp.maximum(history[k], crack_load * crack[k].astype(f32))
-        past[k, LY:SHORT] = past_tile(high, low, k)
+        past[i, 0:LY] = jnp.maximum(history[k], crack_load * crack[k].astype(f32))
+        past[i, LY:SHORT] = past_tile(high, low, k)
         return carry
 
     lax.fori_loop(0, LX, assemble, 0, unroll=2)
@@ -339,31 +367,40 @@
 
 
 def outer_kernel(
-    wide_in, load, gain_in, v0_in, v1_in, v2_in, short_in, past, partial,
-    ahead, ahead_high, ahead_low, behind, behind_high, behind_low, flags,
-    wide, gain, v0, v1, v2, short_damage, sums, first, last, edge_load,
+    wide_in, load, gain_in, v0_in, v1_in, v2_in, short_in, past_in, partial,
+    ahead, behind, ahead_corner, behind_corner, flags,
+    wide, gain, v0, v1, v2, short_damage, past, sums, edge_load,
 ):
     mask = row_mask(flags)
-    for counts, starts, at, middle, above, below, flag in (
-        (AHEAD, AHEAD_AT, OFF + LX, ahead, ahead_high, ahead_low, flags[1]),
-        (BEHIND, BEHIND_AT, OFF, behind, behind_high, behind_low, flags[0]),
+    for counts, starts, high_side, middle, corner, flag in (
+        (AHEAD, AHEAD_AT, True, ahead, ahead_corner, flags[1]),
+        (BEHIND, BEHIND_AT, False, behind, behind_corner, flags[0]),
     ):
-        for k in range(7):
-            begin = at if at > OFF else OFF - counts[k]
+        for k in range(8):
             for c in range(counts[k]):
-                own = middle[starts[k] + c] * flag
-                high = above[starts[k] + c] * (flag * flags[3])
-                low = below[starts[k] + c] * (flag * flags[2])
-                i = begin + c
+                at = starts[k] + c
+                i = OFF + LX + c if high_side else OFF - counts[k] + c
+                own, high, low = middle[at], corner[at, 0:8], corner[at, 8:16]
+                if k == 7:
+                    past[i, 0:LY] = own
+                    past[i, LY:SHORT] = high
+                    continue
                 if k < 3:
                     into = wide.at[k, i]
+                    own = own * flag
+                    high = high * (flag * flags[3])
+                    low = low * (flag * flags[2])
                 elif k < 6:
-                    into = edge_load.at[k - 3, i - 1 if i < OFF else i - OFF - LX + 2]
+                    into = edge_load.at[k - 3, i - OFF - LX + 4 if high_side else i - 1]
                 else:
                     into = gain.at[i]
-                    short_damage[i, 0:LY] = own
-                    short_damage[i, LY:SHORT] = brief(high, low)
-                    own, high, low = ((1.0 - x) * (1.0 - x) + stiff_floor for x in (own, high, low))
+                    short_damage[i, 0:LY] = own * flag
+                    short_damage[i, LY:SHORT] = brief(
+                        high * (flag * flags[3]), low * (flag * flags[2])
+                    )
+                    own, high, low = (
+                        (1.0 - x) * (1.0 - x) + stiff_floor for x in (own, high, low)
+                    )
                     own = own * flag
                     high = high * (mask[0:8] * flag)
                     low = low * (mask[8:16] * flag)
@@ -375,7 +412,7 @@
         if i < OFF:
             return edge_load[j, i - 1]
         if i >= OFF + LX:
-            return edge_load[j, i - OFF - LX + 2]
+            return edge_load[j, i - OFF - LX + 4]
         return load[j, i - OFF]
 
     def both(source, target, low_end, high_begin, diag, load=None):
@@ -383,9 +420,8 @@
             flag = flags[0] if i < OFF else flags[1] if i >= OFF + LX else None
             store_to(target, mask, flag, load)(i, image)
 
-        begin = low_end - 4
-        sweep(source, gain, begin, low_end, diag, store)
-        sweep(source, gain, high_begin, high_begin + 5, diag, store)
+        sweep(source, gain, low_end - 6, low_end, diag, store)
+        sweep(source, gain, high_begin, high_begin + 8, diag, store)
 
     diag = spring_term - SHIFT_U
     both(wide, v0, OFF + 1, OFF + 14, spring_term, force_at)
@@ -397,21 +433,6 @@
     for i in (*range(OFF, OFF + 3), *range(OFF + 12, OFF + 16)):
         acc = add(i, acc)
     moments_out(sums, acc)
-
-    def put(out, at, ref, j, c):
-        out[at, 0:LY] = ref[j, OFF + c, 0:LY]
-        out[at, LY:SHORT] = brief(ref[j, OFF + c, LY : LY + 8], ref[j, OFF + c, LY + 8 : ROWS])
-
-    for j in range(3):
-        put(first, j, v0, j, 3)
-        for c in range(2):
-            put(first, 3 + 2 * j + c, v1, j, 2 + c)
-            put(last, 3 + 2 * j + c, v2, j, 14 + c)
-        for c in range(3):
-            put(first, 9 + 3 * j + c, v2, j, 1 + c)
-        put(last, j, v1, j, 14)
-    first[18:21] = past[0:3]
-    last[9:11] = past[14:16]
 
 
 def coefficients(gathered, shift):
@@ -462,47 +483,26 @@
 
 
 def damage_kernel(
-    gathered, wide, v0, v1, v2, short_damage, past, high, low, flags,
+    gathered, wide, v0, v1, v2, short_damage, past, flags,
     moved, found, w0, w1, w2, sums, now, drive,
 ):
     a0, a1, a2 = coefficients(gathered, SHIFT_U)
 
-    def cut(value):
-        return value[0:LY], brief(value[LY : LY + 8], value[LY + 8 : ROWS])
-
-    def put(j, i, base, far):
-        body, rest = cut(base)
-        now[j, i, 0:LY] = body
-        now[j, i, LY:SHORT] = rest
-        if far is not None:
-            now[j, i] = now[j, i] + far
+    def current(j, i):
+        value = wide[j, i] + a0 * v0[j, i] + a1 * v1[j, i] + a2 * v2[j, i]
+        now[j, i, 0:LY] = value[0:LY]
+        now[j, i, LY:SHORT] = brief(value[LY : LY + 8], value[LY + 8 : ROWS])
+        return value
 
     def middle(i, carry):
         for j in range(3):
-            value = wide[j, i] + a0 * v0[j, i] + a1 * v1[j, i] + a2 * v2[j, i]
-            put(j, i, value, None)
-            moved[j, i - OFF] = value[0:LY]
+            moved[j, i - OFF] = current(j, i)[0:LY]
         return carry
 
     lax.fori_loop(OFF, OFF + LX, middle, 0, unroll=2)
-    for j in range(3):
-        i = OFF + LX
-        put(j, i, wide[j, i] + a0 * v0[j, i] + a1 * v1[j, i] + a2 * v2[j, i], None)
-        i = OFF - 2
-        far = (a1 * low[j] + a2 * low[3 + 2 * j]) * flags[0]
-        put(j, i, wide[j, i] + a0 * v0[j, i], far)
-        i = OFF - 1
-        far = (a2 * low[4 + 2 * j]) * flags[0]
-        put(j, i, wide[j, i] + a0 * v0[j, i] + a1 * v1[j, i], far)
-        i = OFF + LX + 1
-        far = (a2 * high[9 + 3 * j]) * flags[1]
-        put(j, i, wide[j, i] + a0 * v0[j, i] + a1 * v1[j, i], far)
-        i = OFF + LX + 2
-        far = (a1 * high[3 + 2 * j] + a2 * high[10 + 3 * j]) * flags[1]
-        put(j, i, wide[j, i] + a0 * v0[j, i], far)
-        i = OFF + LX + 3
-        far = (a0 * high[j] + a1 * high[4 + 2 * j] + a2 * high[11 + 3 * j]) * flags[1]
-        put(j, i, wide[j, i], far)
+    for i in (OFF - 2, OFF - 1, *range(OFF + LX, OFF + LX + 4)):
+        for j in range(3):
+            current(j, i)
 
     row = lax.broadcasted_iota(jnp.int32, (8, LZ), 0)
     mask = jnp.where(row < 4, flags[3], flags[2])
@@ -520,18 +520,14 @@
         return bulk_half * (positive * positive) + (squares - trace * trace * (1.0 / 3.0))
 
     def step(i, carry):
-        value = jnp.maximum(past[i - OFF], energy(i))
+        value = jnp.maximum(past[i], energy(i))
         drive[i] = value
         found[i - OFF] = value[0:LY]
         return carry
 
     lax.fori_loop(OFF, OFF + LX, step, 0, unroll=4)
-    for c in range(3):
-        i = OFF + LX + c
-        drive[i] = jnp.maximum(high[18 + c], energy(i))
-    for c in range(2):
-        i = OFF - 2 + c
-        drive[i] = jnp.maximum(low[9 + c], energy(i))
+    for i in (OFF - 2, OFF - 1, *range(OFF + LX, OFF + LX + 3)):
+        drive[i] = jnp.maximum(past[i], energy(i))
 
     def flag_of(i):
         return jnp.where(i < OFF, flags[0], jnp.where(i >= OFF + LX, flags[1], 1.0))
@@ -547,7 +543,7 @@
             target[i, LY:SHORT] = value[LY:SHORT] * mask
             return here, n
 
-        lax.fori_loop(begin, end, step, (source[begin - 1], source[begin]), unroll=4)
+        lax.fori_loop(begin, end, step, (source[begin - 1], source[begin]), unroll=7)
 
     full = tough_ratio + 6.0 * length_term
 
@@ -599,15 +595,9 @@
 
 
 def send(values, dx, dy):
-    nx, ny = lax.axis_size("gx"), lax.axis_size("gy")
-    if not dy:
-        return lax.ppermute(values, "gx", [(i, (i + dx) % nx) for i in range(nx)])
-    if not dx:
-        return lax.ppermute(values, "gy", [(k, (k + dy) % ny) for k in range(ny)])
-    pairs = [
-        (i * ny + k, (i + dx) % nx * ny + (k + dy) % ny) for i in range(nx) for k in range(ny)
-    ]
-    return lax.ppermute(values, ("gx", "gy"), pairs)
+    axis, step = ("gx", dx) if dx else ("gy", dy)
+    size = lax.axis_size(axis)
+    return lax.ppermute(values, axis, [(i, (i + step) % size) for i in range(size)])
 
 
 def step(displacement, force, damage, history, crack_flags):
@@ -621,49 +611,43 @@
     def gather(sums):
         return lax.all_to_all(sums, axes, 0, 0, tiled=True)
 
-    edge_rows = (8, LX, 8, LZ)
-    front, back = sum(AHEAD), sum(BEHIND)
-    first, last, front_own, back_own, ff, fl, bf, bl = call(
+    edge_rows, edge_flags = (8, LX, 8, LZ), pltpu.VMEM((LX, 8, LZ), jnp.int32)
+    first, last, front, back = call(
         pack_kernel,
-        [(6, LX, 8, LZ)] * 2
-        + [(front, LY, LZ), (back, LY, LZ)]
-        + [(front, 8, LZ)] * 2
-        + [(back, 8, LZ)] * 2,
+        [(6, LX, 8, LZ), (5, LX, 8, LZ), (FRONT, LY, LZ), (BACK, LY, LZ)],
         [
-            edge_rows, edge_rows,
-            pltpu.VMEM((LX, 8, LZ), jnp.int32), pltpu.VMEM((LX, 8, LZ), jnp.int32),
-            pltpu.SemaphoreType.DMA((24,)),
+            edge_rows, edge_rows, edge_flags, edge_flags,
+            pltpu.VMEM((AHEAD[7], LY, LZ), jnp.int32),
+            pltpu.VMEM((BEHIND[7], LY, LZ), jnp.int32),
+            pltpu.SemaphoreType.DMA((28,)),
         ],
         hbm=True,
     )(displacement, force, damage, history, crack_flags)
     high = send(first, 0, -1)
     low = send(last, 0, 1)
-    ahead, behind = send(front_own, -1, 0), send(back_own, 1, 0)
-    ahead_high, ahead_low = send(ff, -1, -1), send(fl, -1, 1)
-    behind_high, behind_low = send(bf, 1, -1), send(bl, 1, 1)
+    ahead = send(front, -1, 0)
+    behind = send(back, 1, 0)
+    corners = call(corner_kernel, [(FRONT, 16, LZ), (BACK, 16, LZ)])(high, low)
+    ahead_corner = send(corners[0], -1, 0)
+    behind_corner = send(corners[1], 1, 0)
     wide, load, gain, v0, v1, v2, short_damage, past, partial = call(
         inner_kernel,
-        [VECTOR, (3, LX, ROWS, LZ), SCALAR, VECTOR, VECTOR, VECTOR, BRIEF]
-        + [(LX, SHORT, LZ), (6, 8, LZ)],
+        [VECTOR, (3, LX, ROWS, LZ), SCALAR, VECTOR, VECTOR, VECTOR, BRIEF, BRIEF, (6, 8, LZ)],
     )(displacement, force, damage, history, crack_flags, high, low, flags=flags)
-    wide, gain, v0, v1, v2, short_damage, sums, first, last = call(
+    wide, gain, v0, v1, v2, short_damage, past, sums = call(
         outer_kernel,
-        [VECTOR, SCALAR, VECTOR, VECTOR, VECTOR, BRIEF]
-        + [(count, LZ), (21, SHORT, LZ), (11, SHORT, LZ)],
-        scratch=[(3, 5, ROWS, LZ)],
-        aliases={0: 0, 2: 1, 3: 2, 4: 3, 5: 4, 6: 5},
+        [VECTOR, SCALAR, VECTOR, VECTOR, VECTOR, BRIEF, BRIEF, (count, LZ)],
+        scratch=[(3, 10, ROWS, LZ)],
+        aliases={0: 0, 2: 1, 3: 2, 4: 3, 5: 4, 6: 5, 7: 6},
     )(
         wide, load, gain, v0, v1, v2, short_damage, past, partial,
-        ahead, ahead_high, ahead_low, behind, behind_high, behind_low, flags=flags,
+        ahead, behind, ahead_corner, behind_corner, flags=flags,
     )
-    high = send(first, -1, 0)
-    low = send(last, 1, 0)
-    gathered = gather(sums)
     moved, found, w0, w1, w2, sums = call(
         damage_kernel,
         [whole(3, LX, LY, LZ), whole(LX, LY, LZ), BRIEF, BRIEF, BRIEF, (count, LZ)],
         [(3, DEPTH, SHORT, LZ), BRIEF],
-    )(gathered, wide, v0, v1, v2, short_damage, past, high, low, flags=flags)
+    )(gather(sums), wide, v0, v1, v2, short_damage, past, flags=flags)
     (damage_out,) = call(update_kernel, [whole(LX, LY, LZ)])(
         gather(sums), damage, w0, w1, w2
     )

time: 107 us -> 85.2 us (0.80)
  blocking collectives: 20.1 us -> 43.6 us
  local copies, waits for them, and re-layouts: 19.6 us -> 0.02 us
  starting transfers between devices: 33.2 us -> 14 us
  waiting for transfers between devices: 14.6 us -> 6.49 us
  Pallas kernels: 18.3 us -> 20 us
    all_to_all x1 -> x2, blocking collectives: 20.1 us -> 43.6 us  [gather(): return lax.all_to_all(sums, axes, 0, 0, tiled=True)]
    unnamed x44 -> x10, local copies, waits for them, and re-layouts: 19.6 us -> 0.02 us
    ppermute x10 -> x6, starting transfers between devices: 24.8 us -> 14 us  [send(): lax.ppermute(values, axis, [(i, (i + step) % size) for i in range(size)])]
    all_to_all x1 -> x0, starting transfers between devices: 8.42 us -> none  [gather(): return lax.all_to_all(sums, axes, 0, 0, tiled=True)]
    all_to_all x1 -> x0, waiting for transfers between devices: 6.4 us -> none  [gather(): return lax.all_to_all(sums, axes, 0, 0, tiled=True)]
    pallas_call x5 -> x6, Pallas kernels: 18.3 us -> 20 us  [run(): pl.pallas_call(kernel, out_shape=[s if isinstance(s, jax.ShapeDtypeStruct...]
    ppermute x10 -> x6, waiting for transfers between devices: 8.16 us -> 6.49 us  [send(): lax.ppermute(values, axis, [(i, (i + step) % size) for i in range(size)])]
  transfers between devices with their start and end apart: 11 -> 6, of which waited for: 3 -> 2; matrix products, arithmetic and copies ran while one was open for 0% -> 0% of each run, Pallas kernels for 4% -> 7%
where the time goes in v4:
time: 85.2 us; the launch traced here: 85 us
  blocking collectives  43.6 us (51%)
  Pallas kernels  20 us (23%)
  starting transfers between devices  14 us (16%)
  waiting for transfers between devices  6.49 us (8%)
    all_to_all x2, blocking collectives, gather(): return lax.all_to_all(sums, axes, 0, 0, tiled=True)  43.6 us
    pallas_call x6, Pallas kernels, run(): pl.pallas_call(kernel, out_shape=[s if isinstance(s, jax.ShapeDtypeStruct...  20 us
    ppermute x6, starting transfers between devices, send(): lax.ppermute(values, axis, [(i, (i + step) % size) for i in range(size)])  14 us
    ppermute x6, waiting for transfers between devices, send(): lax.ppermute(values, axis, [(i, (i + step) % size) for i in range(size)])  6.49 us
  transfers between devices with their start and end apart: 6, of which 2 were waited for; matrix products, arithmetic and copies ran while one was open for 0% of the time, Pallas kernels for 7%

profile of v4, /device:TPU:1, one launch (start us, length us, event | category | flops | bytes accessed | tf_op | source)
XLA Modules:
  0.0 85.0 jit_solution(6143069125761222628)
XLA Ops:
  0.6 0.0 copy-start.2
  0.6 0.0 copy-start.4
  0.7 0.0 copy-start.3
  0.7 0.0 copy-start.1
  0.7 0.0 copy-start
  0.7 3.2 %shard_map.76 = (f32[6,16,8,128]{3,2,1,0:T(8,128)S(1)}, f32[5,16,8,128]{3,2,1,0:T(8,128)S(1)}, f32[48,32,128]{2,1,0:T(8,128)}, f32[34,32,128]{2,1,0:T(8,128)}) custom-call(f32[3,16,32,128]{3,2,1,0:T(8,128)} %disp.3, f32[3,16,32,128]{3,2,1,0:T(8,128)} %force.3, f32[16,32,128]{2,1,0:T(8,128)} %damage.5, f32[16,32,128]{2,1,0:T(8,128)} %history.3, ...), custom_call_target="tpu_custom_call" | custom-call | tf_op jit(solution)/shard_map/pallas_call | solution.py:50
  3.9 6.5 %collective-permute-start = (f32[6,16,8,128]{3,2,1,0:T(8,128)S(1)}, f32[6,16,8,128]{3,2,1,0:T(8,128)S(1)}, u32[]{:S(2)}, u32[]{:S(2)}) collective-permute-start(f32[6,16,8,128]{3,2,1,0:T(8,128)S(1)} %get-tuple-element.31), channel_id=1, source_target_pairs={{0,7},{1,0},{2,1},{3,2},{4,3},{5,4},{6,5},{7,6},{8,15},{9,8},{10,9... | collective-permute-start | bytes 1179656 | tf_op jit(solution)/shard_map/ppermute | solution.py:600
  10.3 1.0 %collective-permute-start.2 = (f32[48,32,128]{2,1,0:T(8,128)}, f32[48,32,128]{2,1,0:T(8,128)}, u32[]{:S(2)}, u32[]{:S(2)}) collective-permute-start(f32[48,32,128]{2,1,0:T(8,128)} %get-tuple-element.42), channel_id=1, source_target_pairs={{0,248},{8,0},{16,8},{24,16},{32,24},{40,32},{48,40},{56,48},{64,5... | collective-permute-start | bytes 2359304 | tf_op jit(solution)/shard_map/ppermute | solution.py:600
  11.3 0.0 collective-permute-start.1
  11.3 1.1 %collective-permute-start.3 = (f32[34,32,128]{2,1,0:T(8,128)}, f32[34,32,128]{2,1,0:T(8,128)}, u32[]{:S(2)}, u32[]{:S(2)}) collective-permute-start(f32[34,32,128]{2,1,0:T(8,128)} %get-tuple-element.43), channel_id=1, source_target_pairs={{0,8},{8,16},{16,24},{24,32},{32,40},{40,48},{48,56},{56,64},{64,7... | collective-permute-start | bytes 1671176 | tf_op jit(solution)/shard_map/ppermute | solution.py:600
  12.4 6.0 %collective-permute-done.1.low = f32[5,16,8,128]{3,2,1,0:T(8,128)S(1)} collective-permute-done((f32[5,16,8,128]{3,2,1,0:T(8,128)S(1)}, f32[5,16,8,128]{3,2,1,0:T(8,128)S(1)}, u32[]{:S(2)}, u32[]{:S(2)}) %collective-permute-start.1) | collective-permute-done | bytes 327712 | tf_op jit(solution)/shard_map/ppermute | solution.py:600
  18.4 0.0 collective-permute-done.high
  18.4 0.9 %shard_map.78 = (f32[48,16,128]{2,1,0:T(8,128)}, f32[34,16,128]{2,1,0:T(8,128)}) custom-call(f32[6,16,8,128]{3,2,1,0:T(8,128)S(1)} %collective-permute-done.high, f32[5,16,8,128]{3,2,1,0:T(8,128)S(1)} %collective-permute-done.1.low), custom_call_target="tpu_custom_call" | custom-call | tf_op jit(solution)/shard_map/pallas_call | solution.py:50
  19.3 5.5 %collective-permute-start.4 = (f32[48,16,128]{2,1,0:T(8,128)}, f32[48,16,128]{2,1,0:T(8,128)S(1)}, u32[]{:S(2)}, u32[]{:S(2)}) collective-permute-start(f32[48,16,128]{2,1,0:T(8,128)} %get-tuple-element.44), channel_id=1, source_target_pairs={{0,248},{8,0},{16,8},{24,16},{32,24},{40,32},{48,40},{56,48},{64,5... | collective-permute-start | bytes 1179656 | tf_op jit(solution)/shard_map/ppermute | solution.py:600
  24.8 0.0 collective-permute-start.5
  24.8 0.1 add_convert_fusion.flags
  24.9 0.0 copy-done.2
  24.9 0.0 copy-done.4
  24.9 0.0 copy-done.3
  24.9 0.0 copy-done.1
  24.9 0.0 copy-done
  25.0 4.9 %shard_map.77 = (f32[3,28,48,128]{3,2,1,0:T(8,128)S(1)}, f32[3,16,48,128]{3,2,1,0:T(8,128)S(1)}, f32[28,48,128]{2,1,0:T(8,128)S(1)}, f32[3,28,48,128]{3,2,1,0:T(...) custom-call(f32[3,16,32,128]{3,2,1,0:T(8,128)S(1)} %copy-done, ...), custom_call_target="tpu_custom_call" | custom-call | tf_op jit(solution)/shard_map/pallas_call | solution.py:50
  29.8 0.0 collective-permute-done.3.behind
  29.8 0.0 collective-permute-done.5.behind_corner
  29.8 0.4 collective-permute-done.4.ahead_corner
  30.3 0.0 collective-permute-done.2.ahead
  30.3 5.2 %shard_map.79 = (f32[3,28,48,128]{3,2,1,0:T(8,128)S(1)}, f32[28,48,128]{2,1,0:T(8,128)S(1)}, f32[3,28,48,128]{3,2,1,0:T(8,128)S(1)}, f32[3,28,48,128]{3,2,1,0:T(...) custom-call(f32[3,28,48,128]{3,2,1,0:T(8,128)S(1)} %get-tuple-elemen, ...), custom_call_target="tpu_custom_call", output_to_operand_aliasing={{0}: (0, {}), {1}: (2, {}), {2}: (3, {}), {3}: (4, {}), {4}... | custom-call | tf_op jit(solution)/shard_map/pallas_call | solution.py:50
  35.5 25.2 %all_to_all.22 = f32[256,1,128]{2,1,0:T(1,128)S(1)} all-to-all(f32[256,1,128]{2,1,0:T(1,128)S(1)} %bitcast.14), channel_id=1, replica_groups=mesh['gx'=32,'gy'=8] {'gx','gy'}, dimensions={0} | all-to-all | bytes 262144 | tf_op jit(solution)/shard_map/all_to_all | solution.py:612
  60.7 4.9 %shard_map.80 = (f32[3,16,32,128]{3,2,1,0:T(8,128)}, f32[16,32,128]{2,1,0:T(8,128)}, f32[28,40,128]{2,1,0:T(8,128)S(1)}, f32[28,40,128]{2,1,0:T(8,128)S(1)}, f32...) custom-call(f32[256,128]{1,0:T(8,128)S(1)} %bitcast.12, f32[3,28,48,128]{3,2,1,0:T(8,128)S(1)} %get-tuple-element.47.wide, ...), custom_call_target="tpu_custom_call" | custom-call | tf_op jit(solution)/shard_map/pallas_call | solution.py:50
  65.6 18.4 %all_to_all.23 = f32[256,1,128]{2,1,0:T(1,128)S(1)} all-to-all(f32[256,1,128]{2,1,0:T(1,128)S(1)} %bitcast.15), channel_id=1, replica_groups=mesh['gx'=32,'gy'=8] {'gx','gy'}, dimensions={0} | all-to-all | bytes 262144 | tf_op jit(solution)/shard_map/all_to_all | solution.py:612
  84.0 1.0 %shard_map.81 = f32[16,32,128]{2,1,0:T(8,128)} custom-call(f32[256,128]{1,0:T(8,128)S(1)} %bitcast.13, f32[16,32,128]{2,1,0:T(8,128)S(1)} %copy-done.2, f32[28,40,128]{2,1,0:T(8,128)S(1)} %get-tuple-element.55.w0, f32[28,40,128]{2,1,0:T(8,128)S(1)} %get-tuple-element.56.w1, f32[28,40,128]{2,1,0:T(8,128)S(1)} %get-tuple-element.57.w2), custom_call_target="tpu_custom_call" | custom-call | tf_op jit(solution)/shard_map/pallas_call | solution.py:50
Async XLA Ops:
  0.6 24.3 %copy-start.2 = (f32[16,32,128]{2,1,0:T(8,128)S(1)}, f32[16,32,128]{2,1,0:T(8,128)}, u32[]{:S(2)}) copy-start(f32[16,32,128]{2,1,0:T(8,128)} %damage.5) | copy-start | bytes 786436
  0.6 24.3 %copy-start.4 = (s32[16,32,128]{2,1,0:T(8,128)S(1)}, s32[16,32,128]{2,1,0:T(8,128)}, u32[]{:S(2)}) copy-start(s32[16,32,128]{2,1,0:T(8,128)} %crack.3) | copy-start | bytes 786436
  0.7 24.3 %copy-start.3 = (f32[16,32,128]{2,1,0:T(8,128)S(1)}, f32[16,32,128]{2,1,0:T(8,128)}, u32[]{:S(2)}) copy-start(f32[16,32,128]{2,1,0:T(8,128)} %history.3) | copy-start | bytes 786436
  0.7 24.3 %copy-start.1 = (f32[3,16,32,128]{3,2,1,0:T(8,128)S(1)}, f32[3,16,32,128]{3,2,1,0:T(8,128)}, u32[]{:S(2)}) copy-start(f32[3,16,32,128]{3,2,1,0:T(8,128)} %force.3) | copy-start | bytes 2359300
  0.7 24.3 %copy-start = (f32[3,16,32,128]{3,2,1,0:T(8,128)S(1)}, f32[3,16,32,128]{3,2,1,0:T(8,128)}, u32[]{:S(2)}) copy-start(f32[3,16,32,128]{3,2,1,0:T(8,128)} %disp.3) | copy-start | bytes 2359300
  3.9 14.6 %collective-permute-start = (f32[6,16,8,128]{3,2,1,0:T(8,128)S(1)}, f32[6,16,8,128]{3,2,1,0:T(8,128)S(1)}, u32[]{:S(2)}, u32[]{:S(2)}) collective-permute-start(f32[6,16,8,128]{3,2,1,0:T(8,128)S(1)} %get-tuple-element.31), channel_id=1, source_target_pairs={{0,7},{1,0},{2,1},{3,2},{4,3},{5,4},{6,5},{7,6},{8,15},{9,8},{10,9... | collective-permute-start | bytes 1179656 | tf_op jit(solution)/shard_map/ppermute | solution.py:600
  10.3 20.0 %collective-permute-start.2 = (f32[48,32,128]{2,1,0:T(8,128)}, f32[48,32,128]{2,1,0:T(8,128)}, u32[]{:S(2)}, u32[]{:S(2)}) collective-permute-start(f32[48,32,128]{2,1,0:T(8,128)} %get-tuple-element.42), channel_id=1, source_target_pairs={{0,248},{8,0},{16,8},{24,16},{32,24},{40,32},{48,40},{56,48},{64,5... | collective-permute-start | bytes 2359304 | tf_op jit(solution)/shard_map/ppermute | solution.py:600
  11.3 7.1 %collective-permute-start.1 = (f32[5,16,8,128]{3,2,1,0:T(8,128)S(1)}, f32[5,16,8,128]{3,2,1,0:T(8,128)S(1)}, u32[]{:S(2)}, u32[]{:S(2)}) collective-permute-start(f32[5,16,8,128]{3,2,1,0:T(8,128)S(1)} %get-tuple-element.32), channel_id=1, source_target_pairs={{0,1},{1,2},{2,3},{3,4},{4,5},{5,6},{6,7},{7,0},{8,9},{9,10},{10,1... | collective-permute-start | bytes 983048 | tf_op jit(solution)/shard_map/ppermute | solution.py:600
  11.3 18.5 %collective-permute-start.3 = (f32[34,32,128]{2,1,0:T(8,128)}, f32[34,32,128]{2,1,0:T(8,128)}, u32[]{:S(2)}, u32[]{:S(2)}) collective-permute-start(f32[34,32,128]{2,1,0:T(8,128)} %get-tuple-element.43), channel_id=1, source_target_pairs={{0,8},{8,16},{16,24},{24,32},{32,40},{40,48},{48,56},{56,64},{64,7... | collective-permute-start | bytes 1671176 | tf_op jit(solution)/shard_map/ppermute | solution.py:600
  19.3 11.0 %collective-permute-start.4 = (f32[48,16,128]{2,1,0:T(8,128)}, f32[48,16,128]{2,1,0:T(8,128)S(1)}, u32[]{:S(2)}, u32[]{:S(2)}) collective-permute-start(f32[48,16,128]{2,1,0:T(8,128)} %get-tuple-element.44), channel_id=1, source_target_pairs={{0,248},{8,0},{16,8},{24,16},{32,24},{40,32},{48,40},{56,48},{64,5... | collective-permute-start | bytes 1179656 | tf_op jit(solution)/shard_map/ppermute | solution.py:600
  24.8 5.0 %collective-permute-start.5 = (f32[34,16,128]{2,1,0:T(8,128)}, f32[34,16,128]{2,1,0:T(8,128)}, u32[]{:S(2)}, u32[]{:S(2)}) collective-permute-start(f32[34,16,128]{2,1,0:T(8,128)} %get-tuple-element.45), channel_id=1, source_target_pairs={{0,8},{8,16},{16,24},{24,32},{32,40},{40,48},{48,56},{56,64},{64,7... | collective-permute-start | bytes 835592 | tf_op jit(solution)/shard_map/ppermute | solution.py:600

commit v5 on v4

--- a/solution.py
+++ b/solution.py
@@ -25,12 +25,15 @@
 VECTOR = (3, DEPTH, ROWS, LZ)
 SCALAR = (DEPTH, ROWS, LZ)
 BRIEF = (DEPTH, SHORT, LZ)
+FIELD = (LX, LY, LZ)
 
 
 def fast(shape):
-    if INTERPRET:
-        return jax.ShapeDtypeStruct(shape, f32)
-    return pltpu.VMEM(shape, f32)
+    return fast_as(shape, f32)
+
+
+def fast_as(shape, kind):
+    return jax.ShapeDtypeStruct(shape, kind) if INTERPRET else pltpu.VMEM(shape, kind)
 
 
 def whole(*shape):
@@ -49,7 +52,7 @@
             args, specs = (*args, flags), specs + [smem]
         return pl.pallas_call(
             kernel,
-            out_shape=[s if isinstance(s, jax.ShapeDtypeStruct) else fast(s) for s in outs],
+            out_shape=[fast(s) if isinstance(s, tuple) else s for s in outs],
             in_specs=specs,
             out_specs=[vmem] * len(outs),
             scratch_shapes=[pltpu.VMEM(s, f32) if isinstance(s, tuple) else s for s in scratch],
@@ -144,77 +147,72 @@
 
 
 def pack_kernel(
-    disp, force, damage, history, crack,
-    first, last, front, back,
-    top, bottom, top_crack, bottom_crack, front_crack, back_crack, sem,
+    disp_in, force_in, damage_in, history_in, crack_in, flags,
+    disp, force, damage, history, crack, first, last, front, back, sem,
 ):
-    fields = [disp.at[j] for j in range(3)] + [force.at[j] for j in range(3)]
-    fields += [damage, history]
-    near, far = [], []
-    for rows, into, into_crack in ((0, top, top_crack), (24, bottom, bottom_crack)):
-        near += [
-            (disp.at[:, :, rows : rows + 8], into.at[0:3]),
-            (force.at[:, :, rows : rows + 8], into.at[3:6]),
-            (damage.at[:, rows : rows + 8], into.at[6]),
-            (history.at[:, rows : rows + 8], into.at[7]),
-            (crack.at[:, rows : rows + 8], into_crack),
-        ]
-    for k, field in enumerate(fields):
-        at = AHEAD_AT[k]
-        far.append((field.at[0 : AHEAD[k]], front.at[at : at + AHEAD[k]]))
-        at = BEHIND_AT[k]
-        far.append((field.at[LX - BEHIND[k] : LX], back.at[at : at + BEHIND[k]]))
-    far.append((crack.at[0 : AHEAD[7]], front_crack))
-    far.append((crack.at[LX - BEHIND[7] : LX], back_crack))
     copies = [
         pltpu.make_async_copy(source, target, sem.at[n])
-        for n, (source, target) in enumerate(near + far)
+        for n, (source, target) in enumerate(
+            (
+                (crack_in, crack), (history_in, history), (damage_in, damage),
+                (disp_in, disp), (force_in, force),
+            )
+        )
     ]
     for copy in copies:
         copy.start()
-    for copy in copies[: len(near)]:
+    for copy in copies:
         copy.wait()
 
     def step(k, carry):
-        for into, flag, out, pack in (
-            (top, top_crack, first, pack_first),
-            (bottom, bottom_crack, last, pack_last),
-        ):
-            past = jnp.maximum(into[7, k], crack_load * flag[k].astype(f32))
+        for rows, out, pack in ((0, first, pack_first), (24, last, pack_last)):
+            at = slice(rows, rows + 8)
+            past = jnp.maximum(history[k, at], crack_load * crack[k, at].astype(f32))
             tiles = pack(
-                [into[j, k] for j in range(3)], [into[3 + j, k] for j in range(3)],
-                into[6, k], past,
+                [disp[j, k, at] for j in range(3)], [force[j, k, at] for j in range(3)],
+                damage[k, at], past,
             )
-            for at, tile in enumerate(tiles):
-                out[at, k] = tile
+            for n, tile in enumerate(tiles):
+                out[n, k] = tile
         return carry
 
     lax.fori_loop(0, LX, step, 0, unroll=2)
-    for copy in copies[len(near) :]:
-        copy.wait()
-    for out, flag, at in ((front, front_crack, AHEAD_AT[7]), (back, back_crack, BEHIND_AT[7])):
-        for c in range(flag.shape[0]):
-            out[at + c] = jnp.maximum(out[at + c], crack_load * flag[c].astype(f32))
+    for counts, starts, out, ahead in ((AHEAD, AHEAD_AT, front, True), (BEHIND, BEHIND_AT, back, False)):
+        for k in range(8):
+            size, at = counts[k], starts[k]
+            begin = 0 if ahead else LX - size
+            layers = slice(begin, begin + size)
+            if k == 7:
+                flag = crack[layers].astype(f32)
+                out[at : at + size] = jnp.maximum(history[layers], crack_load * flag)
+            else:
+                field = disp.at[k] if k < 3 else force.at[k - 3] if k < 6 else damage
+                out[at : at + size] = field[layers]
+
+
+FRONT_TILES = (7, 7, 7, 6, 6, 6, 7, 7, 7, 6, 6)
+BACK_TILES = (5,) * 11
+FRONT_TILES_AT = tuple(sum(FRONT_TILES[:k]) for k in range(11))
+BACK_TILES_AT = tuple(sum(BACK_TILES[:k]) for k in range(11))
 
 
 def corner_kernel(high, low, front, back):
-    for counts, starts, out, begin in (
-        (AHEAD, AHEAD_AT, front, 0), (BEHIND, BEHIND_AT, back, LX)
+    for counts, starts, out, ahead in (
+        (FRONT_TILES, FRONT_TILES_AT, front, True), (BACK_TILES, BACK_TILES_AT, back, False)
     ):
-        for k in range(8):
-            for c in range(counts[k]):
-                at = starts[k] + c
-                layer = c if begin == 0 else LX - counts[k] + c
-                if k < 6:
-                    out[at, 0:8] = high[k, layer]
-                    out[at, 8:16] = low_tile(low, k, layer)
-                elif k == 6:
-                    above, below = damage_tiles(high, low, layer)
-                    out[at, 0:8] = above
-                    out[at, 8:16] = below
-                else:
-                    out[at, 0:8] = past_tile(high, low, layer)
-                    out[at, 8:16] = jnp.zeros((8, LZ), f32)
+        for k in range(11):
+            size, at = counts[k], starts[k]
+            begin = 0 if ahead else LX - size
+            source = high.at[k] if k < 6 else low.at[k - 6]
+            out[at : at + size] = source[begin : begin + size]
+
+
+class Corner:
+    def __init__(self, ref, starts, offset):
+        self.ref, self.starts, self.offset = ref, starts, offset
+
+    def __getitem__(self, key):
+        return self.ref[self.starts[key[0] + self.offset] + key[1]]
 
 
 def stress(u, n, gain):
@@ -372,19 +370,24 @@
     wide, gain, v0, v1, v2, short_damage, past, sums, edge_load,
 ):
     mask = row_mask(flags)
-    for counts, starts, high_side, middle, corner, flag in (
-        (AHEAD, AHEAD_AT, True, ahead, ahead_corner, flags[1]),
-        (BEHIND, BEHIND_AT, False, behind, behind_corner, flags[0]),
+    for counts, starts, high_side, middle, corner, tiles, flag in (
+        (AHEAD, AHEAD_AT, True, ahead, ahead_corner, FRONT_TILES_AT, flags[1]),
+        (BEHIND, BEHIND_AT, False, behind, behind_corner, BACK_TILES_AT, flags[0]),
     ):
+        above, below = Corner(corner, tiles, 0), Corner(corner, tiles, 6)
         for k in range(8):
             for c in range(counts[k]):
-                at = starts[k] + c
+                own = middle[starts[k] + c]
                 i = OFF + LX + c if high_side else OFF - counts[k] + c
-                own, high, low = middle[at], corner[at, 0:8], corner[at, 8:16]
+                layer = c if high_side else 5 - counts[k] + c
                 if k == 7:
                     past[i, 0:LY] = own
-                    past[i, LY:SHORT] = high
+                    past[i, LY:SHORT] = past_tile(above, below, layer)
                     continue
+                if k < 6:
+                    high, low = above[k, layer], low_tile(below, k, layer)
+                else:
+                    high, low = damage_tiles(above, below, layer)
                 if k < 3:
                     into = wide.at[k, i]
                     own = own * flag
@@ -611,29 +614,26 @@
     def gather(sums):
         return lax.all_to_all(sums, axes, 0, 0, tiled=True)
 
-    edge_rows, edge_flags = (8, LX, 8, LZ), pltpu.VMEM((LX, 8, LZ), jnp.int32)
-    first, last, front, back = call(
+    disp, load, old, history, crack, first, last, front, back = call(
         pack_kernel,
-        [(6, LX, 8, LZ), (5, LX, 8, LZ), (FRONT, LY, LZ), (BACK, LY, LZ)],
-        [
-            edge_rows, edge_rows, edge_flags, edge_flags,
-            pltpu.VMEM((AHEAD[7], LY, LZ), jnp.int32),
-            pltpu.VMEM((BEHIND[7], LY, LZ), jnp.int32),
-            pltpu.SemaphoreType.DMA((28,)),
-        ],
+        [(3, *FIELD), (3, *FIELD), FIELD, FIELD, fast_as(FIELD, jnp.int32)]
+        + [(6, LX, 8, LZ), (5, LX, 8, LZ), (FRONT, LY, LZ), (BACK, LY, LZ)],
+        [pltpu.SemaphoreType.DMA((5,))],
         hbm=True,
-    )(displacement, force, damage, history, crack_flags)
+    )(displacement, force, damage, history, crack_flags, flags=flags)
     high = send(first, 0, -1)
     low = send(last, 0, 1)
     ahead = send(front, -1, 0)
     behind = send(back, 1, 0)
-    corners = call(corner_kernel, [(FRONT, 16, LZ), (BACK, 16, LZ)])(high, low)
+    corners = call(
+        corner_kernel, [(sum(FRONT_TILES), 8, LZ), (sum(BACK_TILES), 8, LZ)]
+    )(high, low)
     ahead_corner = send(corners[0], -1, 0)
     behind_corner = send(corners[1], 1, 0)
     wide, load, gain, v0, v1, v2, short_damage, past, partial = call(
         inner_kernel,
         [VECTOR, (3, LX, ROWS, LZ), SCALAR, VECTOR, VECTOR, VECTOR, BRIEF, BRIEF, (6, 8, LZ)],
-    )(displacement, force, damage, history, crack_flags, high, low, flags=flags)
+    )(disp, load, old, history, crack, high, low, flags=flags)
     wide, gain, v0, v1, v2, short_damage, past, sums = call(
         outer_kernel,
         [VECTOR, SCALAR, VECTOR, VECTOR, VECTOR, BRIEF, BRIEF, (count, LZ)],
@@ -649,7 +649,7 @@
         [(3, DEPTH, SHORT, LZ), BRIEF],
     )(gather(sums), wide, v0, v1, v2, short_damage, past, flags=flags)
     (damage_out,) = call(update_kernel, [whole(LX, LY, LZ)])(
-        gather(sums), damage, w0, w1, w2
+        gather(sums), old, w0, w1, w2
     )
     return moved, damage_out, found
 

time: 85.2 us -> 81.1 us (0.952)
  Pallas kernels: 20 us -> 17.6 us
  blocking collectives: 43.6 us -> 42.2 us
    pallas_call x6, Pallas kernels: 20 us -> 17.6 us  [run(): pl.pallas_call(kernel, out_shape=[fast(s) if isinstance(s, tuple) else s...]
    all_to_all x2, blocking collectives: 43.6 us -> 42.2 us  [gather(): return lax.all_to_all(sums, axes, 0, 0, tiled=True)]
  transfers between devices with their start and end apart: 6 -> 6, of which waited for: 2 -> 1; matrix products, arithmetic and copies ran while one was open for 0% -> 0% of each run, Pallas kernels for 7% -> 6%
where the time goes in v5:
time: 81.1 us; the launch traced here: 81 us
  blocking collectives  42.2 us (52%)
  Pallas kernels  17.6 us (22%)
  starting transfers between devices  14.8 us (18%)
  waiting for transfers between devices  5.68 us (7%)
    all_to_all x2, blocking collectives, gather(): return lax.all_to_all(sums, axes, 0, 0, tiled=True)  42.2 us
    pallas_call x6, Pallas kernels, run(): pl.pallas_call(kernel, out_shape=[fast(s) if isinstance(s, tuple) else s...  17.6 us
    ppermute x6, starting transfers between devices, send(): lax.ppermute(values, axis, [(i, (i + step) % size) for i in range(size)])  14.8 us
    ppermute x6, waiting for transfers between devices, send(): lax.ppermute(values, axis, [(i, (i + step) % size) for i in range(size)])  5.68 us
  transfers between devices with their start and end apart: 6, of which 1 were waited for; matrix products, arithmetic and copies ran while one was open for 0% of the time, Pallas kernels for 6%

profile of v5, /device:TPU:1, one launch (start us, length us, event | category | flops | bytes accessed | tf_op | source)
XLA Modules:
  0.0 81.0 jit_solution(11662563054557159376)
XLA Ops:
  0.6 0.1 add_convert_fusion.flags
  0.7 2.4 %shard_map.76 = (f32[3,16,32,128]{3,2,1,0:T(8,128)S(1)}, f32[3,16,32,128]{3,2,1,0:T(8,128)S(1)}, f32[16,32,128]{2,1,0:T(8,128)S(1)}, f32[16,32,128]{2,1,0:T(8,12...) custom-call(f32[3,16,32,128]{3,2,1,0:T(8,128)} %disp_in.1, ...), custom_call_target="tpu_custom_call" | custom-call | tf_op jit(solution)/shard_map/pallas_call | solution.py:53
  3.1 3.3 %collective-permute-start.2 = (f32[48,32,128]{2,1,0:T(8,128)S(1)}, f32[48,32,128]{2,1,0:T(8,128)S(1)}, u32[]{:S(2)}, u32[]{:S(2)}) collective-permute-start(f32[48,32,128]{2,1,0:T(8,128)S(1)} %get-tuple-element.52), channel_id=1, source_target_pairs={{0,248},{8,0},{16,8},{24,16},{32,24},{40,32},{48,40},{56,48},{64,5... | collective-permute-start | bytes 2359304 | tf_op jit(solution)/shard_map/ppermute | solution.py:603
  6.4 3.9 %collective-permute-start = (f32[6,16,8,128]{3,2,1,0:T(8,128)S(1)}, f32[6,16,8,128]{3,2,1,0:T(8,128)S(1)}, u32[]{:S(2)}, u32[]{:S(2)}) collective-permute-start(f32[6,16,8,128]{3,2,1,0:T(8,128)S(1)} %get-tuple-element.41), channel_id=1, source_target_pairs={{0,7},{1,0},{2,1},{3,2},{4,3},{5,4},{6,5},{7,6},{8,15},{9,8},{10,9... | collective-permute-start | bytes 1179656 | tf_op jit(solution)/shard_map/ppermute | solution.py:603
  10.3 0.0 collective-permute-start.1
  10.3 1.5 %collective-permute-start.3 = (f32[34,32,128]{2,1,0:T(8,128)S(1)}, f32[34,32,128]{2,1,0:T(8,128)S(1)}, u32[]{:S(2)}, u32[]{:S(2)}) collective-permute-start(f32[34,32,128]{2,1,0:T(8,128)S(1)} %get-tuple-element.53), channel_id=1, source_target_pairs={{0,8},{8,16},{16,24},{24,32},{32,40},{40,48},{48,56},{56,64},{64,7... | collective-permute-start | bytes 1671176 | tf_op jit(solution)/shard_map/ppermute | solution.py:603
  11.7 5.7 %collective-permute-done.1.low = f32[5,16,8,128]{3,2,1,0:T(8,128)S(1)} collective-permute-done((f32[5,16,8,128]{3,2,1,0:T(8,128)S(1)}, f32[5,16,8,128]{3,2,1,0:T(8,128)S(1)}, u32[]{:S(2)}, u32[]{:S(2)}) %collective-permute-start.1) | collective-permute-done | bytes 327712 | tf_op jit(solution)/shard_map/ppermute | solution.py:603
  17.4 0.0 collective-permute-done.high
  17.5 6.2 %collective-permute-start.4 = (f32[72,8,128]{2,1,0:T(8,128)S(1)}, f32[72,8,128]{2,1,0:T(8,128)S(1)}, u32[]{:S(2)}, u32[]{:S(2)}) collective-permute-start(f32[72,8,128]{2,1,0:T(8,128)S(1)} %get-tuple-element.54), channel_id=1, source_target_pairs={{0,248},{8,0},{16,8},{24,16},{32,24},{40,32},{48,40},{56,48},{64,5... | collective-permute-start | bytes 884744 | tf_op jit(solution)/shard_map/ppermute | solution.py:603
  23.6 0.0 collective-permute-start.5
  23.6 4.9 %shard_map.77 = (f32[3,28,48,128]{3,2,1,0:T(8,128)S(1)}, f32[3,16,48,128]{3,2,1,0:T(8,128)S(1)}, f32[28,48,128]{2,1,0:T(8,128)S(1)}, f32[3,28,48,128]{3,2,1,0:T(...) custom-call(f32[3,16,32,128]{3,2,1,0:T(8,128)S(1)} %get-tuple-elemen, ...), custom_call_target="tpu_custom_call" | custom-call | tf_op jit(solution)/shard_map/pallas_call | solution.py:53
  28.5 0.0 collective-permute-done.3.behind
  28.5 0.0 collective-permute-done.5.behind_corner
  28.5 0.0 collective-permute-done.4.ahead_corner
  28.5 0.0 collective-permute-done.2.ahead
  28.5 4.4 %shard_map.79 = (f32[3,28,48,128]{3,2,1,0:T(8,128)S(1)}, f32[28,48,128]{2,1,0:T(8,128)S(1)}, f32[3,28,48,128]{3,2,1,0:T(8,128)S(1)}, f32[3,28,48,128]{3,2,1,0:T(...) custom-call(f32[3,28,48,128]{3,2,1,0:T(8,128)S(1)} %get-tuple-elemen, ...), custom_call_target="tpu_custom_call", output_to_operand_aliasing={{0}: (0, {}), {1}: (2, {}), {2}: (3, {}), {3}: (4, {}), {4}... | custom-call | tf_op jit(solution)/shard_map/pallas_call | solution.py:53
  32.9 23.8 %all_to_all.22 = f32[256,1,128]{2,1,0:T(1,128)S(1)} all-to-all(f32[256,1,128]{2,1,0:T(1,128)S(1)} %bitcast.14), channel_id=1, replica_groups=mesh['gx'=32,'gy'=8] {'gx','gy'}, dimensions={0} | all-to-all | bytes 262144 | tf_op jit(solution)/shard_map/all_to_all | solution.py:615
  56.7 4.9 %shard_map.80 = (f32[3,16,32,128]{3,2,1,0:T(8,128)}, f32[16,32,128]{2,1,0:T(8,128)}, f32[28,40,128]{2,1,0:T(8,128)S(1)}, f32[28,40,128]{2,1,0:T(8,128)S(1)}, f32...) custom-call(f32[256,128]{1,0:T(8,128)S(1)} %bitcast.12, f32[3,28,48,128]{3,2,1,0:T(8,128)S(1)} %get-tuple-element.57.wide, ...), custom_call_target="tpu_custom_call" | custom-call | tf_op jit(solution)/shard_map/pallas_call | solution.py:53
  61.6 18.4 %all_to_all.23 = f32[256,1,128]{2,1,0:T(1,128)S(1)} all-to-all(f32[256,1,128]{2,1,0:T(1,128)S(1)} %bitcast.15), channel_id=1, replica_groups=mesh['gx'=32,'gy'=8] {'gx','gy'}, dimensions={0} | all-to-all | bytes 262144 | tf_op jit(solution)/shard_map/all_to_all | solution.py:615
  80.0 1.0 %shard_map.81 = f32[16,32,128]{2,1,0:T(8,128)} custom-call(f32[256,128]{1,0:T(8,128)S(1)} %bitcast.13, f32[16,32,128]{2,1,0:T(8,128)S(1)} %get-tuple-element.38.damage, f32[28,40,128]{2,1,0:T(8,128)S(1)} %get-tuple-element.65.w0, f32[28,40,128]{2,1,0:T(8,128)S(1)} %get-tuple-element.66.w1, f32[28,40,128]{2,1,0:T(8,128)S(1)} %get-tuple-element.67.w2), custom_call_target="tpu_custom_call" | custom-call | tf_op jit(solution)/shard_map/pallas_call | solution.py:53
  (1 shorter events, 0.0 us)
Async XLA Ops:
  3.1 25.4 %collective-permute-start.2 = (f32[48,32,128]{2,1,0:T(8,128)S(1)}, f32[48,32,128]{2,1,0:T(8,128)S(1)}, u32[]{:S(2)}, u32[]{:S(2)}) collective-permute-start(f32[48,32,128]{2,1,0:T(8,128)S(1)} %get-tuple-element.52), channel_id=1, source_target_pairs={{0,248},{8,0},{16,8},{24,16},{32,24},{40,32},{48,40},{56,48},{64,5... | collective-permute-start | bytes 2359304 | tf_op jit(solution)/shard_map/ppermute | solution.py:603
  6.4 11.0 %collective-permute-start = (f32[6,16,8,128]{3,2,1,0:T(8,128)S(1)}, f32[6,16,8,128]{3,2,1,0:T(8,128)S(1)}, u32[]{:S(2)}, u32[]{:S(2)}) collective-permute-start(f32[6,16,8,128]{3,2,1,0:T(8,128)S(1)} %get-tuple-element.41), channel_id=1, source_target_pairs={{0,7},{1,0},{2,1},{3,2},{4,3},{5,4},{6,5},{7,6},{8,15},{9,8},{10,9... | collective-permute-start | bytes 1179656 | tf_op jit(solution)/shard_map/ppermute | solution.py:603
  10.3 7.1 %collective-permute-start.1 = (f32[5,16,8,128]{3,2,1,0:T(8,128)S(1)}, f32[5,16,8,128]{3,2,1,0:T(8,128)S(1)}, u32[]{:S(2)}, u32[]{:S(2)}) collective-permute-start(f32[5,16,8,128]{3,2,1,0:T(8,128)S(1)} %get-tuple-element.42), channel_id=1, source_target_pairs={{0,1},{1,2},{2,3},{3,4},{4,5},{5,6},{6,7},{7,0},{8,9},{9,10},{10,1... | collective-permute-start | bytes 983048 | tf_op jit(solution)/shard_map/ppermute | solution.py:603
  10.3 18.2 %collective-permute-start.3 = (f32[34,32,128]{2,1,0:T(8,128)S(1)}, f32[34,32,128]{2,1,0:T(8,128)S(1)}, u32[]{:S(2)}, u32[]{:S(2)}) collective-permute-start(f32[34,32,128]{2,1,0:T(8,128)S(1)} %get-tuple-element.53), channel_id=1, source_target_pairs={{0,8},{8,16},{16,24},{24,32},{32,40},{40,48},{48,56},{56,64},{64,7... | collective-permute-start | bytes 1671176 | tf_op jit(solution)/shard_map/ppermute | solution.py:603
  17.5 11.0 %collective-permute-start.4 = (f32[72,8,128]{2,1,0:T(8,128)S(1)}, f32[72,8,128]{2,1,0:T(8,128)S(1)}, u32[]{:S(2)}, u32[]{:S(2)}) collective-permute-start(f32[72,8,128]{2,1,0:T(8,128)S(1)} %get-tuple-element.54), channel_id=1, source_target_pairs={{0,248},{8,0},{16,8},{24,16},{32,24},{40,32},{48,40},{56,48},{64,5... | collective-permute-start | bytes 884744 | tf_op jit(solution)/shard_map/ppermute | solution.py:603
  23.6 4.9 %collective-permute-start.5 = (f32[55,8,128]{2,1,0:T(8,128)S(1)}, f32[55,8,128]{2,1,0:T(8,128)S(1)}, u32[]{:S(2)}, u32[]{:S(2)}) collective-permute-start(f32[55,8,128]{2,1,0:T(8,128)S(1)} %get-tuple-element.55), channel_id=1, source_target_pairs={{0,8},{8,16},{16,24},{24,32},{32,40},{40,48},{48,56},{56,64},{64,7... | collective-permute-start | bytes 675848 | tf_op jit(solution)/shard_map/ppermute | solution.py:603

commit v6 on v5

--- a/solution.py
+++ b/solution.py
@@ -40,7 +40,7 @@
     return jax.ShapeDtypeStruct(shape, f32)
 
 
-def call(kernel, outs, scratch=(), limit=8 << 20, aliases=None, hbm=False):
+def call(kernel, outs, scratch=(), limit=8 << 20, aliases=None, hbm=False, far=0):
     vmem = pl.BlockSpec(memory_space=pltpu.VMEM)
     smem = pl.BlockSpec(memory_space=pltpu.SMEM)
 
@@ -54,7 +54,7 @@
             kernel,
             out_shape=[fast(s) if isinstance(s, tuple) else s for s in outs],
             in_specs=specs,
-            out_specs=[vmem] * len(outs),
+            out_specs=[pl.BlockSpec(memory_space=pltpu.HBM)] * far + [vmem] * (len(outs) - far),
             scratch_shapes=[pltpu.VMEM(s, f32) if isinstance(s, tuple) else s for s in scratch],
             input_output_aliases=aliases or {},
             compiler_params=pltpu.CompilerParams(vmem_limit_bytes=limit),
@@ -146,9 +146,44 @@
 FRONT, BACK = sum(AHEAD), sum(BEHIND)
 
 
-def pack_kernel(
-    disp_in, force_in, damage_in, history_in, crack_in, flags,
-    disp, force, damage, history, crack, first, last, front, back, sem,
+def rows_kernel(
+    disp, force, damage, history, crack, flags,
+    first, last, top, bottom, top_crack, bottom_crack, sem,
+):
+    copies = []
+    for rows, into, into_crack in ((0, top, top_crack), (24, bottom, bottom_crack)):
+        for source, target in (
+            (crack.at[:, rows : rows + 8], into_crack),
+            (history.at[:, rows : rows + 8], into.at[7]),
+            (damage.at[:, rows : rows + 8], into.at[6]),
+            (disp.at[:, :, rows : rows + 8], into.at[0:3]),
+            (force.at[:, :, rows : rows + 8], into.at[3:6]),
+        ):
+            copies.append(pltpu.make_async_copy(source, target, sem.at[len(copies)]))
+    for copy in copies:
+        copy.start()
+    for copy in copies:
+        copy.wait()
+
+    def step(k, carry):
+        for into, flag, out, pack in (
+            (top, top_crack, first, pack_first), (bottom, bottom_crack, last, pack_last)
+        ):
+            past = jnp.maximum(into[7, k], crack_load * flag[k].astype(f32))
+            tiles = pack(
+                [into[j, k] for j in range(3)], [into[3 + j, k] for j in range(3)],
+                into[6, k], past,
+            )
+            for n, tile in enumerate(tiles):
+                out[n, k] = tile
+        return carry
+
+    lax.fori_loop(0, LX, step, 0, unroll=2)
+
+
+def bulk_kernel(
+    disp_in, force_in, damage_in, history_in, crack_in,
+    disp, force, damage, history, crack, front, back, sem,
 ):
     copies = [
         pltpu.make_async_copy(source, target, sem.at[n])
@@ -163,21 +198,9 @@
         copy.start()
     for copy in copies:
         copy.wait()
-
-    def step(k, carry):
-        for rows, out, pack in ((0, first, pack_first), (24, last, pack_last)):
-            at = slice(rows, rows + 8)
-            past = jnp.maximum(history[k, at], crack_load * crack[k, at].astype(f32))
-            tiles = pack(
-                [disp[j, k, at] for j in range(3)], [force[j, k, at] for j in range(3)],
-                damage[k, at], past,
-            )
-            for n, tile in enumerate(tiles):
-                out[n, k] = tile
-        return carry
-
-    lax.fori_loop(0, LX, step, 0, unroll=2)
-    for counts, starts, out, ahead in ((AHEAD, AHEAD_AT, front, True), (BEHIND, BEHIND_AT, back, False)):
+    for counts, starts, out, ahead in (
+        (AHEAD, AHEAD_AT, front, True), (BEHIND, BEHIND_AT, back, False)
+    ):
         for k in range(8):
             size, at = counts[k], starts[k]
             begin = 0 if ahead else LX - size
@@ -215,10 +238,10 @@
         return self.ref[self.starts[key[0] + self.offset] + key[1]]
 
 
-def stress(u, n, gain):
+def stress(u, n, gain, ahead):
     dx = [n[j] - u[j] for j in range(3)]
     dy = [next_row(u[j]) - u[j] for j in range(3)]
-    dz = [next_lane(u[j]) - u[j] for j in range(3)]
+    dz = [ahead[j] - u[j] for j in range(3)]
     twice = gain + gain
     part = 0.75 * (dx[0] + dy[1] + dz[2])
     return (
@@ -246,16 +269,17 @@
 
 def sweep(source, gain, begin, end, diag, store, unroll=None):
     u, n = vector(source, begin), vector(source, begin + 1)
-    s = stress(u, n, gain[begin])
+    s = stress(u, n, gain[begin], [next_lane(x) for x in u])
 
     def step(i, carry):
-        before, u = carry
+        before, u, ahead = carry
         n = vector(source, i + 1)
-        s = stress(u, n, gain[i])
+        s = stress(u, n, gain[i], ahead)
+        ahead = tuple(next_lane(x) for x in n)
         store(i, divergence(u, s, before, diag))
-        return (s[0], s[3], s[4]), n
-
-    carry = ((s[0], s[3], s[4]), n)
+        return (s[0], s[3], s[4]), n, ahead
+
+    carry = ((s[0], s[3], s[4]), n, tuple(next_lane(x) for x in n))
     if unroll is None:
         for i in range(begin + 1, end):
             carry = step(i, carry)
@@ -487,7 +511,7 @@
 
 def damage_kernel(
     gathered, wide, v0, v1, v2, short_damage, past, flags,
-    moved, found, w0, w1, w2, sums, now, drive,
+    moved_out, found_out, w0, w1, w2, sums, now, drive, moved, found, sem,
 ):
     a0, a1, a2 = coefficients(gathered, SHIFT_U)
 
@@ -503,6 +527,8 @@
         return carry
 
     lax.fori_loop(OFF, OFF + LX, middle, 0, unroll=2)
+    moved_copy = pltpu.make_async_copy(moved, moved_out, sem.at[0])
+    moved_copy.start()
     for i in (OFF - 2, OFF - 1, *range(OFF + LX, OFF + LX + 4)):
         for j in range(3):
             current(j, i)
@@ -529,6 +555,8 @@
         return carry
 
     lax.fori_loop(OFF, OFF + LX, step, 0, unroll=4)
+    found_copy = pltpu.make_async_copy(found, found_out, sem.at[1])
+    found_copy.start()
     for i in (OFF - 2, OFF - 1, *range(OFF + LX, OFF + LX + 3)):
         drive[i] = jnp.maximum(past[i], energy(i))
 
@@ -583,6 +611,8 @@
 
     zero = jnp.zeros((8, LZ), f32)
     moments_out(sums, lax.fori_loop(OFF, OFF + LX, add, (zero,) * 6, unroll=4))
+    moved_copy.wait()
+    found_copy.wait()
 
 
 def update_kernel(gathered, damage, w0, w1, w2, out):
@@ -614,13 +644,21 @@
     def gather(sums):
         return lax.all_to_all(sums, axes, 0, 0, tiled=True)
 
-    disp, load, old, history, crack, first, last, front, back = call(
-        pack_kernel,
+    given = (displacement, force, damage, history, crack_flags)
+    edge_rows, edge_flags = (8, LX, 8, LZ), pltpu.VMEM((LX, 8, LZ), jnp.int32)
+    first, last = call(
+        rows_kernel,
+        [(6, LX, 8, LZ), (5, LX, 8, LZ)],
+        [edge_rows, edge_rows, edge_flags, edge_flags, pltpu.SemaphoreType.DMA((10,))],
+        hbm=True,
+    )(*given, flags=flags)
+    disp, load, old, history, crack, front, back = call(
+        bulk_kernel,
         [(3, *FIELD), (3, *FIELD), FIELD, FIELD, fast_as(FIELD, jnp.int32)]
-        + [(6, LX, 8, LZ), (5, LX, 8, LZ), (FRONT, LY, LZ), (BACK, LY, LZ)],
+        + [(FRONT, LY, LZ), (BACK, LY, LZ)],
         [pltpu.SemaphoreType.DMA((5,))],
         hbm=True,
-    )(displacement, force, damage, history, crack_flags, flags=flags)
+    )(*given)
     high = send(first, 0, -1)
     low = send(last, 0, 1)
     ahead = send(front, -1, 0)
@@ -646,7 +684,8 @@
     moved, found, w0, w1, w2, sums = call(
         damage_kernel,
         [whole(3, LX, LY, LZ), whole(LX, LY, LZ), BRIEF, BRIEF, BRIEF, (count, LZ)],
-        [(3, DEPTH, SHORT, LZ), BRIEF],
+        [(3, DEPTH, SHORT, LZ), BRIEF, (3, *FIELD), FIELD, pltpu.SemaphoreType.DMA((2,))],
+        far=2,
     )(gather(sums), wide, v0, v1, v2, short_damage, past, flags=flags)
     (damage_out,) = call(update_kernel, [whole(LX, LY, LZ)])(
         gather(sums), old, w0, w1, w2

time: 81.1 us -> 82.7 us (1.020)
    pallas_call x6 -> x7, Pallas kernels: 17.6 us -> 17.8 us  [run(): pl.pallas_call(kernel, out_shape=[fast(s) if isinstance(s, tuple) else s...]
  transfers between devices with their start and end apart: 6 -> 6, of which waited for: 1 -> 1; matrix products, arithmetic and copies ran while one was open for 0% -> 0% of each run, Pallas kernels for 6% -> 8%
where the time goes in v6:
time: 82.7 us; the launch traced here: 82.5 us
  blocking collectives  42.6 us (52%)
  Pallas kernels  17.8 us (22%)
  starting transfers between devices  14.7 us (18%)
  waiting for transfers between devices  5.76 us (7%)
    all_to_all x2, blocking collectives, gather(): return lax.all_to_all(sums, axes, 0, 0, tiled=True)  42.6 us
    pallas_call x7, Pallas kernels, run(): pl.pallas_call(kernel, out_shape=[fast(s) if isinstance(s, tuple) else s...  17.8 us
    ppermute x6, starting transfers between devices, send(): lax.ppermute(values, axis, [(i, (i + step) % size) for i in range(size)])  14.7 us
    ppermute x6, waiting for transfers between devices, send(): lax.ppermute(values, axis, [(i, (i + step) % size) for i in range(size)])  5.76 us
  transfers between devices with their start and end apart: 6, of which 1 were waited for; matrix products, arithmetic and copies ran while one was open for 0% of the time, Pallas kernels for 8%

profile of v6, /device:TPU:1, one launch (start us, length us, event | category | flops | bytes accessed | tf_op | source)
XLA Modules:
  0.0 82.5 jit_solution(17045979120442962748)
XLA Ops:
  0.6 2.6 %shard_map.76 = (f32[3,16,32,128]{3,2,1,0:T(8,128)S(1)}, f32[3,16,32,128]{3,2,1,0:T(8,128)S(1)}, f32[16,32,128]{2,1,0:T(8,128)S(1)}, f32[16,32,128]{2,1,0:T(8,12...) custom-call(f32[3,16,32,128]{3,2,1,0:T(8,128)} %disp.1, ...), custom_call_target="tpu_custom_call" | custom-call | tf_op jit(solution)/shard_map/pallas_call | solution.py:53
  3.3 0.0 copy-start
  3.3 0.8 copy-done
  4.1 3.2 %collective-permute-start.2 = (f32[48,32,128]{2,1,0:T(8,128)}, f32[48,32,128]{2,1,0:T(8,128)S(1)}, u32[]{:S(2)}, u32[]{:S(2)}) collective-permute-start(f32[48,32,128]{2,1,0:T(8,128)} %get-tuple-element.52), channel_id=1, source_target_pairs={{0,248},{8,0},{16,8},{24,16},{32,24},{40,32},{48,40},{56,48},{64,5... | collective-permute-start | bytes 2359304 | tf_op jit(solution)/shard_map/ppermute | solution.py:633
  7.3 0.0 copy-start.1
  7.3 0.1 add_convert_fusion.flags
  7.3 2.1 %shard_map.77 = (f32[6,16,8,128]{3,2,1,0:T(8,128)S(1)}, f32[5,16,8,128]{3,2,1,0:T(8,128)S(1)}) custom-call(f32[3,16,32,128]{3,2,1,0:T(8,128)} %disp.1, f32[3,16,32,128]{3,2,1,0:T(8,128)} %force.1, f32[16,32,128]{2,1,0:T(8,128)} %damage.1, f32[16,32,128]{2,1,0:T(8,128)} %history.1, s32[16,32,128]{2,1,0:T(8,128)} %crack.1, f32[4]{0:T(128)S(1)} %add_convert_fusion.flags), custom_call_target="tpu_custom_call" | custom-call | tf_op jit(solution)/shard_map/pallas_call | solution.py:53
  9.4 3.9 %collective-permute-start = (f32[6,16,8,128]{3,2,1,0:T(8,128)S(1)}, f32[6,16,8,128]{3,2,1,0:T(8,128)S(1)}, u32[]{:S(2)}, u32[]{:S(2)}) collective-permute-start(f32[6,16,8,128]{3,2,1,0:T(8,128)S(1)} %get-tuple-element.41), channel_id=1, source_target_pairs={{0,7},{1,0},{2,1},{3,2},{4,3},{5,4},{6,5},{7,6},{8,15},{9,8},{10,9... | collective-permute-start | bytes 1179656 | tf_op jit(solution)/shard_map/ppermute | solution.py:633
  13.4 0.0 collective-permute-start.1
  13.4 0.0 copy-done.1
  13.4 1.4 %collective-permute-start.3 = (f32[34,32,128]{2,1,0:T(8,128)S(1)}, f32[34,32,128]{2,1,0:T(8,128)S(1)}, u32[]{:S(2)}, u32[]{:S(2)}) collective-permute-start(f32[34,32,128]{2,1,0:T(8,128)S(1)} %copy-done.1), channel_id=1, source_target_pairs={{0,8},{8,16},{16,24},{24,32},{32,40},{40,48},{48,56},{56,64},{64,7... | collective-permute-start | bytes 1671176 | tf_op jit(solution)/shard_map/ppermute | solution.py:633
  14.8 5.7 %collective-permute-done.1.low = f32[5,16,8,128]{3,2,1,0:T(8,128)S(1)} collective-permute-done((f32[5,16,8,128]{3,2,1,0:T(8,128)S(1)}, f32[5,16,8,128]{3,2,1,0:T(8,128)S(1)}, u32[]{:S(2)}, u32[]{:S(2)}) %collective-permute-start.1) | collective-permute-done | bytes 327712 | tf_op jit(solution)/shard_map/ppermute | solution.py:633
  20.5 0.0 collective-permute-done.high
  20.6 6.2 %collective-permute-start.4 = (f32[72,8,128]{2,1,0:T(8,128)S(1)}, f32[72,8,128]{2,1,0:T(8,128)S(1)}, u32[]{:S(2)}, u32[]{:S(2)}) collective-permute-start(f32[72,8,128]{2,1,0:T(8,128)S(1)} %get-tuple-element.54), channel_id=1, source_target_pairs={{0,248},{8,0},{16,8},{24,16},{32,24},{40,32},{48,40},{56,48},{64,5... | collective-permute-start | bytes 884744 | tf_op jit(solution)/shard_map/ppermute | solution.py:633
  26.7 0.0 collective-permute-start.5
  26.7 4.4 %shard_map.78 = (f32[3,28,48,128]{3,2,1,0:T(8,128)S(1)}, f32[3,16,48,128]{3,2,1,0:T(8,128)S(1)}, f32[28,48,128]{2,1,0:T(8,128)S(1)}, f32[3,28,48,128]{3,2,1,0:T(...) custom-call(f32[3,16,32,128]{3,2,1,0:T(8,128)S(1)} %get-tuple-elemen, ...), custom_call_target="tpu_custom_call" | custom-call | tf_op jit(solution)/shard_map/pallas_call | solution.py:53
  31.1 0.0 collective-permute-done.3.behind
  31.2 0.0 collective-permute-done.5.behind_corner
  31.2 0.0 collective-permute-done.4.ahead_corner
  31.2 0.0 collective-permute-done.2.ahead
  31.2 3.5 %shard_map.80 = (f32[3,28,48,128]{3,2,1,0:T(8,128)S(1)}, f32[28,48,128]{2,1,0:T(8,128)S(1)}, f32[3,28,48,128]{3,2,1,0:T(8,128)S(1)}, f32[3,28,48,128]{3,2,1,0:T(...) custom-call(f32[3,28,48,128]{3,2,1,0:T(8,128)S(1)} %get-tuple-elemen, ...), custom_call_target="tpu_custom_call", output_to_operand_aliasing={{0}: (0, {}), {1}: (2, {}), {2}: (3, {}), {3}: (4, {}), {4}... | custom-call | tf_op jit(solution)/shard_map/pallas_call | solution.py:53
  34.7 24.2 %all_to_all.22 = f32[256,1,128]{2,1,0:T(1,128)S(1)} all-to-all(f32[256,1,128]{2,1,0:T(1,128)S(1)} %bitcast.14), channel_id=1, replica_groups=mesh['gx'=32,'gy'=8] {'gx','gy'}, dimensions={0} | all-to-all | bytes 262144 | tf_op jit(solution)/shard_map/all_to_all | solution.py:645
  58.9 4.1 %shard_map.81 = (f32[3,16,32,128]{3,2,1,0:T(8,128)}, f32[16,32,128]{2,1,0:T(8,128)}, f32[28,40,128]{2,1,0:T(8,128)S(1)}, f32[28,40,128]{2,1,0:T(8,128)S(1)}, f32...) custom-call(f32[256,128]{1,0:T(8,128)S(1)} %bitcast.12, f32[3,28,48,128]{3,2,1,0:T(8,128)S(1)} %get-tuple-element.57.wide, ...), custom_call_target="tpu_custom_call" | custom-call | tf_op jit(solution)/shard_map/pallas_call | solution.py:53
  63.0 18.4 %all_to_all.23 = f32[256,1,128]{2,1,0:T(1,128)S(1)} all-to-all(f32[256,1,128]{2,1,0:T(1,128)S(1)} %bitcast.15), channel_id=1, replica_groups=mesh['gx'=32,'gy'=8] {'gx','gy'}, dimensions={0} | all-to-all | bytes 262144 | tf_op jit(solution)/shard_map/all_to_all | solution.py:645
  81.5 1.0 %shard_map.82 = f32[16,32,128]{2,1,0:T(8,128)} custom-call(f32[256,128]{1,0:T(8,128)S(1)} %bitcast.13, f32[16,32,128]{2,1,0:T(8,128)S(1)} %get-tuple-element.38.damage, f32[28,40,128]{2,1,0:T(8,128)S(1)} %get-tuple-element.65.w0, f32[28,40,128]{2,1,0:T(8,128)S(1)} %get-tuple-element.66.w1, f32[28,40,128]{2,1,0:T(8,128)S(1)} %get-tuple-element.67.w2), custom_call_target="tpu_custom_call" | custom-call | tf_op jit(solution)/shard_map/pallas_call | solution.py:53
  (1 shorter events, 0.0 us)
Async XLA Ops:
  3.3 0.8 copy-start
  4.1 27.1 %collective-permute-start.2 = (f32[48,32,128]{2,1,0:T(8,128)}, f32[48,32,128]{2,1,0:T(8,128)S(1)}, u32[]{:S(2)}, u32[]{:S(2)}) collective-permute-start(f32[48,32,128]{2,1,0:T(8,128)} %get-tuple-element.52), channel_id=1, source_target_pairs={{0,248},{8,0},{16,8},{24,16},{32,24},{40,32},{48,40},{56,48},{64,5... | collective-permute-start | bytes 2359304 | tf_op jit(solution)/shard_map/ppermute | solution.py:633
  7.3 6.1 %copy-start.1 = (f32[34,32,128]{2,1,0:T(8,128)S(1)}, f32[34,32,128]{2,1,0:T(8,128)}, u32[]{:S(2)}) copy-start(f32[34,32,128]{2,1,0:T(8,128)} %copy-done) | copy-start | bytes 1671172
  9.4 11.1 %collective-permute-start = (f32[6,16,8,128]{3,2,1,0:T(8,128)S(1)}, f32[6,16,8,128]{3,2,1,0:T(8,128)S(1)}, u32[]{:S(2)}, u32[]{:S(2)}) collective-permute-start(f32[6,16,8,128]{3,2,1,0:T(8,128)S(1)} %get-tuple-element.41), channel_id=1, source_target_pairs={{0,7},{1,0},{2,1},{3,2},{4,3},{5,4},{6,5},{7,6},{8,15},{9,8},{10,9... | collective-permute-start | bytes 1179656 | tf_op jit(solution)/shard_map/ppermute | solution.py:633
  13.4 7.1 %collective-permute-start.1 = (f32[5,16,8,128]{3,2,1,0:T(8,128)S(1)}, f32[5,16,8,128]{3,2,1,0:T(8,128)S(1)}, u32[]{:S(2)}, u32[]{:S(2)}) collective-permute-start(f32[5,16,8,128]{3,2,1,0:T(8,128)S(1)} %get-tuple-element.42), channel_id=1, source_target_pairs={{0,1},{1,2},{2,3},{3,4},{4,5},{5,6},{6,7},{7,0},{8,9},{9,10},{10,1... | collective-permute-start | bytes 983048 | tf_op jit(solution)/shard_map/ppermute | solution.py:633
  13.4 17.7 %collective-permute-start.3 = (f32[34,32,128]{2,1,0:T(8,128)S(1)}, f32[34,32,128]{2,1,0:T(8,128)S(1)}, u32[]{:S(2)}, u32[]{:S(2)}) collective-permute-start(f32[34,32,128]{2,1,0:T(8,128)S(1)} %copy-done.1), channel_id=1, source_target_pairs={{0,8},{8,16},{16,24},{24,32},{32,40},{40,48},{48,56},{56,64},{64,7... | collective-permute-start | bytes 1671176 | tf_op jit(solution)/shard_map/ppermute | solution.py:633
  20.6 10.6 %collective-permute-start.4 = (f32[72,8,128]{2,1,0:T(8,128)S(1)}, f32[72,8,128]{2,1,0:T(8,128)S(1)}, u32[]{:S(2)}, u32[]{:S(2)}) collective-permute-start(f32[72,8,128]{2,1,0:T(8,128)S(1)} %get-tuple-element.54), channel_id=1, source_target_pairs={{0,248},{8,0},{16,8},{24,16},{32,24},{40,32},{48,40},{56,48},{64,5... | collective-permute-start | bytes 884744 | tf_op jit(solution)/shard_map/ppermute | solution.py:633
  26.7 4.4 %collective-permute-start.5 = (f32[55,8,128]{2,1,0:T(8,128)S(1)}, f32[55,8,128]{2,1,0:T(8,128)S(1)}, u32[]{:S(2)}, u32[]{:S(2)}) collective-permute-start(f32[55,8,128]{2,1,0:T(8,128)S(1)} %get-tuple-element.55), channel_id=1, source_target_pairs={{0,8},{8,16},{16,24},{24,32},{32,40},{40,48},{48,56},{56,64},{64,7... | collective-permute-start | bytes 675848 | tf_op jit(solution)/shard_map/ppermute | solution.py:633

commit v7 on v6

--- a/solution.py
+++ b/solution.py
@@ -94,40 +94,63 @@
 
 def pack_first(u, load, damage, past):
     row = tile_row()
-    tiles = [jnp.where(row == 7, roll(past, 7 - j, 0), u[j]) for j in range(3)]
-    return tiles + [jnp.where(row < 6, load[j], roll(damage, 6 - 2 * j, 0)) for j in range(3)]
+    return [
+        jnp.where(row < 6, u[0], roll(damage, 6, 0)),
+        jnp.where(row < 6, u[1], roll(damage, 4, 0)),
+        jnp.where(row < 6, u[2], roll(past, 6, 0)),
+        jnp.where(row < 5, load[0], roll(load[2], 5, 0)),
+        jnp.where(
+            row < 5, load[1], jnp.where(row == 5, roll(damage, 1, 0), roll(load[2], 3, 0))
+        ),
+    ]
 
 
 def pack_last(u, load, damage, past):
     row = tile_row()
     return [
-        jnp.where(row < 3, roll(damage, -1, 0), u[0]),
-        jnp.where(row < 3, roll(past, 2, 0), u[1]),
-        u[2],
-        jnp.where(row < 4, roll(load[1], 4, 0), load[0]),
-        jnp.where(row < 4, roll(damage, 4, 0), load[2]),
+        jnp.where(row < 2, roll(damage, -2, 0), u[0]),
+        jnp.where(row < 2, roll(damage, -4, 0), u[1]),
+        jnp.where(row < 2, roll(damage, -6, 0), u[2]),
+        jnp.where(row < 3, roll(load[2], -3, 0), load[0]),
+        jnp.where(
+            row < 3, jnp.where(row == 2, roll(past, -3, 0), roll(load[2], -6, 0)), load[1]
+        ),
     ]
 
 
+def high_tile(high, field, k):
+    if field < 5:
+        return high[field, k]
+    return jnp.where(tile_row() < 3, roll(high[3, k], 3, 0), roll(high[4, k], 5, 0))
+
+
 def low_tile(low, field, k):
-    if field < 4:
+    if field < 5:
         return low[field, k]
-    return roll(low[3, k], 4, 0) if field == 4 else low[4, k]
+    return jnp.where(tile_row() < 6, roll(low[3, k], 3, 0), roll(low[4, k], 6, 0))
 
 
 def damage_tiles(high, low, k):
     row = tile_row()
-    above = jnp.where(row < 2, roll(high[3, k], 2, 0), roll(high[4, k], 4, 0))
-    above = jnp.where(row < 4, above, roll(high[5, k], 6, 0))
-    below = jnp.where(row < 4, roll(low[0, k], 1, 0), roll(low[4, k], 4, 0))
+    above = jnp.where(row < 2, roll(high[0, k], 2, 0), roll(high[1, k], 4, 0))
+    above = jnp.where(row < 4, above, roll(high[4, k], -1, 0))
+    below = jnp.where(row < 4, roll(low[0, k], 2, 0), roll(low[1, k], 4, 0))
+    below = jnp.where(row < 6, below, roll(low[2, k], 6, 0))
     return above, below
 
 
-def past_tile(high, low, k):
+def past_tile(high, low, k, shared, place):
     row = tile_row()
-    above = jnp.where(row < 1, roll(high[0, k], 1, 0), roll(high[1, k], 2, 0))
-    above = jnp.where(row < 2, above, roll(high[2, k], 3, 0))
-    return jnp.where(row < 4, above, roll(low[1, k], -2, 0))
+    below = jnp.where(row < 6, roll(low[4, k], 3, 0), roll(shared, 6 - 2 * place, 0))
+    return jnp.where(row < 4, roll(high[2, k], 2, 0), below)
+
+
+class Tiles:
+    def __init__(self, ref, starts):
+        self.ref, self.starts = ref, starts
+
+    def __getitem__(self, key):
+        return self.ref[self.starts[key[0]] + key[1]]
 
 
 def brief(above, below):
@@ -165,20 +188,29 @@
     for copy in copies:
         copy.wait()
 
-    def step(k, carry):
-        for into, flag, out, pack in (
-            (top, top_crack, first, pack_first), (bottom, bottom_crack, last, pack_last)
-        ):
-            past = jnp.maximum(into[7, k], crack_load * flag[k].astype(f32))
-            tiles = pack(
-                [into[j, k] for j in range(3)], [into[3 + j, k] for j in range(3)],
-                into[6, k], past,
-            )
-            for n, tile in enumerate(tiles):
-                out[n, k] = tile
+    row = tile_row()
+
+    def step(group, carry):
+        shared = jnp.zeros((8, LZ), f32)
+        for place in range(4):
+            k = 4 * group + place
+            for into, flag, out, pack in (
+                (top, top_crack, first, pack_first), (bottom, bottom_crack, last, pack_last)
+            ):
+                past = jnp.maximum(into[7, k], crack_load * flag[k].astype(f32))
+                tiles = pack(
+                    [into[j, k] for j in range(3)], [into[3 + j, k] for j in range(3)],
+                    into[6, k], past,
+                )
+                for n, tile in enumerate(tiles):
+                    out[n * LX + k] = tile
+                if out is last:
+                    here = (row >= 2 * place) & (row < 2 * place + 2)
+                    shared = jnp.where(here, roll(past, 2 * place + 2, 0), shared)
+        last[5 * LX + group] = shared
         return carry
 
-    lax.fori_loop(0, LX, step, 0, unroll=2)
+    lax.fori_loop(0, 4, step, 0)
 
 
 def bulk_kernel(
@@ -213,29 +245,23 @@
                 out[at : at + size] = field[layers]
 
 
-FRONT_TILES = (7, 7, 7, 6, 6, 6, 7, 7, 7, 6, 6)
-BACK_TILES = (5,) * 11
+FRONT_TILES = (7, 7, 7, 6, 6, 7, 7, 7, 6, 6, 1)
+BACK_TILES = (5,) * 10 + (1,)
 FRONT_TILES_AT = tuple(sum(FRONT_TILES[:k]) for k in range(11))
 BACK_TILES_AT = tuple(sum(BACK_TILES[:k]) for k in range(11))
+ROW_TILES_AT = tuple(LX * k for k in range(6))
 
 
 def corner_kernel(high, low, front, back):
     for counts, starts, out, ahead in (
         (FRONT_TILES, FRONT_TILES_AT, front, True), (BACK_TILES, BACK_TILES_AT, back, False)
     ):
-        for k in range(11):
+        for k in range(10):
             size, at = counts[k], starts[k]
-            begin = 0 if ahead else LX - size
-            source = high.at[k] if k < 6 else low.at[k - 6]
+            begin = LX * (k % 5) + (0 if ahead else LX - size)
+            source = high if k < 5 else low
             out[at : at + size] = source[begin : begin + size]
-
-
-class Corner:
-    def __init__(self, ref, starts, offset):
-        self.ref, self.starts, self.offset = ref, starts, offset
-
-    def __getitem__(self, key):
-        return self.ref[self.starts[key[0] + self.offset] + key[1]]
+        out[starts[10]] = low[5 * LX + (0 if ahead else 3)]
 
 
 def stress(u, n, gain, ahead):
@@ -348,30 +374,34 @@
 ):
     mask = row_mask(flags)
 
-    def assemble(k, carry):
-        i = OFF + k
-        for j in range(3):
-            wide[j, i, 0:LY] = disp[j, k]
-            wide[j, i, LY : LY + 8] = high[j, k] * flags[3]
-            wide[j, i, LY + 8 : ROWS] = low_tile(low, j, k) * flags[2]
-            load[j, k, 0:LY] = force[j, k]
-            load[j, k, LY : LY + 8] = high[3 + j, k]
-            load[j, k, LY + 8 : ROWS] = low_tile(low, 3 + j, k)
-        own = damage[k]
-        above, below = damage_tiles(high, low, k)
-        short_damage[i, 0:LY] = own
-        short_damage[i, LY:SHORT] = brief(above * flags[3], below * flags[2])
-        left = 1.0 - own
-        gain[i, 0:LY] = left * left + stiff_floor
-        left = 1.0 - above
-        gain[i, LY : LY + 8] = (left * left + stiff_floor) * mask[0:8]
-        left = 1.0 - below
-        gain[i, LY + 8 : ROWS] = (left * left + stiff_floor) * mask[8:16]
-        past[i, 0:LY] = jnp.maximum(history[k], crack_load * crack[k].astype(f32))
-        past[i, LY:SHORT] = past_tile(high, low, k)
+    high, low = Tiles(high, ROW_TILES_AT), Tiles(low, ROW_TILES_AT)
+
+    def assemble(group, carry):
+        for place in range(4):
+            k = 4 * group + place
+            i = OFF + k
+            for j in range(3):
+                wide[j, i, 0:LY] = disp[j, k]
+                wide[j, i, LY : LY + 8] = high[j, k] * flags[3]
+                wide[j, i, LY + 8 : ROWS] = low[j, k] * flags[2]
+                load[j, k, 0:LY] = force[j, k]
+                load[j, k, LY : LY + 8] = high_tile(high, 3 + j, k)
+                load[j, k, LY + 8 : ROWS] = low_tile(low, 3 + j, k)
+            own = damage[k]
+            above, below = damage_tiles(high, low, k)
+            short_damage[i, 0:LY] = own
+            short_damage[i, LY:SHORT] = brief(above * flags[3], below * flags[2])
+            left = 1.0 - own
+            gain[i, 0:LY] = left * left + stiff_floor
+            left = 1.0 - above
+            gain[i, LY : LY + 8] = (left * left + stiff_floor) * mask[0:8]
+            left = 1.0 - below
+            gain[i, LY + 8 : ROWS] = (left * left + stiff_floor) * mask[8:16]
+            past[i, 0:LY] = jnp.maximum(history[k], crack_load * crack[k].astype(f32))
+            past[i, LY:SHORT] = past_tile(high, low, k, low[5, group], place)
         return carry
 
-    lax.fori_loop(0, LX, assemble, 0, unroll=2)
+    lax.fori_loop(0, 4, assemble, 0)
     diag = spring_term - SHIFT_U
     first = store_to(v0, mask, load=lambda j, i: load[j, i - OFF])
     sweep(wide, gain, OFF, OFF + 15, spring_term, first, unroll=UNROLL)
@@ -398,7 +428,7 @@
         (AHEAD, AHEAD_AT, True, ahead, ahead_corner, FRONT_TILES_AT, flags[1]),
         (BEHIND, BEHIND_AT, False, behind, behind_corner, BACK_TILES_AT, flags[0]),
     ):
-        above, below = Corner(corner, tiles, 0), Corner(corner, tiles, 6)
+        above, below = Tiles(corner, tiles[:5]), Tiles(corner, tiles[5:])
         for k in range(8):
             for c in range(counts[k]):
                 own = middle[starts[k] + c]
@@ -406,10 +436,10 @@
                 layer = c if high_side else 5 - counts[k] + c
                 if k == 7:
                     past[i, 0:LY] = own
-                    past[i, LY:SHORT] = past_tile(above, below, layer)
+                    past[i, LY:SHORT] = past_tile(above, below, layer, below[5, 0], (layer if high_side else layer + 3) % 4)
                     continue
                 if k < 6:
-                    high, low = above[k, layer], low_tile(below, k, layer)
+                    high, low = high_tile(above, k, layer), low_tile(below, k, layer)
                 else:
                     high, low = damage_tiles(above, below, layer)
                 if k < 3:
@@ -592,14 +622,14 @@
     lane = lanes((LY, LZ))
     row = lax.broadcasted_iota(jnp.int32, (LY, LZ), 0)
     edge = jnp.where(lane == 0, length_term, 0.0)
-    edge = edge + jnp.where(row == 0, length_term * (1.0 - flags[2]), 0.0)
+    edge = edge + jnp.where(row == LY - 1, length_term * (1.0 - flags[3]), 0.0)
     edge = edge + (tough_ratio - SHIFT_D)
 
     def add(i, acc):
         wide_now = w2[i]
         u = wide_now[0:LY]
         dx = w2[i + 1, 0:LY] - u
-        dy = next_row(wide_now)[0:LY] - u
+        dy = last_row(wide_now)[0:LY] - u
         dz = next_lane(u) - u
         side = jnp.where(i == OFF, length_term * (1.0 - flags[0]), 0.0)
         square = u * u
@@ -648,7 +678,7 @@
     edge_rows, edge_flags = (8, LX, 8, LZ), pltpu.VMEM((LX, 8, LZ), jnp.int32)
     first, last = call(
         rows_kernel,
-        [(6, LX, 8, LZ), (5, LX, 8, LZ)],
+        [(5 * LX, 8, LZ), (5 * LX + 4, 8, LZ)],
         [edge_rows, edge_rows, edge_flags, edge_flags, pltpu.SemaphoreType.DMA((10,))],
         hbm=True,
     )(*given, flags=flags)
@@ -663,9 +693,7 @@
     low = send(last, 0, 1)
     ahead = send(front, -1, 0)
     behind = send(back, 1, 0)
-    corners = call(
-        corner_kernel, [(sum(FRONT_TILES), 8, LZ), (sum(BACK_TILES), 8, LZ)]
-    )(high, low)
+    corners = call(corner_kernel, [(sum(FRONT_TILES), 8, LZ), (sum(BACK_TILES), 8, LZ)])(high, low)
     ahead_corner = send(corners[0], -1, 0)
     behind_corner = send(corners[1], 1, 0)
     wide, load, gain, v0, v1, v2, short_damage, past, partial = call(
@@ -687,9 +715,7 @@
         [(3, DEPTH, SHORT, LZ), BRIEF, (3, *FIELD), FIELD, pltpu.SemaphoreType.DMA((2,))],
         far=2,
     )(gather(sums), wide, v0, v1, v2, short_damage, past, flags=flags)
-    (damage_out,) = call(update_kernel, [whole(LX, LY, LZ)])(
-        gather(sums), old, w0, w1, w2
-    )
+    (damage_out,) = call(update_kernel, [whole(LX, LY, LZ)])(gather(sums), old, w0, w1, w2)
     return moved, damage_out, found
 
 

time: 82.7 us -> 81.9 us (level)
  waiting for transfers between devices: 5.76 us -> 3.18 us
  blocking collectives: 42.6 us -> 45 us
    ppermute x6, waiting for transfers between devices: 5.76 us -> 3.18 us  [send(): lax.ppermute(values, axis, [(i, (i + step) % size) for i in range(size)])]
    all_to_all x2, blocking collectives: 42.6 us -> 45 us  [gather(): return lax.all_to_all(sums, axes, 0, 0, tiled=True)]
  transfers between devices with their start and end apart: 6 -> 6, of which waited for: 1 -> 2; matrix products, arithmetic and copies ran while one was open for 0% -> 0% of each run, Pallas kernels for 8% -> 8%
where the time goes in v7:
time: 81.9 us; the launch traced here: 81.7 us
  blocking collectives  45 us (55%)
  Pallas kernels  17.7 us (22%)
  starting transfers between devices  14.2 us (17%)
  waiting for transfers between devices  3.18 us (4%)
    all_to_all x2, blocking collectives, gather(): return lax.all_to_all(sums, axes, 0, 0, tiled=True)  45 us
    pallas_call x7, Pallas kernels, run(): pl.pallas_call(kernel, out_shape=[fast(s) if isinstance(s, tuple) else s...  17.7 us
    ppermute x6, starting transfers between devices, send(): lax.ppermute(values, axis, [(i, (i + step) % size) for i in range(size)])  14.2 us
    ppermute x6, waiting for transfers between devices, send(): lax.ppermute(values, axis, [(i, (i + step) % size) for i in range(size)])  3.18 us
  transfers between devices with their start and end apart: 6, of which 2 were waited for; matrix products, arithmetic and copies ran while one was open for 0% of the time, Pallas kernels for 8%

profile of v7, /device:TPU:1, one launch (start us, length us, event | category | flops | bytes accessed | tf_op | source)
XLA Modules:
  0.0 81.7 jit_solution(15223089108023328681)
XLA Ops:
  0.6 2.6 %shard_map.76 = (f32[3,16,32,128]{3,2,1,0:T(8,128)S(1)}, f32[3,16,32,128]{3,2,1,0:T(8,128)S(1)}, f32[16,32,128]{2,1,0:T(8,128)S(1)}, f32[16,32,128]{2,1,0:T(8,12...) custom-call(f32[3,16,32,128]{3,2,1,0:T(8,128)} %disp.1, ...), custom_call_target="tpu_custom_call" | custom-call | tf_op jit(solution)/shard_map/pallas_call | solution.py:53
  3.3 0.0 copy-start
  3.3 0.8 copy-done
  4.1 3.2 %collective-permute-start.2 = (f32[48,32,128]{2,1,0:T(8,128)}, f32[48,32,128]{2,1,0:T(8,128)S(1)}, u32[]{:S(2)}, u32[]{:S(2)}) collective-permute-start(f32[48,32,128]{2,1,0:T(8,128)} %get-tuple-element.52), channel_id=1, source_target_pairs={{0,248},{8,0},{16,8},{24,16},{32,24},{40,32},{48,40},{56,48},{64,5... | collective-permute-start | bytes 2359304 | tf_op jit(solution)/shard_map/ppermute | solution.py:663
  7.3 0.0 copy-start.1
  7.3 0.1 add_convert_fusion.flags
  7.3 2.1 %shard_map.77 = (f32[80,8,128]{2,1,0:T(8,128)S(1)}, f32[84,8,128]{2,1,0:T(8,128)S(1)}) custom-call(f32[3,16,32,128]{3,2,1,0:T(8,128)} %disp.1, f32[3,16,32,128]{3,2,1,0:T(8,128)} %force.1, f32[16,32,128]{2,1,0:T(8,128)} %damage.1, f32[16,32,128]{2,1,0:T(8,128)} %history.1, s32[16,32,128]{2,1,0:T(8,128)} %crack.1, f32[4]{0:T(128)S(1)} %add_convert_fusion.flags), custom_call_target="tpu_custom_call" | custom-call | tf_op jit(solution)/shard_map/pallas_call | solution.py:53
  9.4 0.1 collective-permute-start.1
  9.5 3.9 %collective-permute-start = (f32[80,8,128]{2,1,0:T(8,128)S(1)}, f32[80,8,128]{2,1,0:T(8,128)S(1)}, u32[]{:S(2)}, u32[]{:S(2)}) collective-permute-start(f32[80,8,128]{2,1,0:T(8,128)S(1)} %get-tuple-element.41), channel_id=1, source_target_pairs={{0,7},{1,0},{2,1},{3,2},{4,3},{5,4},{6,5},{7,6},{8,15},{9,8},{10,9... | collective-permute-start | bytes 983048 | tf_op jit(solution)/shard_map/ppermute | solution.py:663
  13.5 0.0 copy-done.1
  13.5 1.4 %collective-permute-start.3 = (f32[34,32,128]{2,1,0:T(8,128)S(1)}, f32[34,32,128]{2,1,0:T(8,128)S(1)}, u32[]{:S(2)}, u32[]{:S(2)}) collective-permute-start(f32[34,32,128]{2,1,0:T(8,128)S(1)} %copy-done.1), channel_id=1, source_target_pairs={{0,8},{8,16},{16,24},{24,32},{32,40},{40,48},{48,56},{56,64},{64,7... | collective-permute-start | bytes 1671176 | tf_op jit(solution)/shard_map/ppermute | solution.py:663
  14.8 2.6 %collective-permute-done.high = f32[80,8,128]{2,1,0:T(8,128)S(1)} collective-permute-done((f32[80,8,128]{2,1,0:T(8,128)S(1)}, f32[80,8,128]{2,1,0:T(8,128)S(1)}, u32[]{:S(2)}, u32[]{:S(2)}) %collective-permute-start) | collective-permute-done | bytes 327712 | tf_op jit(solution)/shard_map/ppermute | solution.py:663
  17.5 0.5 collective-permute-done.1.low
  18.0 5.6 %collective-permute-start.4 = (f32[67,8,128]{2,1,0:T(8,128)S(1)}, f32[67,8,128]{2,1,0:T(8,128)S(1)}, u32[]{:S(2)}, u32[]{:S(2)}) collective-permute-start(f32[67,8,128]{2,1,0:T(8,128)S(1)} %get-tuple-element.54), channel_id=1, source_target_pairs={{0,248},{8,0},{16,8},{24,16},{32,24},{40,32},{48,40},{56,48},{64,5... | collective-permute-start | bytes 823304 | tf_op jit(solution)/shard_map/ppermute | solution.py:663
  23.6 0.0 collective-permute-start.5
  23.7 4.4 %shard_map.78 = (f32[3,28,48,128]{3,2,1,0:T(8,128)S(1)}, f32[3,16,48,128]{3,2,1,0:T(8,128)S(1)}, f32[28,48,128]{2,1,0:T(8,128)S(1)}, f32[3,28,48,128]{3,2,1,0:T(...) custom-call(f32[3,16,32,128]{3,2,1,0:T(8,128)S(1)} %get-tuple-elemen, ...), custom_call_target="tpu_custom_call" | custom-call | tf_op jit(solution)/shard_map/pallas_call | solution.py:53
  28.1 0.0 collective-permute-done.5.behind_corner
  28.1 0.0 collective-permute-done.3.behind
  28.1 0.0 collective-permute-done.4.ahead_corner
  28.1 0.0 collective-permute-done.2.ahead
  28.1 3.5 %shard_map.80 = (f32[3,28,48,128]{3,2,1,0:T(8,128)S(1)}, f32[28,48,128]{2,1,0:T(8,128)S(1)}, f32[3,28,48,128]{3,2,1,0:T(8,128)S(1)}, f32[3,28,48,128]{3,2,1,0:T(...) custom-call(f32[3,28,48,128]{3,2,1,0:T(8,128)S(1)} %get-tuple-elemen, ...), custom_call_target="tpu_custom_call", output_to_operand_aliasing={{0}: (0, {}), {1}: (2, {}), {2}: (3, {}), {3}: (4, {}), {4}... | custom-call | tf_op jit(solution)/shard_map/pallas_call | solution.py:53
  31.6 26.5 %all_to_all.22 = f32[256,1,128]{2,1,0:T(1,128)S(1)} all-to-all(f32[256,1,128]{2,1,0:T(1,128)S(1)} %bitcast.14), channel_id=1, replica_groups=mesh['gx'=32,'gy'=8] {'gx','gy'}, dimensions={0} | all-to-all | bytes 262144 | tf_op jit(solution)/shard_map/all_to_all | solution.py:675
  58.2 4.1 %shard_map.81 = (f32[3,16,32,128]{3,2,1,0:T(8,128)}, f32[16,32,128]{2,1,0:T(8,128)}, f32[28,40,128]{2,1,0:T(8,128)S(1)}, f32[28,40,128]{2,1,0:T(8,128)S(1)}, f32...) custom-call(f32[256,128]{1,0:T(8,128)S(1)} %bitcast.12, f32[3,28,48,128]{3,2,1,0:T(8,128)S(1)} %get-tuple-element.57.wide, ...), custom_call_target="tpu_custom_call" | custom-call | tf_op jit(solution)/shard_map/pallas_call | solution.py:53
  62.3 18.4 %all_to_all.23 = f32[256,1,128]{2,1,0:T(1,128)S(1)} all-to-all(f32[256,1,128]{2,1,0:T(1,128)S(1)} %bitcast.15), channel_id=1, replica_groups=mesh['gx'=32,'gy'=8] {'gx','gy'}, dimensions={0} | all-to-all | bytes 262144 | tf_op jit(solution)/shard_map/all_to_all | solution.py:675
  80.7 1.0 %shard_map.82 = f32[16,32,128]{2,1,0:T(8,128)} custom-call(f32[256,128]{1,0:T(8,128)S(1)} %bitcast.13, f32[16,32,128]{2,1,0:T(8,128)S(1)} %get-tuple-element.38.damage, f32[28,40,128]{2,1,0:T(8,128)S(1)} %get-tuple-element.65.w0, f32[28,40,128]{2,1,0:T(8,128)S(1)} %get-tuple-element.66.w1, f32[28,40,128]{2,1,0:T(8,128)S(1)} %get-tuple-element.67.w2), custom_call_target="tpu_custom_call" | custom-call | tf_op jit(solution)/shard_map/pallas_call | solution.py:53
  (1 shorter events, 0.0 us)
Async XLA Ops:
  3.3 0.8 copy-start
  4.1 24.1 %collective-permute-start.2 = (f32[48,32,128]{2,1,0:T(8,128)}, f32[48,32,128]{2,1,0:T(8,128)S(1)}, u32[]{:S(2)}, u32[]{:S(2)}) collective-permute-start(f32[48,32,128]{2,1,0:T(8,128)} %get-tuple-element.52), channel_id=1, source_target_pairs={{0,248},{8,0},{16,8},{24,16},{32,24},{40,32},{48,40},{56,48},{64,5... | collective-permute-start | bytes 2359304 | tf_op jit(solution)/shard_map/ppermute | solution.py:663
  7.3 6.2 %copy-start.1 = (f32[34,32,128]{2,1,0:T(8,128)S(1)}, f32[34,32,128]{2,1,0:T(8,128)}, u32[]{:S(2)}) copy-start(f32[34,32,128]{2,1,0:T(8,128)} %copy-done) | copy-start | bytes 1671172
  9.4 8.6 %collective-permute-start.1 = (f32[84,8,128]{2,1,0:T(8,128)S(1)}, f32[84,8,128]{2,1,0:T(8,128)S(1)}, u32[]{:S(2)}, u32[]{:S(2)}) collective-permute-start(f32[84,8,128]{2,1,0:T(8,128)S(1)} %get-tuple-element.42), channel_id=1, source_target_pairs={{0,1},{1,2},{2,3},{3,4},{4,5},{5,6},{6,7},{7,0},{8,9},{9,10},{10,1... | collective-permute-start | bytes 1032200 | tf_op jit(solution)/shard_map/ppermute | solution.py:663
  9.5 8.0 %collective-permute-start = (f32[80,8,128]{2,1,0:T(8,128)S(1)}, f32[80,8,128]{2,1,0:T(8,128)S(1)}, u32[]{:S(2)}, u32[]{:S(2)}) collective-permute-start(f32[80,8,128]{2,1,0:T(8,128)S(1)} %get-tuple-element.41), channel_id=1, source_target_pairs={{0,7},{1,0},{2,1},{3,2},{4,3},{5,4},{6,5},{7,6},{8,15},{9,8},{10,9... | collective-permute-start | bytes 983048 | tf_op jit(solution)/shard_map/ppermute | solution.py:663
  13.5 14.6 %collective-permute-start.3 = (f32[34,32,128]{2,1,0:T(8,128)S(1)}, f32[34,32,128]{2,1,0:T(8,128)S(1)}, u32[]{:S(2)}, u32[]{:S(2)}) collective-permute-start(f32[34,32,128]{2,1,0:T(8,128)S(1)} %copy-done.1), channel_id=1, source_target_pairs={{0,8},{8,16},{16,24},{24,32},{32,40},{40,48},{48,56},{56,64},{64,7... | collective-permute-start | bytes 1671176 | tf_op jit(solution)/shard_map/ppermute | solution.py:663
  18.0 10.1 %collective-permute-start.4 = (f32[67,8,128]{2,1,0:T(8,128)S(1)}, f32[67,8,128]{2,1,0:T(8,128)S(1)}, u32[]{:S(2)}, u32[]{:S(2)}) collective-permute-start(f32[67,8,128]{2,1,0:T(8,128)S(1)} %get-tuple-element.54), channel_id=1, source_target_pairs={{0,248},{8,0},{16,8},{24,16},{32,24},{40,32},{48,40},{56,48},{64,5... | collective-permute-start | bytes 823304 | tf_op jit(solution)/shard_map/ppermute | solution.py:663
  23.6 4.4 %collective-permute-start.5 = (f32[51,8,128]{2,1,0:T(8,128)S(1)}, f32[51,8,128]{2,1,0:T(8,128)S(1)}, u32[]{:S(2)}, u32[]{:S(2)}) collective-permute-start(f32[51,8,128]{2,1,0:T(8,128)S(1)} %get-tuple-element.55), channel_id=1, source_target_pairs={{0,8},{8,16},{16,24},{24,32},{32,40},{40,48},{48,56},{56,64},{64,7... | collective-permute-start | bytes 626696 | tf_op jit(solution)/shard_map/ppermute | solution.py:663

commit v8 on v7

--- a/solution.py
+++ b/solution.py
@@ -17,7 +17,7 @@
 bulk_half = 0.5 * (1.5 + 2.0 / 3.0)
 
 LX, LY, LZ = 16, 32, 128
-ROWS, SHORT, DEPTH, OFF = 48, 40, 28, 5
+ROWS, SHORT, DEPTH, OFF = 48, 40, 28, 6
 
 SHIFT_U = 14.0
 SHIFT_D = 18.0
@@ -162,8 +162,8 @@
     return jnp.where(row < 8, flags[3], flags[2])
 
 
-AHEAD = (7, 7, 7, 6, 6, 6, 6, 3)
-BEHIND = (5, 5, 5, 4, 4, 4, 5, 2)
+AHEAD = (6, 6, 6, 5, 5, 5, 5, 2)
+BEHIND = (6, 6, 6, 5, 5, 5, 6, 3)
 AHEAD_AT = tuple(sum(AHEAD[:k]) for k in range(8))
 BEHIND_AT = tuple(sum(BEHIND[:k]) for k in range(8))
 FRONT, BACK = sum(AHEAD), sum(BEHIND)
@@ -245,8 +245,8 @@
                 out[at : at + size] = field[layers]
 
 
-FRONT_TILES = (7, 7, 7, 6, 6, 7, 7, 7, 6, 6, 1)
-BACK_TILES = (5,) * 10 + (1,)
+FRONT_TILES = (6, 6, 6, 5, 5, 6, 6, 6, 5, 5, 1)
+BACK_TILES = (6,) * 10 + (1,)
 FRONT_TILES_AT = tuple(sum(FRONT_TILES[:k]) for k in range(11))
 BACK_TILES_AT = tuple(sum(BACK_TILES[:k]) for k in range(11))
 ROW_TILES_AT = tuple(LX * k for k in range(6))
@@ -433,10 +433,10 @@
             for c in range(counts[k]):
                 own = middle[starts[k] + c]
                 i = OFF + LX + c if high_side else OFF - counts[k] + c
-                layer = c if high_side else 5 - counts[k] + c
+                layer = c if high_side else 6 - counts[k] + c
                 if k == 7:
                     past[i, 0:LY] = own
-                    past[i, LY:SHORT] = past_tile(above, below, layer, below[5, 0], (layer if high_side else layer + 3) % 4)
+                    past[i, LY:SHORT] = past_tile(above, below, layer, below[5, 0], (layer if high_side else layer + 2) % 4)
                     continue
                 if k < 6:
                     high, low = high_tile(above, k, layer), low_tile(below, k, layer)
@@ -448,7 +448,7 @@
                     high = high * (flag * flags[3])
                     low = low * (flag * flags[2])
                 elif k < 6:
-                    into = edge_load.at[k - 3, i - OFF - LX + 4 if high_side else i - 1]
+                    into = edge_load.at[k - 3, i - OFF - LX + 5 if high_side else i - 1]
                 else:
                     into = gain.at[i]
                     short_damage[i, 0:LY] = own * flag
@@ -469,7 +469,7 @@
         if i < OFF:
             return edge_load[j, i - 1]
         if i >= OFF + LX:
-            return edge_load[j, i - OFF - LX + 4]
+            return edge_load[j, i - OFF - LX + 5]
         return load[j, i - OFF]
 
     def both(source, target, low_end, high_begin, diag, load=None):
@@ -477,8 +477,8 @@
             flag = flags[0] if i < OFF else flags[1] if i >= OFF + LX else None
             store_to(target, mask, flag, load)(i, image)
 
-        sweep(source, gain, low_end - 6, low_end, diag, store)
-        sweep(source, gain, high_begin, high_begin + 8, diag, store)
+        sweep(source, gain, low_end - 7, low_end, diag, store)
+        sweep(source, gain, high_begin, high_begin + 7, diag, store)
 
     diag = spring_term - SHIFT_U
     both(wide, v0, OFF + 1, OFF + 14, spring_term, force_at)
@@ -559,7 +559,7 @@
     lax.fori_loop(OFF, OFF + LX, middle, 0, unroll=2)
     moved_copy = pltpu.make_async_copy(moved, moved_out, sem.at[0])
     moved_copy.start()
-    for i in (OFF - 2, OFF - 1, *range(OFF + LX, OFF + LX + 4)):
+    for i in (*range(OFF - 3, OFF), *range(OFF + LX, OFF + LX + 3)):
         for j in range(3):
             current(j, i)
 
@@ -587,7 +587,7 @@
     lax.fori_loop(OFF, OFF + LX, step, 0, unroll=4)
     found_copy = pltpu.make_async_copy(found, found_out, sem.at[1])
     found_copy.start()
-    for i in (OFF - 2, OFF - 1, *range(OFF + LX, OFF + LX + 3)):
+    for i in (*range(OFF - 3, OFF), *range(OFF + LX, OFF + LX + 2)):
         drive[i] = jnp.maximum(past[i], energy(i))
 
     def flag_of(i):
@@ -615,9 +615,9 @@
     def image(i, here, beside):
         return ((full - SHIFT_D) + 2.0 * drive[i]) * here - length_term * beside
 
-    apply(short_damage, OFF - 2, OFF + LX + 3, start, w0)
-    apply(w0, OFF - 1, OFF + LX + 2, image, w1)
-    apply(w1, OFF, OFF + LX + 1, image, w2)
+    apply(short_damage, OFF - 3, OFF + LX + 2, start, w0)
+    apply(w0, OFF - 2, OFF + LX + 1, image, w1)
+    apply(w1, OFF - 1, OFF + LX, image, w2)
 
     lane = lanes((LY, LZ))
     row = lax.broadcasted_iota(jnp.int32, (LY, LZ), 0)
@@ -628,10 +628,10 @@
     def add(i, acc):
         wide_now = w2[i]
         u = wide_now[0:LY]
-        dx = w2[i + 1, 0:LY] - u
+        dx = w2[i - 1, 0:LY] - u
         dy = last_row(wide_now)[0:LY] - u
         dz = next_lane(u) - u
-        side = jnp.where(i == OFF, length_term * (1.0 - flags[0]), 0.0)
+        side = jnp.where(i == OFF + LX - 1, length_term * (1.0 - flags[1]), 0.0)
         square = u * u
         work = (edge + side + 2.0 * drive[i, 0:LY]) * square
         work = work + length_term * (dx * dx + dy * dy + dz * dz)

time: 81.9 us -> 84 us (1.026)
  waiting for transfers between devices: 3.18 us -> 6.24 us
  starting transfers between devices: 14.2 us -> 12.8 us
    ppermute x6, waiting for transfers between devices: 3.18 us -> 6.24 us  [send(): lax.ppermute(values, axis, [(i, (i + step) % size) for i in range(size)])]
    ppermute x6, starting transfers between devices: 14.2 us -> 12.8 us  [send(): lax.ppermute(values, axis, [(i, (i + step) % size) for i in range(size)])]
  transfers between devices with their start and end apart: 6 -> 6, of which waited for: 2 -> 3; matrix products, arithmetic and copies ran while one was open for 0% -> 0% of each run, Pallas kernels for 8% -> 8%
where the time goes in v8:
time: 84 us; the launch traced here: 83.8 us
  blocking collectives  45.4 us (54%)
  Pallas kernels  17.9 us (21%)
  starting transfers between devices  12.8 us (15%)
  waiting for transfers between devices  6.24 us (7%)
    all_to_all x2, blocking collectives, gather(): return lax.all_to_all(sums, axes, 0, 0, tiled=True)  45.4 us
    pallas_call x7, Pallas kernels, run(): pl.pallas_call(kernel, out_shape=[fast(s) if isinstance(s, tuple) else s...  17.9 us
    ppermute x6, starting transfers between devices, send(): lax.ppermute(values, axis, [(i, (i + step) % size) for i in range(size)])  12.8 us
    ppermute x6, waiting for transfers between devices, send(): lax.ppermute(values, axis, [(i, (i + step) % size) for i in range(size)])  6.24 us
  transfers between devices with their start and end apart: 6, of which 3 were waited for; matrix products, arithmetic and copies ran while one was open for 0% of the time, Pallas kernels for 8%

profile of v8, /device:TPU:1, one launch (start us, length us, event | category | flops | bytes accessed | tf_op | source)
XLA Modules:
  0.0 83.8 jit_solution(10409204225585129269)
XLA Ops:
  0.6 2.8 %shard_map.76 = (f32[3,16,32,128]{3,2,1,0:T(8,128)S(1)}, f32[3,16,32,128]{3,2,1,0:T(8,128)S(1)}, f32[16,32,128]{2,1,0:T(8,128)S(1)}, f32[16,32,128]{2,1,0:T(8,12...) custom-call(f32[3,16,32,128]{3,2,1,0:T(8,128)} %disp.1, ...), custom_call_target="tpu_custom_call" | custom-call | tf_op jit(solution)/shard_map/pallas_call | solution.py:53
  3.4 0.0 copy-start
  3.5 0.7 copy-done
  4.2 3.2 %collective-permute-start.2 = (f32[40,32,128]{2,1,0:T(8,128)}, f32[40,32,128]{2,1,0:T(8,128)S(1)}, u32[]{:S(2)}, u32[]{:S(2)}) collective-permute-start(f32[40,32,128]{2,1,0:T(8,128)} %get-tuple-element.52), channel_id=1, source_target_pairs={{0,248},{8,0},{16,8},{24,16},{32,24},{40,32},{48,40},{56,48},{64,5... | collective-permute-start | bytes 1966088 | tf_op jit(solution)/shard_map/ppermute | solution.py:663
  7.4 0.0 collective-permute-start.3
  7.4 0.0 copy-start.1
  7.4 0.1 add_convert_fusion.flags
  7.4 2.1 %shard_map.77 = (f32[80,8,128]{2,1,0:T(8,128)S(1)}, f32[84,8,128]{2,1,0:T(8,128)S(1)}) custom-call(f32[3,16,32,128]{3,2,1,0:T(8,128)} %disp.1, f32[3,16,32,128]{3,2,1,0:T(8,128)} %force.1, f32[16,32,128]{2,1,0:T(8,128)} %damage.1, f32[16,32,128]{2,1,0:T(8,128)} %history.1, s32[16,32,128]{2,1,0:T(8,128)} %crack.1, f32[4]{0:T(128)S(1)} %add_convert_fusion.flags), custom_call_target="tpu_custom_call" | custom-call | tf_op jit(solution)/shard_map/pallas_call | solution.py:53
  9.5 1.1 %collective-permute-start.1 = (f32[84,8,128]{2,1,0:T(8,128)S(1)}, f32[84,8,128]{2,1,0:T(8,128)S(1)}, u32[]{:S(2)}, u32[]{:S(2)}) collective-permute-start(f32[84,8,128]{2,1,0:T(8,128)S(1)} %get-tuple-element.42), channel_id=1, source_target_pairs={{0,1},{1,2},{2,3},{3,4},{4,5},{5,6},{6,7},{7,0},{8,9},{9,10},{10,1... | collective-permute-start | bytes 1032200 | tf_op jit(solution)/shard_map/ppermute | solution.py:663
  10.6 4.0 %collective-permute-start = (f32[80,8,128]{2,1,0:T(8,128)S(1)}, f32[80,8,128]{2,1,0:T(8,128)S(1)}, u32[]{:S(2)}, u32[]{:S(2)}) collective-permute-start(f32[80,8,128]{2,1,0:T(8,128)S(1)} %get-tuple-element.41), channel_id=1, source_target_pairs={{0,7},{1,0},{2,1},{3,2},{4,3},{5,4},{6,5},{7,6},{8,15},{9,8},{10,9... | collective-permute-start | bytes 983048 | tf_op jit(solution)/shard_map/ppermute | solution.py:663
  14.7 4.0 %collective-permute-done.high = f32[80,8,128]{2,1,0:T(8,128)S(1)} collective-permute-done((f32[80,8,128]{2,1,0:T(8,128)S(1)}, f32[80,8,128]{2,1,0:T(8,128)S(1)}, u32[]{:S(2)}, u32[]{:S(2)}) %collective-permute-start) | collective-permute-done | bytes 327712 | tf_op jit(solution)/shard_map/ppermute | solution.py:663
  18.7 0.8 collective-permute-done.1.low
  19.5 4.4 %collective-permute-start.5 = (f32[61,8,128]{2,1,0:T(8,128)S(1)}, f32[61,8,128]{2,1,0:T(8,128)S(1)}, u32[]{:S(2)}, u32[]{:S(2)}) collective-permute-start(f32[61,8,128]{2,1,0:T(8,128)S(1)} %get-tuple-element.55), channel_id=1, source_target_pairs={{0,8},{8,16},{16,24},{24,32},{32,40},{40,48},{48,56},{56,64},{64,7... | collective-permute-start | bytes 749576 | tf_op jit(solution)/shard_map/ppermute | solution.py:663
  24.0 0.0 collective-permute-start.4
  24.0 0.0 copy-done.1
  24.0 4.4 %shard_map.78 = (f32[3,28,48,128]{3,2,1,0:T(8,128)S(1)}, f32[3,16,48,128]{3,2,1,0:T(8,128)S(1)}, f32[28,48,128]{2,1,0:T(8,128)S(1)}, f32[3,28,48,128]{3,2,1,0:T(...) custom-call(f32[3,16,32,128]{3,2,1,0:T(8,128)S(1)} %get-tuple-elemen, ...), custom_call_target="tpu_custom_call" | custom-call | tf_op jit(solution)/shard_map/pallas_call | solution.py:53
  28.4 1.4 %collective-permute-done.4.ahead_corner = f32[57,8,128]{2,1,0:T(8,128)S(1)} collective-permute-done((f32[57,8,128]{2,1,0:T(8,128)S(1)}, f32[57,8,128]{2,1,0:T(8,128)S(1)}, u32[]{:S(2)}, u32[]{:S(2)}) %collective-permute-start.4) | collective-permute-done | bytes 233504 | tf_op jit(solution)/shard_map/ppermute | solution.py:663
  29.8 0.0 collective-permute-done.5.behind_corner
  29.8 0.0 collective-permute-done.2.ahead
  29.8 0.0 collective-permute-done.3.behind
  29.8 3.5 %shard_map.80 = (f32[3,28,48,128]{3,2,1,0:T(8,128)S(1)}, f32[28,48,128]{2,1,0:T(8,128)S(1)}, f32[3,28,48,128]{3,2,1,0:T(8,128)S(1)}, f32[3,28,48,128]{3,2,1,0:T(...) custom-call(f32[3,28,48,128]{3,2,1,0:T(8,128)S(1)} %get-tuple-elemen, ...), custom_call_target="tpu_custom_call", output_to_operand_aliasing={{0}: (0, {}), {1}: (2, {}), {2}: (3, {}), {3}: (4, {}), {4}... | custom-call | tf_op jit(solution)/shard_map/pallas_call | solution.py:53
  33.3 27.0 %all_to_all.22 = f32[256,1,128]{2,1,0:T(1,128)S(1)} all-to-all(f32[256,1,128]{2,1,0:T(1,128)S(1)} %bitcast.14), channel_id=1, replica_groups=mesh['gx'=32,'gy'=8] {'gx','gy'}, dimensions={0} | all-to-all | bytes 262144 | tf_op jit(solution)/shard_map/all_to_all | solution.py:675
  60.3 4.1 %shard_map.81 = (f32[3,16,32,128]{3,2,1,0:T(8,128)}, f32[16,32,128]{2,1,0:T(8,128)}, f32[28,40,128]{2,1,0:T(8,128)S(1)}, f32[28,40,128]{2,1,0:T(8,128)S(1)}, f32...) custom-call(f32[256,128]{1,0:T(8,128)S(1)} %bitcast.12, f32[3,28,48,128]{3,2,1,0:T(8,128)S(1)} %get-tuple-element.57.wide, ...), custom_call_target="tpu_custom_call" | custom-call | tf_op jit(solution)/shard_map/pallas_call | solution.py:53
  64.4 18.4 %all_to_all.23 = f32[256,1,128]{2,1,0:T(1,128)S(1)} all-to-all(f32[256,1,128]{2,1,0:T(1,128)S(1)} %bitcast.15), channel_id=1, replica_groups=mesh['gx'=32,'gy'=8] {'gx','gy'}, dimensions={0} | all-to-all | bytes 262144 | tf_op jit(solution)/shard_map/all_to_all | solution.py:675
  82.8 1.0 %shard_map.82 = f32[16,32,128]{2,1,0:T(8,128)} custom-call(f32[256,128]{1,0:T(8,128)S(1)} %bitcast.13, f32[16,32,128]{2,1,0:T(8,128)S(1)} %get-tuple-element.38.damage, f32[28,40,128]{2,1,0:T(8,128)S(1)} %get-tuple-element.65.w0, f32[28,40,128]{2,1,0:T(8,128)S(1)} %get-tuple-element.66.w1, f32[28,40,128]{2,1,0:T(8,128)S(1)} %get-tuple-element.67.w2), custom_call_target="tpu_custom_call" | custom-call | tf_op jit(solution)/shard_map/pallas_call | solution.py:53
  (1 shorter events, 0.0 us)
Async XLA Ops:
  3.4 0.7 copy-start
  4.2 25.6 %collective-permute-start.2 = (f32[40,32,128]{2,1,0:T(8,128)}, f32[40,32,128]{2,1,0:T(8,128)S(1)}, u32[]{:S(2)}, u32[]{:S(2)}) collective-permute-start(f32[40,32,128]{2,1,0:T(8,128)} %get-tuple-element.52), channel_id=1, source_target_pairs={{0,248},{8,0},{16,8},{24,16},{32,24},{40,32},{48,40},{56,48},{64,5... | collective-permute-start | bytes 1966088 | tf_op jit(solution)/shard_map/ppermute | solution.py:663
  7.4 22.4 %collective-permute-start.3 = (f32[42,32,128]{2,1,0:T(8,128)}, f32[42,32,128]{2,1,0:T(8,128)S(1)}, u32[]{:S(2)}, u32[]{:S(2)}) collective-permute-start(f32[42,32,128]{2,1,0:T(8,128)} %get-tuple-element.53), channel_id=1, source_target_pairs={{0,8},{8,16},{16,24},{24,32},{32,40},{40,48},{48,56},{56,64},{64,7... | collective-permute-start | bytes 2064392 | tf_op jit(solution)/shard_map/ppermute | solution.py:663
  7.4 16.6 %copy-start.1 = (s32[16,32,128]{2,1,0:T(8,128)S(1)}, s32[16,32,128]{2,1,0:T(8,128)}, u32[]{:S(2)}) copy-start(s32[16,32,128]{2,1,0:T(8,128)} %copy-done) | copy-start | bytes 786436
  9.5 10.0 %collective-permute-start.1 = (f32[84,8,128]{2,1,0:T(8,128)S(1)}, f32[84,8,128]{2,1,0:T(8,128)S(1)}, u32[]{:S(2)}, u32[]{:S(2)}) collective-permute-start(f32[84,8,128]{2,1,0:T(8,128)S(1)} %get-tuple-element.42), channel_id=1, source_target_pairs={{0,1},{1,2},{2,3},{3,4},{4,5},{5,6},{6,7},{7,0},{8,9},{9,10},{10,1... | collective-permute-start | bytes 1032200 | tf_op jit(solution)/shard_map/ppermute | solution.py:663
  10.6 8.0 %collective-permute-start = (f32[80,8,128]{2,1,0:T(8,128)S(1)}, f32[80,8,128]{2,1,0:T(8,128)S(1)}, u32[]{:S(2)}, u32[]{:S(2)}) collective-permute-start(f32[80,8,128]{2,1,0:T(8,128)S(1)} %get-tuple-element.41), channel_id=1, source_target_pairs={{0,7},{1,0},{2,1},{3,2},{4,3},{5,4},{6,5},{7,6},{8,15},{9,8},{10,9... | collective-permute-start | bytes 983048 | tf_op jit(solution)/shard_map/ppermute | solution.py:663
  19.5 10.2 %collective-permute-start.5 = (f32[61,8,128]{2,1,0:T(8,128)S(1)}, f32[61,8,128]{2,1,0:T(8,128)S(1)}, u32[]{:S(2)}, u32[]{:S(2)}) collective-permute-start(f32[61,8,128]{2,1,0:T(8,128)S(1)} %get-tuple-element.55), channel_id=1, source_target_pairs={{0,8},{8,16},{16,24},{24,32},{32,40},{40,48},{48,56},{56,64},{64,7... | collective-permute-start | bytes 749576 | tf_op jit(solution)/shard_map/ppermute | solution.py:663
  24.0 5.8 %collective-permute-start.4 = (f32[57,8,128]{2,1,0:T(8,128)S(1)}, f32[57,8,128]{2,1,0:T(8,128)S(1)}, u32[]{:S(2)}, u32[]{:S(2)}) collective-permute-start(f32[57,8,128]{2,1,0:T(8,128)S(1)} %get-tuple-element.54), channel_id=1, source_target_pairs={{0,248},{8,0},{16,8},{24,16},{32,24},{40,32},{48,40},{56,48},{64,5... | collective-permute-start | bytes 700424 | tf_op jit(solution)/shard_map/ppermute | solution.py:663
